TPU v7x, 32 devices: a whole 2x2x4 slice. The times are simulated.
32 devices in a mesh: gx: 2 (over x), gy: 4 (over z), gz: 4 (over y, core).
Axes of the slice: x: 2, y: 2, z: 4, core: 2. Of those that a mesh axis runs over, the one named last changes fastest.
Arguments:
- conductivity: float32 [16, 32, 1024], P('gx', 'gy', 'gz'), may hold values from 0.1 to 10
- source: float32 [16, 32, 1024], P('gx', 'gy', 'gz'), may hold values from -5 to 5
Outputs:
- solution: float32 [16, 32, 1024], P('gx', 'gy', 'gz')
- residual: float32 [16, 32, 1024], P('gx', 'gy', 'gz')
All inputs are finite; a program needn't handle non-finite values.
Results may differ from a plain program's by a relative error of at most 0.0003.
Values sent between devices are 32-bit elements; how exact they have to be, the bound alone decides.
No kernel may reach another device: no remote copies, remote signals or barrier semaphores. Data moves between devices by JAX's collectives and lax.ppermute only.
A program may use at most 64 MiB of HBM per device.

v0:
```python
import jax
import jax.numpy as jnp
from jax import lax
from jax.experimental import pallas as pl
from jax.experimental.pallas import tpu as pltpu
from jax.sharding import PartitionSpec as P

DEGREE = 4
COARSE_DEGREE = 8
smooth_low = 0.5
coarse_low = 0.03
upper_bound = 2.0

F32 = jnp.float32
LANES = 128
PAD = 8
HALO = 5
COARSE_PAD = 4
FACE = 14.0 / 3.0
CORNER = 1.0 / 3.0
TOTAL = 128.0 / 3.0
SCALE = 0.05


def chebyshev_coefs(degree, lower):
    centre = (upper_bound + lower) / 2.0
    half_width = (upper_bound - lower) / 2.0
    ratio_term = centre / half_width
    rho_prev = 1.0 / ratio_term
    weights = []
    for number in range(1, degree):
        rho_next = 1.0 / (2.0 * ratio_term - rho_prev)
        weights.append((rho_next * rho_prev, 2.0 * rho_next / half_width))
        rho_prev = rho_next
    return centre, weights


def loop(start, stop, body, unroll=1):
    def step(i, carry):
        body(i)
        return carry

    lax.fori_loop(start, stop, step, 0, unroll=unroll)


def third_pairs(values):
    tiles, rows, _ = values.shape
    flat = values.reshape(tiles * rows, LANES)
    up = pltpu.roll(flat, 1, 1).reshape(tiles, rows, LANES)
    down = pltpu.roll(flat, LANES - 1, 1).reshape(tiles, rows, LANES)
    if tiles > 1:
        lane = lax.broadcasted_iota(jnp.int32, (tiles, rows, LANES), 2)
        up_other = jnp.concatenate([up[tiles - 1 :], up[: tiles - 1]], axis=0)
        down_other = jnp.concatenate([down[1:], down[:1]], axis=0)
        up = jnp.where(lane == 0, up_other, up)
        down = jnp.where(lane == LANES - 1, down_other, down)
    return up + down


def neighbour_sum(ref, y, row):
    centre = ref[y, :, row : row + 8, :]
    before = ref[y - 1, :, row : row + 8, :]
    after = ref[y + 1, :, row : row + 8, :]
    side = ref[y, :, row - 1 : row + 7, :] + ref[y, :, row + 1 : row + 9, :]
    corner = (ref[y - 1, :, row - 1 : row + 7, :] + ref[y - 1, :, row + 1 : row + 9, :]) + (
        ref[y + 1, :, row - 1 : row + 7, :] + ref[y + 1, :, row + 1 : row + 9, :]
    )
    face = (before + after) + side
    plane = FACE * face + corner
    beside = FACE * centre + face + CORNER * corner
    return plane + third_pairs(beside), centre


def zero_pads(refs):
    for ref in refs:
        count, tiles, rows, _ = ref.shape
        zero = jnp.zeros((tiles, PAD, LANES), F32)

        def body(y, ref=ref, rows=rows, zero=zero):
            ref[y, :, 0:PAD, :] = zero
            ref[y, :, rows - PAD : rows, :] = zero

        loop(0, count, body, 2)


def zero_rows(ref, rows):
    zero = jnp.zeros(ref.shape[1:], F32)
    for y in rows:
        ref[y] = zero


def tiles_of(ref):
    return range(0, ref.shape[2], 8)


def make_diagonal(kap, diag, inv, lo, hi, unroll=1):
    def body(y):
        for x in tiles_of(diag):
            total, centre = neighbour_sum(kap, y, PAD + x)
            value = TOTAL * centre + total
            diag[y, :, x : x + 8, :] = value
            inv[y, :, x : x + 8, :] = jnp.where(centre > 0.0, 1.0 / value, 0.0)

    loop(lo, hi, body, unroll)


def first_update(kap, inv, res, v, w, acc, lo, hi, scale, add, unroll=1):
    def body(y):
        for x in tiles_of(inv):
            step = (inv[y, :, x : x + 8, :] * scale) * res[y, :, x : x + 8, :]
            v[y, :, PAD + x : PAD + x + 8, :] = step
            w[y, :, PAD + x : PAD + x + 8, :] = kap[y, :, PAD + x : PAD + x + 8, :] * step
            acc[y, :, x : x + 8, :] = acc[y, :, x : x + 8, :] + step if add else step

    loop(lo, hi, body, unroll)


def times(kap, v, w, lo, hi, unroll=1):
    def body(y):
        w[y] = kap[y] * v[y]

    loop(lo, hi, body, unroll)


def new_residual(kap, diag, res, v, w, y, x):
    total, centre = neighbour_sum(v, y, PAD + x)
    weighted, _ = neighbour_sum(w, y, PAD + x)
    return (
        res[y, :, x : x + 8, :]
        - diag[y, :, x : x + 8, :] * centre
        + (kap[y, :, PAD + x : PAD + x + 8, :] * total + weighted)
    ), centre


def residual_only(kap, diag, res, v, w, lo, hi, unroll=1):
    def body(y):
        for x in tiles_of(diag):
            value, _ = new_residual(kap, diag, res, v, w, y, x)
            res[y, :, x : x + 8, :] = value

    loop(lo, hi, body, unroll)


def smoothing_step(kap, diag, inv, res, old, new, acc, lo, hi, pair, unroll=1):
    def body(y):
        for x in tiles_of(diag):
            value, centre = new_residual(kap, diag, res, old[0], old[1], y, x)
            res[y, :, x : x + 8, :] = value
            step = pair[0] * centre + (pair[1] * inv[y, :, x : x + 8, :]) * value
            new[0][y, :, PAD + x : PAD + x + 8, :] = step
            new[1][y, :, PAD + x : PAD + x + 8, :] = (
                kap[y, :, PAD + x : PAD + x + 8, :] * step
            )
            acc[y, :, x : x + 8, :] = acc[y, :, x : x + 8, :] + step

    loop(lo, hi, body, unroll)


def halving(rows):
    row = lax.broadcasted_iota(jnp.int32, (rows, rows // 2), 0)
    col = lax.broadcasted_iota(jnp.int32, (rows, rows // 2), 1)
    return jnp.where(row // 2 == col, 0.125, 0.0).astype(F32)


def doubling(cols):
    row = lax.broadcasted_iota(jnp.int32, (cols // 2, cols), 0)
    col = lax.broadcasted_iota(jnp.int32, (cols // 2, cols), 1)
    return jnp.where(col // 2 == row, 1.0, 0.0).astype(F32)


def halo_doubling():
    row = lax.broadcasted_iota(jnp.int32, (LANES, LANES), 0)
    col = lax.broadcasted_iota(jnp.int32, (LANES, LANES), 1)
    source = col // 2 + jnp.where(col < LANES // 2, 0, LANES // 2)
    return jnp.where(source == row, 1.0, 0.0).astype(F32)


def product(left, right):
    return jnp.dot(left, right, precision=lax.Precision.HIGHEST, preferred_element_type=F32)


def along_lanes(values):
    return jnp.concatenate([values[t] for t in range(values.shape[0])], axis=-1)


def before_kernel(flags, own, ylo, yhi, kap, diag, inv, xout, rout, coarse, va, wa, vb, wb, res, acc, flat):
    rows = own.shape[1]
    x_count = own.shape[3]
    inner = slice(PAD, PAD + x_count)
    last = HALO + rows
    has_lo = flags[2] > 0
    has_hi = flags[3] > 0
    zero_pads((kap, va, wa, vb, wb))

    def fill(y):
        kap[HALO + y, :, inner, :] = SCALE * own[0, y]
        res[HALO + y] = own[1, y]

    loop(0, rows, fill)
    for j in range(HALO):
        kap[j, :, inner, :] = jnp.where(has_lo, SCALE * ylo[j], 0.0)
        kap[last + j, :, inner, :] = jnp.where(has_hi, SCALE * yhi[j], 0.0)
    for j in range(HALO - 1):
        res[1 + j] = ylo[HALO + j]
        res[last + j] = yhi[HALO + j]
    make_diagonal(kap, diag, inv, 1, last + HALO - 1)
    centre, weights = chebyshev_coefs(DEGREE, smooth_low)
    first_update(kap, inv, res, va, wa, acc, 1, last + HALO - 1, 1.0 / centre, False)
    old, new = (va, wa), (vb, wb)
    lo, hi = 2, last + HALO - 2
    for pair in weights:
        smoothing_step(kap, diag, inv, res, old, new, acc, lo, hi, pair)
        old, new = new, old
        lo, hi = lo + 1, hi - 1
    residual_only(kap, diag, res, old[0], old[1], HALO, last)
    tiles = rout.shape[1]

    def emit(y):
        xout[y] = acc[HALO + y, 0:tiles]
        rout[y] = res[HALO + y, 0:tiles]

    loop(0, rows, emit)
    pieces = []
    for source, offset in ((kap, PAD), (res, 0)):
        for y in range(0, rows, 2):
            both = (
                source[HALO + y, 0:tiles, offset : offset + x_count, :]
                + source[HALO + y + 1, 0:tiles, offset : offset + x_count, :]
            )
            pieces.append(along_lanes(both))
    flat[...] = product(jnp.concatenate(pieces, axis=0), halving(tiles * LANES))
    total = flat.shape[0]
    coarse[...] = flat[pl.ds(0, total // 2, stride=2), :] + flat[pl.ds(1, total // 2, stride=2), :]


def after_kernel(flags, *refs, count, offsets):
    blocks = refs[:count]
    (kap, diag, inv, xpre, rown, rlo, rhi, sol, resid) = refs[count : count + 9]
    (k1, d1, i1, r1, x1, va1, wa1, vb1, wb1, k2, d2, i2, r2, x2, va2, wa2, vb2, wb2, flat, va, wa, vb, wb, res, acc) = refs[count + 9 :]
    me_x, me_y = flags[4], flags[5]
    zero_pads((k1, va1, wa1, vb1, wb1, k2, va2, wa2, vb2, wb2, va, wa, vb, wb))
    each = blocks[0].shape[1]
    xc = blocks[0].shape[3]
    yc = each * count
    lo1, hi1 = COARSE_PAD, COARSE_PAD + yc
    edge = [lo1 - 1, hi1]
    for ref in (k1, va1, wa1, vb1, wb1):
        zero_rows(ref, edge)
    zero_rows(x1, list(range(lo1)) + list(range(hi1, hi1 + COARSE_PAD)))
    for block, offset in zip(blocks, offsets):
        at = lax.rem(me_y - offset + count, count) * each + COARSE_PAD
        for y in range(each):
            k1[at + y, :, PAD : PAD + xc, :] = block[0, y] * 0.25
            r1[at + y] = block[1, y]
    make_diagonal(k1, d1, i1, lo1, hi1)
    centre, weights = chebyshev_coefs(DEGREE, smooth_low)
    first_update(k1, i1, r1, va1, wa1, x1, lo1, hi1, 1.0 / centre, False)
    old, new = (va1, wa1), (vb1, wb1)
    for pair in weights:
        smoothing_step(k1, d1, i1, r1, old, new, x1, lo1, hi1, pair)
        old, new = new, old
    residual_only(k1, d1, r1, old[0], old[1], lo1, hi1)
    tiles1 = k1.shape[1]
    y2 = yc // 2
    half = xc // 2
    for target, source, offset, factor in ((k2, k1, PAD, 0.25), (r2, r1, 0, 1.0)):
        pieces = []
        for y in range(y2):
            a = lo1 + 2 * y
            both = source[a, :, offset : offset + xc, :] + source[a + 1, :, offset : offset + xc, :]
            pieces.append(along_lanes(both))
        flat[0 : y2 * xc, :] = product(jnp.concatenate(pieces, axis=0), halving(tiles1 * LANES))[:, 0:LANES]
        if target is k2:
            zero_rows(k2, range(y2 + 2))
        for y in range(y2):
            value = flat[pl.ds(y * xc, half, stride=2), :] + flat[pl.ds(y * xc + 1, half, stride=2), :]
            if target is k2:
                k2[1 + y, 0, PAD : PAD + half, :] = value * factor
            else:
                r2[1 + y] = jnp.zeros(r2.shape[1:], F32)
                r2[1 + y, 0, 0:half, :] = value
    for ref in (va2, wa2, vb2, wb2):
        zero_rows(ref, [0, y2 + 1])
    make_diagonal(k2, d2, i2, 1, 1 + y2, y2)
    centre, weights = chebyshev_coefs(COARSE_DEGREE, coarse_low)
    first_update(k2, i2, r2, va2, wa2, x2, 1, 1 + y2, 1.0 / centre, False, y2)
    old, new = (va2, wa2), (vb2, wb2)
    for pair in weights:
        smoothing_step(k2, d2, i2, r2, old, new, x2, 1, 1 + y2, pair, y2)
        old, new = new, old
    for y in range(y2):
        value = x2[1 + y, 0, 0:half, :]
        flat[pl.ds(y * xc, half, stride=2), :] = value
        flat[pl.ds(y * xc + 1, half, stride=2), :] = value
    wide = product(flat[0 : y2 * xc, :], doubling(2 * LANES))
    for y in range(y2):
        for t in range(tiles1):
            value = wide[y * xc : (y + 1) * xc, t * LANES : (t + 1) * LANES]
            for s in (0, 1):
                at = lo1 + 2 * y + s
                va1[at, t, PAD : PAD + xc, :] = value
                x1[at, t] = x1[at, t] + value
    times(k1, va1, wa1, lo1, hi1)
    centre, weights = chebyshev_coefs(DEGREE, smooth_low)
    residual_only(k1, d1, r1, va1, wa1, lo1, hi1)
    first_update(k1, i1, r1, va1, wa1, x1, lo1, hi1, 1.0 / centre, True)
    old, new = (va1, wa1), (vb1, wb1)
    for pair in weights:
        smoothing_step(k1, d1, i1, r1, old, new, x1, lo1, hi1, pair)
        old, new = new, old
    rows = rown.shape[0]
    last = HALO + rows
    x_count = rown.shape[2]
    wide_rows = (rows + 2 * HALO) // 2 + 1
    start = COARSE_PAD - (HALO + 1) // 2 + each * me_y
    for t in range(tiles1):
        for y in range(wide_rows):
            value = x1[start + y, t]
            base = (t * wide_rows + y) * x_count
            flat[pl.ds(base, xc, stride=2), :] = value
            flat[pl.ds(base + 1, xc, stride=2), :] = value
    n = wide_rows * x_count
    parts = []
    for t in range(tiles1 - 1):
        both = product(flat[t * n : (t + 1) * n, :], doubling(2 * LANES))
        parts += [both[:, 0:LANES], both[:, LANES:]]
    parts.append(product(flat[(tiles1 - 1) * n : tiles1 * n, :], halo_doubling()))
    own_tiles = len(parts) - 1
    for j in range(rows + 2 * HALO):
        y = (j + 1) // 2
        for t, part in enumerate(parts):
            value = part[y * x_count : (y + 1) * x_count, :]
            va[j, t, PAD : PAD + x_count, :] = value
            if HALO <= j < last and t < own_tiles:
                acc[j, t] = xpre[j - HALO, t] + value
    times(kap, va, wa, 0, rows + 2 * HALO)

    def fill(y):
        res[HALO + y] = rown[y]

    loop(0, rows, fill)
    for j in range(HALO - 1):
        res[1 + j] = rlo[j]
        res[last + j] = rhi[j]
    residual_only(kap, diag, res, va, wa, 1, last + HALO - 1)
    first_update(kap, inv, res, va, wa, acc, 1, last + HALO - 1, 1.0 / centre, True)
    old, new = (va, wa), (vb, wb)
    lo, hi = 2, last + HALO - 2
    for pair in weights:
        smoothing_step(kap, diag, inv, res, old, new, acc, lo, hi, pair)
        old, new = new, old
        lo, hi = lo + 1, hi - 1
    residual_only(kap, diag, res, old[0], old[1], HALO, last)
    block_x = sol.shape[0]
    first = pl.multiple_of(me_x * block_x, 8)
    for y in range(rows):
        for t in range(own_tiles):
            lanes = slice(t * LANES, (t + 1) * LANES)
            sol[:, y, lanes] = acc[HALO + y, t, pl.ds(first, block_x), :]
            resid[:, y, lanes] = res[HALO + y, t, pl.ds(first, block_x), :]


def ring(values, axis, step):
    count = lax.axis_size(axis)
    return lax.ppermute(values, axis, [(i, (i + step) % count) for i in range(count)])


def gather_first(values, axis, dim):
    count = lax.axis_size(axis)
    if count == 1:
        return values
    if count == 2:
        other = lax.ppermute(values, axis, [(0, 1), (1, 0)])
        first = lax.axis_index(axis) == 0
        return jnp.concatenate(
            [jnp.where(first, values, other), jnp.where(first, other, values)], axis=dim
        )
    every = lax.all_gather(values, axis)
    return jnp.concatenate([every[i] for i in range(count)], axis=dim)


def halo_tile(from_low, from_high, has_low, has_high):
    lane = lax.broadcasted_iota(jnp.int32, from_low.shape, from_low.ndim - 1)
    low = jnp.where(has_low, from_low, 0.0)
    high = jnp.where(has_high, from_high, 0.0)
    return jnp.where(lane < LANES // 2, high, low)


def vmem(shape):
    return pltpu.VMEM(shape, F32)


def call(kernel, out_shapes, scratch, inputs):
    limit = 4 * 2**20
    for s in scratch:
        size = 4
        for n in s.shape:
            size *= n
        limit += size
    for a in list(inputs) + list(out_shapes):
        limit += 4 * a.size if hasattr(a, "size") else 0
    limit = min(limit + 8 * 2**20, 60 * 2**20)
    whole = pl.BlockSpec(memory_space=pltpu.VMEM)
    return pl.pallas_call(
        kernel,
        out_shape=out_shapes,
        in_specs=[pl.BlockSpec(memory_space=pltpu.SMEM)] + [whole] * (len(inputs) - 1),
        out_specs=[whole] * len(out_shapes),
        scratch_shapes=scratch,
        compiler_params=pltpu.CompilerParams(vmem_limit_bytes=limit),
    )(*inputs)


def body(conductivity, source):
    bx, by, bz = conductivity.shape
    tiles = bz // LANES
    nx, ny, nz = (lax.axis_size(a) for a in ("gx", "gy", "gz"))
    ix, iy, iz = (lax.axis_index(a) for a in ("gx", "gy", "gz"))
    flags = jnp.stack([iz > 0, iz < nz - 1, iy > 0, iy < ny - 1, ix, iy]).astype(jnp.int32)
    has_left, has_right = iz > 0, iz < nz - 1
    x_count = bx * nx

    def shape(*dims):
        return jax.ShapeDtypeStruct(dims, F32)

    both = jnp.stack([conductivity, source]).reshape(2, bx, by, tiles, LANES)
    both = gather_first(both.transpose(0, 2, 3, 1, 4), "gx", 3)
    left = ring(both[:, :, tiles - 1], "gz", 1)
    right = ring(both[:, :, 0], "gz", -1)
    halo = halo_tile(left, right, has_left, has_right)
    own = jnp.concatenate([both, halo[:, :, None]], axis=2)
    ylo = ring(jnp.concatenate([own[0, by - HALO :], own[1, by - HALO + 1 :]], axis=0), "gy", 1)
    yhi = ring(jnp.concatenate([own[0, :HALO], own[1, : HALO - 1]], axis=0), "gy", -1)

    ext = by + 2 * HALO
    padded = x_count + 2 * PAD
    wide = (ext, tiles + 1, padded, LANES)
    plain = (ext, tiles + 1, x_count, LANES)
    each = by // 2
    xc = x_count // 2
    kap, diag, inv, xpre, rpre, coarse = call(
        before_kernel,
        [
            shape(*wide),
            shape(*plain),
            shape(*plain),
            shape(by, tiles, x_count, LANES),
            shape(by, tiles, x_count, LANES),
            shape(2 * each * xc, LANES),
        ],
        [vmem(wide)] * 4 + [vmem(plain)] * 2 + [vmem((2 * each * x_count, LANES))],
        [flags, own, ylo, yhi],
    )

    small = coarse.reshape(2 * each * xc, LANES)

    def with_tile(t):
        return jnp.concatenate([small, rpre[:, t].reshape(by * x_count, LANES)], axis=0)

    left = ring(with_tile(tiles - 1), "gz", 1)
    right = ring(with_tile(0), "gz", -1)
    halo = halo_tile(left, right, has_left, has_right)
    cut = 2 * each * xc
    coarse_halo = halo[:cut].reshape(2, each, 1, xc, LANES)
    coarse_own = jnp.concatenate([coarse.reshape(2, each, 1, xc, LANES), coarse_halo], axis=2)
    rown = jnp.concatenate([rpre, halo[cut:].reshape(by, 1, x_count, LANES)], axis=1)
    flat_coarse = coarse_own.reshape(-1, LANES)
    edge = HALO - 1
    n_flat = flat_coarse.shape[0]
    blocks, offsets = [coarse_own], [0]
    rlo = rhi = rown[:edge]
    for step in range(1, ny):
        parts = [flat_coarse]
        if step == 1:
            parts.append(rown[by - edge :].reshape(-1, LANES))
        if step == ny - 1:
            parts.append(rown[:edge].reshape(-1, LANES))
        got = ring(jnp.concatenate(parts, axis=0), "gy", step)
        blocks.append(got[:n_flat].reshape(coarse_own.shape))
        offsets.append(step)
        rest = got[n_flat:]
        size = edge * (tiles + 1) * x_count
        if step == 1:
            rlo = rest[:size].reshape(edge, tiles + 1, x_count, LANES)
            rest = rest[size:]
        if step == ny - 1:
            rhi = rest[:size].reshape(edge, tiles + 1, x_count, LANES)

    yc = each * ny
    tiles1 = tiles // 2 + 1
    wide1 = (yc + 2 * COARSE_PAD, tiles1, xc + 2 * PAD, LANES)
    plain1 = (yc + 2 * COARSE_PAD, tiles1, xc, LANES)
    y2 = yc // 2
    x2 = max(xc // 2, 8)
    wide2 = (y2 + 2, 1, x2 + 2 * PAD, LANES)
    plain2 = (y2 + 2, 1, x2, LANES)
    flat_rows = max(y2 * xc, tiles1 * (ext // 2 + 1) * x_count)

    def kernel(*refs):
        after_kernel(*refs, count=len(blocks), offsets=offsets)

    sol, resid = call(
        kernel,
        [shape(bx, by, bz), shape(bx, by, bz)],
        [vmem(wide1)] + [vmem(plain1)] * 4 + [vmem(wide1)] * 4
        + [vmem(wide2)] + [vmem(plain2)] * 4 + [vmem(wide2)] * 4
        + [vmem((flat_rows, LANES))] + [vmem(wide)] * 4 + [vmem(plain)] * 2,
        [flags] + blocks + [kap, diag, inv, xpre, rown, rlo, rhi],
    )
    return sol, resid


def solution(mesh):
    spec = P("gx", "gy", "gz")
    return jax.shard_map(body, mesh=mesh, in_specs=(spec, spec), out_specs=(spec, spec), check_vma=False)
```

profile of v0, /device:TPU:0, one launch (start us, length us, event | category | flops | bytes accessed | tf_op | source)
XLA Modules:
  0.0 79.4 jit_solution(1559455372115144934)
XLA Ops:
  0.6 0.9 %copy.5 = f32[1,8,8,2,128]{4,1,2,0,3:T(8,128)S(1)} copy(f32[1,8,8,2,128]{4,2,3,1,0:T(8,128)} %bitcast.56) | data formatting | bytes 131072 | tf_op jit(solution)/shard_map/stack | solution.py:426
  1.6 3.0 %collective-permute-start = (f32[2,8,2,8,128]{4,3,1,0,2:T(8,128)S(1)}, f32[2,8,2,8,128]{4,3,1,0,2:T(8,128)S(1)}, u32[]{:S(2)}, u32[]{:S(2)}) collective-permute-start(f32[2,8,2,8,128]{4,3,1,0,2:T(8,128)S(1)} %maximum_bitcast_fusion), channel_id=1, source_target_pairs={{0,16},{16,0},{1,17},{17,1},{2,18},{18,2},{3,19},{19,3},{4,20},{20... | collective-permute-start | bytes 393224 | tf_op jit(solution)/shard_map/ppermute | solution.py:373
  4.6 3.5 %collective-permute-done = f32[2,8,2,8,128]{4,3,1,0,2:T(8,128)S(1)} collective-permute-done((f32[2,8,2,8,128]{4,3,1,0,2:T(8,128)S(1)}, f32[2,8,2,8,128]{4,3,1,0,2:T(8,128)S(1)}, u32[]{:S(2)}, u32[]{:S(2)}) %collective-permute-start) | collective-permute-done | bytes 131104 | tf_op jit(solution)/shard_map/ppermute | solution.py:373
  8.2 0.4 collective-permute-start.1
  8.6 0.2 collective-permute-start.2
  8.7 2.8 %collective-permute-done.1 = f32[2,8,16,128]{3,2,1,0:T(8,128)S(1)} collective-permute-done((f32[2,8,16,128]{3,2,1,0:T(8,128)S(1)}, f32[2,8,16,128]{3,2,1,0:T(8,128)S(1)}, u32[]{:S(2)}, u32[]{:S(2)}) %collective-permute-start.1) | collective-permute-done | bytes 131104 | tf_op jit(solution)/shard_map/ppermute | solution.py:365
  11.6 2.8 %collective-permute-done.2 = f32[2,8,16,128]{3,2,1,0:T(8,128)S(1)} collective-permute-done((f32[2,8,16,128]{3,2,1,0:T(8,128)S(1)}, f32[2,8,16,128]{3,2,1,0:T(8,128)S(1)}, u32[]{:S(2)}, u32[]{:S(2)}) %collective-permute-start.2) | collective-permute-done | bytes 131104 | tf_op jit(solution)/shard_map/ppermute | solution.py:365
  14.4 1.6 %collective-permute-start.3 = (f32[9,3,16,128]{3,2,1,0:T(8,128)S(1)}, f32[9,3,16,128]{3,2,1,0:T(8,128)S(1)}, u32[]{:S(2)}, u32[]{:S(2)}) collective-permute-start(f32[9,3,16,128]{3,2,1,0:T(8,128)S(1)} %pad_maximum_fusion.3), channel_id=1, source_target_pairs={{0,4},{4,8},{8,12},{12,0},{1,5},{5,9},{9,13},{13,1},{2,6},{6,10},{... | collective-permute-start | bytes 663560 | tf_op jit(solution)/shard_map/ppermute | solution.py:365
  16.1 2.3 %collective-permute-start.4 = (f32[9,3,16,128]{3,2,1,0:T(8,128)S(1)}, f32[9,3,16,128]{3,2,1,0:T(8,128)S(1)}, u32[]{:S(2)}, u32[]{:S(2)}) collective-permute-start(f32[9,3,16,128]{3,2,1,0:T(8,128)S(1)} %pad_maximum_fusion.4), channel_id=1, source_target_pairs={{0,12},{4,0},{8,4},{12,8},{1,13},{5,1},{9,5},{13,9},{2,14},{6,2},{... | collective-permute-start | bytes 663560 | tf_op jit(solution)/shard_map/ppermute | solution.py:365
  18.4 0.1 stack.52.flags.refs_0_
  18.5 6.1 %collective-permute-done.3.ylo = f32[9,3,16,128]{3,2,1,0:T(8,128)S(1)} collective-permute-done((f32[9,3,16,128]{3,2,1,0:T(8,128)S(1)}, f32[9,3,16,128]{3,2,1,0:T(8,128)S(1)}, u32[]{:S(2)}, u32[]{:S(2)}) %collective-permute-start.3) | collective-permute-done | bytes 221216 | tf_op jit(solution)/shard_map/ppermute | solution.py:365
  24.6 3.4 %collective-permute-done.4.yhi = f32[9,3,16,128]{3,2,1,0:T(8,128)S(1)} collective-permute-done((f32[9,3,16,128]{3,2,1,0:T(8,128)S(1)}, f32[9,3,16,128]{3,2,1,0:T(8,128)S(1)}, u32[]{:S(2)}, u32[]{:S(2)}) %collective-permute-start.4) | collective-permute-done | bytes 221216 | tf_op jit(solution)/shard_map/ppermute | solution.py:365
  28.0 8.3 %shard_map.41 = (f32[18,3,32,128]{3,2,1,0:T(8,128)S(1)}, f32[18,3,16,128]{3,2,1,0:T(8,128)S(1)}, f32[18,3,16,128]{3,2,1,0:T(8,128)S(1)}, f32[8,2,16,128]{3,2,1,0...) custom-call(s32[6]{0:T(128)S(1)} %stack.52.flags.refs_0_, ...), custom_call_target="tpu_custom_call" | custom-call | tf_op jit(solution)/shard_map/pallas_call | solution.py:404
  36.4 0.1 collective-permute-start.5
  36.5 0.5 collective-permute-start.6
  37.0 2.1 %collective-permute-done.5 = f32[192,128]{1,0:T(8,128)S(1)} collective-permute-done((f32[192,128]{1,0:T(8,128)S(1)}, f32[192,128]{1,0:T(8,128)S(1)}, u32[]{:S(2)}, u32[]{:S(2)}) %collective-permute-start.5) | collective-permute-done | bytes 98336 | tf_op jit(solution)/shard_map/ppermute | solution.py:365
  39.1 2.2 %collective-permute-done.6 = f32[192,128]{1,0:T(8,128)S(1)} collective-permute-done((f32[192,128]{1,0:T(8,128)S(1)}, f32[192,128]{1,0:T(8,128)S(1)}, u32[]{:S(2)}, u32[]{:S(2)}) %collective-permute-start.6) | collective-permute-done | bytes 98336 | tf_op jit(solution)/shard_map/ppermute | solution.py:365
  41.4 1.8 %collective-permute-start.9 = (f32[320,128]{1,0:T(8,128)S(1)}, f32[320,128]{1,0:T(8,128)S(1)}, u32[]{:S(2)}, u32[]{:S(2)}) collective-permute-start(f32[320,128]{1,0:T(8,128)S(1)} %get-tuple-element.26), channel_id=1, source_target_pairs={{0,12},{4,0},{8,4},{12,8},{1,13},{5,1},{9,5},{13,9},{2,14},{6,2},{... | collective-permute-start | bytes 491528 | tf_op jit(solution)/shard_map/ppermute | solution.py:365
  43.2 0.3 collective-permute-start.7
  43.4 0.9 %collective-permute-start.8 = (f32[128,128]{1,0:T(8,128)S(1)}, f32[128,128]{1,0:T(8,128)S(1)}, u32[]{:S(2)}, u32[]{:S(2)}) collective-permute-start(f32[128,128]{1,0:T(8,128)S(1)} %bitcast.42), channel_id=1, source_target_pairs={{0,8},{4,12},{8,0},{12,4},{1,9},{5,13},{9,1},{13,5},{2,10},{6,14},... | collective-permute-start | bytes 196616 | tf_op jit(solution)/shard_map/ppermute | solution.py:365
  44.3 3.6 %collective-permute-done.9 = f32[320,128]{1,0:T(8,128)S(1)} collective-permute-done((f32[320,128]{1,0:T(8,128)S(1)}, f32[320,128]{1,0:T(8,128)S(1)}, u32[]{:S(2)}, u32[]{:S(2)}) %collective-permute-start.9) | collective-permute-done | bytes 163872 | tf_op jit(solution)/shard_map/ppermute | solution.py:365
  47.9 3.6 %collective-permute-done.7 = f32[320,128]{1,0:T(8,128)S(1)} collective-permute-done((f32[320,128]{1,0:T(8,128)S(1)}, f32[320,128]{1,0:T(8,128)S(1)}, u32[]{:S(2)}, u32[]{:S(2)}) %collective-permute-start.7) | collective-permute-done | bytes 163872 | tf_op jit(solution)/shard_map/ppermute | solution.py:365
  51.5 3.1 %collective-permute-done.8 = f32[128,128]{1,0:T(8,128)S(1)} collective-permute-done((f32[128,128]{1,0:T(8,128)S(1)}, f32[128,128]{1,0:T(8,128)S(1)}, u32[]{:S(2)}, u32[]{:S(2)}) %collective-permute-start.8) | collective-permute-done | bytes 65568 | tf_op jit(solution)/shard_map/ppermute | solution.py:365
  54.7 24.8 %shard_map.42 = (f32[8,8,256]{2,1,0:T(8,128)}, f32[8,8,256]{2,1,0:T(8,128)}) custom-call(s32[6]{0:T(128)S(1)} %stack.52.flags.refs_0_, f32[2,4,2,8,128]{4,3,2,1,0:T(8,128)S(1)} %pad_maximum_fusion.9.refs_1_, f32[2,4,2,8,128]{4,3,2,1,0:T(8,128)S(1)} %bitcast.46, f32[2,4,2,8,128]{4,3,2,1,0:T(8,128)S(1)} %bitcast.48, f32[2,4,2,8,128]{4,3,2,1,0:T(8,128)S(1)} %bitcast.45, ...), custom_call_target="tpu_custom_call" | custom-call | tf_op jit(solution)/shard_map/pallas_call | solution.py:404
  (26 shorter events, 0.3 us)
Async XLA Ops:
  0.6 0.9 %copy-start = (f32[8,8,256]{2,1,0:T(8,128)S(1)}, f32[8,8,256]{2,1,0:T(8,128)}, u32[]{:S(2)}) copy-start(f32[8,8,256]{2,1,0:T(8,128)} %param.3) | copy-start | bytes 196612
  1.6 6.5 %collective-permute-start = (f32[2,8,2,8,128]{4,3,1,0,2:T(8,128)S(1)}, f32[2,8,2,8,128]{4,3,1,0,2:T(8,128)S(1)}, u32[]{:S(2)}, u32[]{:S(2)}) collective-permute-start(f32[2,8,2,8,128]{4,3,1,0,2:T(8,128)S(1)} %maximum_bitcast_fusion), channel_id=1, source_target_pairs={{0,16},{16,0},{1,17},{17,1},{2,18},{18,2},{3,19},{19,3},{4,20},{20... | collective-permute-start | bytes 393224 | tf_op jit(solution)/shard_map/ppermute | solution.py:373
  8.2 3.4 %collective-permute-start.1 = (f32[2,8,16,128]{3,2,1,0:T(8,128)S(1)}, f32[2,8,16,128]{3,2,1,0:T(8,128)S(1)}, u32[]{:S(2)}, u32[]{:S(2)}) collective-permute-start(f32[2,8,16,128]{3,2,1,0:T(8,128)S(1)} %get-tuple-element.18), channel_id=1, source_target_pairs={{0,3},{1,0},{2,1},{3,2},{4,7},{5,4},{6,5},{7,6},{8,11},{9,8},{10,9... | collective-permute-start | bytes 393224 | tf_op jit(solution)/shard_map/ppermute | solution.py:365
  8.6 5.8 %collective-permute-start.2 = (f32[2,8,16,128]{3,2,1,0:T(8,128)S(1)}, f32[2,8,16,128]{3,2,1,0:T(8,128)S(1)}, u32[]{:S(2)}, u32[]{:S(2)}) collective-permute-start(f32[2,8,16,128]{3,2,1,0:T(8,128)S(1)} %get-tuple-element.19), channel_id=1, source_target_pairs={{0,1},{1,2},{2,3},{3,0},{4,5},{5,6},{6,7},{7,4},{8,9},{9,10},{10,1... | collective-permute-start | bytes 393224 | tf_op jit(solution)/shard_map/ppermute | solution.py:365
  14.4 10.2 %collective-permute-start.3 = (f32[9,3,16,128]{3,2,1,0:T(8,128)S(1)}, f32[9,3,16,128]{3,2,1,0:T(8,128)S(1)}, u32[]{:S(2)}, u32[]{:S(2)}) collective-permute-start(f32[9,3,16,128]{3,2,1,0:T(8,128)S(1)} %pad_maximum_fusion.3), channel_id=1, source_target_pairs={{0,4},{4,8},{8,12},{12,0},{1,5},{5,9},{9,13},{13,1},{2,6},{6,10},{... | collective-permute-start | bytes 663560 | tf_op jit(solution)/shard_map/ppermute | solution.py:365
  16.1 11.9 %collective-permute-start.4 = (f32[9,3,16,128]{3,2,1,0:T(8,128)S(1)}, f32[9,3,16,128]{3,2,1,0:T(8,128)S(1)}, u32[]{:S(2)}, u32[]{:S(2)}) collective-permute-start(f32[9,3,16,128]{3,2,1,0:T(8,128)S(1)} %pad_maximum_fusion.4), channel_id=1, source_target_pairs={{0,12},{4,0},{8,4},{12,8},{1,13},{5,1},{9,5},{13,9},{2,14},{6,2},{... | collective-permute-start | bytes 663560 | tf_op jit(solution)/shard_map/ppermute | solution.py:365
  36.4 2.7 %collective-permute-start.5 = (f32[192,128]{1,0:T(8,128)S(1)}, f32[192,128]{1,0:T(8,128)S(1)}, u32[]{:S(2)}, u32[]{:S(2)}) collective-permute-start(f32[192,128]{1,0:T(8,128)S(1)} %get-tuple-element.28), channel_id=1, source_target_pairs={{0,3},{1,0},{2,1},{3,2},{4,7},{5,4},{6,5},{7,6},{8,11},{9,8},{10,9... | collective-permute-start | bytes 294920 | tf_op jit(solution)/shard_map/ppermute | solution.py:365
  36.5 4.8 %collective-permute-start.6 = (f32[192,128]{1,0:T(8,128)S(1)}, f32[192,128]{1,0:T(8,128)S(1)}, u32[]{:S(2)}, u32[]{:S(2)}) collective-permute-start(f32[192,128]{1,0:T(8,128)S(1)} %get-tuple-element.29), channel_id=1, source_target_pairs={{0,1},{1,2},{2,3},{3,0},{4,5},{5,6},{6,7},{7,4},{8,9},{9,10},{10,1... | collective-permute-start | bytes 294920 | tf_op jit(solution)/shard_map/ppermute | solution.py:365
  41.4 6.6 %collective-permute-start.9 = (f32[320,128]{1,0:T(8,128)S(1)}, f32[320,128]{1,0:T(8,128)S(1)}, u32[]{:S(2)}, u32[]{:S(2)}) collective-permute-start(f32[320,128]{1,0:T(8,128)S(1)} %get-tuple-element.26), channel_id=1, source_target_pairs={{0,12},{4,0},{8,4},{12,8},{1,13},{5,1},{9,5},{13,9},{2,14},{6,2},{... | collective-permute-start | bytes 491528 | tf_op jit(solution)/shard_map/ppermute | solution.py:365
  43.2 8.4 %collective-permute-start.7 = (f32[320,128]{1,0:T(8,128)S(1)}, f32[320,128]{1,0:T(8,128)S(1)}, u32[]{:S(2)}, u32[]{:S(2)}) collective-permute-start(f32[320,128]{1,0:T(8,128)S(1)} %get-tuple-element.27), channel_id=1, source_target_pairs={{0,4},{4,8},{8,12},{12,0},{1,5},{5,9},{9,13},{13,1},{2,6},{6,10},{... | collective-permute-start | bytes 491528 | tf_op jit(solution)/shard_map/ppermute | solution.py:365
  43.4 11.2 %collective-permute-start.8 = (f32[128,128]{1,0:T(8,128)S(1)}, f32[128,128]{1,0:T(8,128)S(1)}, u32[]{:S(2)}, u32[]{:S(2)}) collective-permute-start(f32[128,128]{1,0:T(8,128)S(1)} %bitcast.42), channel_id=1, source_target_pairs={{0,8},{4,12},{8,0},{12,4},{1,9},{5,13},{9,1},{13,5},{2,10},{6,14},... | collective-permute-start | bytes 196616 | tf_op jit(solution)/shard_map/ppermute | solution.py:365
where the time goes:
time: 79.6 us; the launch traced here: 79.4 us
  waiting for transfers between devices  33.2 us (42%)
  Pallas kernels  33.1 us (42%)
  starting transfers between devices  11 us (14%)
  local copies, waits for them, and re-layouts  1.05 us (1%)
    pallas_call x2, Pallas kernels, call(): pl.pallas_call(kernel, out_shape=out_shapes, in_specs=[pl.BlockSpec(memor...  33.1 us
    ppermute x9, waiting for transfers between devices, ring(): lax.ppermute(values, axis, [(i, (i + step) % count) for i in range(count)])  29.7 us
    ppermute x9, starting transfers between devices, ring(): lax.ppermute(values, axis, [(i, (i + step) % count) for i in range(count)])  7.99 us
    ppermute x1, waiting for transfers between devices, gather_first(): other = lax.ppermute(values, axis, [(0, 1), (1, 0)])  3.5 us
    ppermute x1, starting transfers between devices, gather_first(): other = lax.ppermute(values, axis, [(0, 1), (1, 0)])  3.03 us
  transfers between devices with their start and end apart: 10, of which 10 were waited for; matrix products, arithmetic and copies ran while one was open for 0% of the time, Pallas kernels for 0%

commit v1 on v0

--- a/solution.py
+++ b/solution.py
@@ -35,12 +35,31 @@
     return centre, weights
 
 
-def loop(start, stop, body, unroll=1):
-    def step(i, carry):
-        body(i)
-        return carry
-
-    lax.fori_loop(start, stop, step, 0, unroll=unroll)
+CHUNK = 16
+
+
+def chunks(start, stop, body):
+    count = stop - start
+    full = count // CHUNK
+    if full == 1:
+        body(start, CHUNK)
+    elif full > 1:
+
+        def step(i, carry):
+            body(start + i * CHUNK, CHUNK)
+            return carry
+
+        lax.fori_loop(0, full, step, 0)
+    if count % CHUNK:
+        body(start + full * CHUNK, count % CHUNK)
+
+
+def loop(start, stop, body):
+    def group(first, rows):
+        for i in range(rows):
+            body(first + i)
+
+    chunks(start, stop, group)
 
 
 def third_pairs(values):
@@ -57,18 +76,18 @@
     return up + down
 
 
-def neighbour_sum(ref, y, row):
-    centre = ref[y, :, row : row + 8, :]
-    before = ref[y - 1, :, row : row + 8, :]
-    after = ref[y + 1, :, row : row + 8, :]
-    side = ref[y, :, row - 1 : row + 7, :] + ref[y, :, row + 1 : row + 9, :]
-    corner = (ref[y - 1, :, row - 1 : row + 7, :] + ref[y - 1, :, row + 1 : row + 9, :]) + (
-        ref[y + 1, :, row - 1 : row + 7, :] + ref[y + 1, :, row + 1 : row + 9, :]
-    )
-    face = (before + after) + side
-    plane = FACE * face + corner
-    beside = FACE * centre + face + CORNER * corner
-    return plane + third_pairs(beside), centre
+def neighbour_sums(ref, first, rows, row):
+    at = range(first - 1, first + rows + 1) if isinstance(first, int) else [first + i for i in range(-1, rows + 1)]
+    centre = [ref[y, :, row : row + 8, :] for y in at]
+    side = [ref[y, :, row - 1 : row + 7, :] + ref[y, :, row + 1 : row + 9, :] for y in at]
+    out = []
+    for i in range(1, rows + 1):
+        corner = side[i - 1] + side[i + 1]
+        face = (centre[i - 1] + centre[i + 1]) + side[i]
+        plane = FACE * face + corner
+        beside = FACE * centre[i] + face + CORNER * corner
+        out.append((plane + third_pairs(beside), centre[i]))
+    return out
 
 
 def zero_pads(refs):
@@ -80,7 +99,7 @@
             ref[y, :, 0:PAD, :] = zero
             ref[y, :, rows - PAD : rows, :] = zero
 
-        loop(0, count, body, 2)
+        loop(0, count, body)
 
 
 def zero_rows(ref, rows):
@@ -93,18 +112,18 @@
     return range(0, ref.shape[2], 8)
 
 
-def make_diagonal(kap, diag, inv, lo, hi, unroll=1):
-    def body(y):
+def make_diagonal(kap, diag, inv, lo, hi):
+    def body(first, rows):
         for x in tiles_of(diag):
-            total, centre = neighbour_sum(kap, y, PAD + x)
-            value = TOTAL * centre + total
-            diag[y, :, x : x + 8, :] = value
-            inv[y, :, x : x + 8, :] = jnp.where(centre > 0.0, 1.0 / value, 0.0)
-
-    loop(lo, hi, body, unroll)
-
-
-def first_update(kap, inv, res, v, w, acc, lo, hi, scale, add, unroll=1):
+            for i, (total, centre) in enumerate(neighbour_sums(kap, first, rows, PAD + x)):
+                value = TOTAL * centre + total
+                diag[first + i, :, x : x + 8, :] = value
+                inv[first + i, :, x : x + 8, :] = jnp.where(centre > 0.0, 1.0 / value, 0.0)
+
+    chunks(lo, hi, body)
+
+
+def first_update(kap, inv, res, v, w, acc, lo, hi, scale, add):
     def body(y):
         for x in tiles_of(inv):
             step = (inv[y, :, x : x + 8, :] * scale) * res[y, :, x : x + 8, :]
@@ -112,48 +131,51 @@
             w[y, :, PAD + x : PAD + x + 8, :] = kap[y, :, PAD + x : PAD + x + 8, :] * step
             acc[y, :, x : x + 8, :] = acc[y, :, x : x + 8, :] + step if add else step
 
-    loop(lo, hi, body, unroll)
-
-
-def times(kap, v, w, lo, hi, unroll=1):
+    loop(lo, hi, body)
+
+
+def times(kap, v, w, lo, hi):
     def body(y):
         w[y] = kap[y] * v[y]
 
-    loop(lo, hi, body, unroll)
-
-
-def new_residual(kap, diag, res, v, w, y, x):
-    total, centre = neighbour_sum(v, y, PAD + x)
-    weighted, _ = neighbour_sum(w, y, PAD + x)
-    return (
-        res[y, :, x : x + 8, :]
-        - diag[y, :, x : x + 8, :] * centre
-        + (kap[y, :, PAD + x : PAD + x + 8, :] * total + weighted)
-    ), centre
-
-
-def residual_only(kap, diag, res, v, w, lo, hi, unroll=1):
-    def body(y):
+    loop(lo, hi, body)
+
+
+def new_residuals(kap, diag, res, v, w, first, rows, x):
+    total = neighbour_sums(v, first, rows, PAD + x)
+    weighted = neighbour_sums(w, first, rows, PAD + x)
+    for i in range(rows):
+        y = first + i
+        k = kap[y, :, PAD + x : PAD + x + 8, :]
+        centre = total[i][1]
+        value = (
+            res[y, :, x : x + 8, :]
+            - diag[y, :, x : x + 8, :] * centre
+            + (k * total[i][0] + weighted[i][0])
+        )
+        res[y, :, x : x + 8, :] = value
+        yield y, k, centre, value
+
+
+def residual_only(kap, diag, res, v, w, lo, hi):
+    def body(first, rows):
         for x in tiles_of(diag):
-            value, _ = new_residual(kap, diag, res, v, w, y, x)
-            res[y, :, x : x + 8, :] = value
-
-    loop(lo, hi, body, unroll)
-
-
-def smoothing_step(kap, diag, inv, res, old, new, acc, lo, hi, pair, unroll=1):
-    def body(y):
+            for _ in new_residuals(kap, diag, res, v, w, first, rows, x):
+                pass
+
+    chunks(lo, hi, body)
+
+
+def smoothing_step(kap, diag, inv, res, old, new, acc, lo, hi, pair):
+    def body(first, rows):
         for x in tiles_of(diag):
-            value, centre = new_residual(kap, diag, res, old[0], old[1], y, x)
-            res[y, :, x : x + 8, :] = value
-            step = pair[0] * centre + (pair[1] * inv[y, :, x : x + 8, :]) * value
-            new[0][y, :, PAD + x : PAD + x + 8, :] = step
-            new[1][y, :, PAD + x : PAD + x + 8, :] = (
-                kap[y, :, PAD + x : PAD + x + 8, :] * step
-            )
-            acc[y, :, x : x + 8, :] = acc[y, :, x : x + 8, :] + step
-
-    loop(lo, hi, body, unroll)
+            for y, k, centre, value in new_residuals(kap, diag, res, old[0], old[1], first, rows, x):
+                step = pair[0] * centre + (pair[1] * inv[y, :, x : x + 8, :]) * value
+                new[0][y, :, PAD + x : PAD + x + 8, :] = step
+                new[1][y, :, PAD + x : PAD + x + 8, :] = k * step
+                acc[y, :, x : x + 8, :] = acc[y, :, x : x + 8, :] + step
+
+    chunks(lo, hi, body)
 
 
 def halving(rows):
@@ -281,12 +303,12 @@
                 r2[1 + y, 0, 0:half, :] = value
     for ref in (va2, wa2, vb2, wb2):
         zero_rows(ref, [0, y2 + 1])
-    make_diagonal(k2, d2, i2, 1, 1 + y2, y2)
+    make_diagonal(k2, d2, i2, 1, 1 + y2)
     centre, weights = chebyshev_coefs(COARSE_DEGREE, coarse_low)
-    first_update(k2, i2, r2, va2, wa2, x2, 1, 1 + y2, 1.0 / centre, False, y2)
+    first_update(k2, i2, r2, va2, wa2, x2, 1, 1 + y2, 1.0 / centre, False)
     old, new = (va2, wa2), (vb2, wb2)
     for pair in weights:
-        smoothing_step(k2, d2, i2, r2, old, new, x2, 1, 1 + y2, pair, y2)
+        smoothing_step(k2, d2, i2, r2, old, new, x2, 1, 1 + y2, pair)
         old, new = new, old
     for y in range(y2):
         value = x2[1 + y, 0, 0:half, :]

time: 79.6 us -> 57 us (0.72)
  Pallas kernels: 33.1 us -> 10.5 us
    pallas_call x2, Pallas kernels: 33.1 us -> 10.5 us  [call(): pl.pallas_call(kernel, out_shape=out_shapes, in_specs=[pl.BlockSpec(memor...]
where the time goes in v1:
time: 57 us; the launch traced here: 56.9 us
  waiting for transfers between devices  33.2 us (58%)
  starting transfers between devices  11 us (19%)
  Pallas kernels  10.5 us (18%)
  local copies, waits for them, and re-layouts  1.05 us (2%)
  between operations  0.79 us (1%)
    ppermute x9, waiting for transfers between devices, ring(): lax.ppermute(values, axis, [(i, (i + step) % count) for i in range(count)])  29.7 us
    pallas_call x2, Pallas kernels, call(): pl.pallas_call(kernel, out_shape=out_shapes, in_specs=[pl.BlockSpec(memor...  10.5 us
    ppermute x9, starting transfers between devices, ring(): lax.ppermute(values, axis, [(i, (i + step) % count) for i in range(count)])  8 us
    ppermute x1, waiting for transfers between devices, gather_first(): other = lax.ppermute(values, axis, [(0, 1), (1, 0)])  3.5 us
    ppermute x1, starting transfers between devices, gather_first(): other = lax.ppermute(values, axis, [(0, 1), (1, 0)])  3.03 us
  transfers between devices with their start and end apart: 10, of which 10 were waited for; matrix products, arithmetic and copies ran while one was open for 0% of the time, Pallas kernels for 0%

profile of v1, /device:TPU:0, one launch (start us, length us, event | category | flops | bytes accessed | tf_op | source)
XLA Modules:
  0.0 56.9 jit_solution(9692756884291054627)
XLA Ops:
  0.6 0.9 %copy.5 = f32[1,8,8,2,128]{4,1,2,0,3:T(8,128)S(1)} copy(f32[1,8,8,2,128]{4,2,3,1,0:T(8,128)} %bitcast.56) | data formatting | bytes 131072 | tf_op jit(solution)/shard_map/stack | solution.py:448
  1.6 3.0 %collective-permute-start = (f32[2,8,2,8,128]{4,3,1,0,2:T(8,128)S(1)}, f32[2,8,2,8,128]{4,3,1,0,2:T(8,128)S(1)}, u32[]{:S(2)}, u32[]{:S(2)}) collective-permute-start(f32[2,8,2,8,128]{4,3,1,0,2:T(8,128)S(1)} %maximum_bitcast_fusion), channel_id=1, source_target_pairs={{0,16},{16,0},{1,17},{17,1},{2,18},{18,2},{3,19},{19,3},{4,20},{20... | collective-permute-start | bytes 393224 | tf_op jit(solution)/shard_map/ppermute | solution.py:395
  4.6 3.5 %collective-permute-done = f32[2,8,2,8,128]{4,3,1,0,2:T(8,128)S(1)} collective-permute-done((f32[2,8,2,8,128]{4,3,1,0,2:T(8,128)S(1)}, f32[2,8,2,8,128]{4,3,1,0,2:T(8,128)S(1)}, u32[]{:S(2)}, u32[]{:S(2)}) %collective-permute-start) | collective-permute-done | bytes 131104 | tf_op jit(solution)/shard_map/ppermute | solution.py:395
  8.2 0.4 collective-permute-start.1
  8.6 0.2 collective-permute-start.2
  8.7 2.8 %collective-permute-done.1 = f32[2,8,16,128]{3,2,1,0:T(8,128)S(1)} collective-permute-done((f32[2,8,16,128]{3,2,1,0:T(8,128)S(1)}, f32[2,8,16,128]{3,2,1,0:T(8,128)S(1)}, u32[]{:S(2)}, u32[]{:S(2)}) %collective-permute-start.1) | collective-permute-done | bytes 131104 | tf_op jit(solution)/shard_map/ppermute | solution.py:387
  11.6 2.8 %collective-permute-done.2 = f32[2,8,16,128]{3,2,1,0:T(8,128)S(1)} collective-permute-done((f32[2,8,16,128]{3,2,1,0:T(8,128)S(1)}, f32[2,8,16,128]{3,2,1,0:T(8,128)S(1)}, u32[]{:S(2)}, u32[]{:S(2)}) %collective-permute-start.2) | collective-permute-done | bytes 131104 | tf_op jit(solution)/shard_map/ppermute | solution.py:387
  14.4 1.6 %collective-permute-start.3 = (f32[9,3,16,128]{3,2,1,0:T(8,128)S(1)}, f32[9,3,16,128]{3,2,1,0:T(8,128)S(1)}, u32[]{:S(2)}, u32[]{:S(2)}) collective-permute-start(f32[9,3,16,128]{3,2,1,0:T(8,128)S(1)} %pad_maximum_fusion.3), channel_id=1, source_target_pairs={{0,4},{4,8},{8,12},{12,0},{1,5},{5,9},{9,13},{13,1},{2,6},{6,10},{... | collective-permute-start | bytes 663560 | tf_op jit(solution)/shard_map/ppermute | solution.py:387
  16.1 2.3 %collective-permute-start.4 = (f32[9,3,16,128]{3,2,1,0:T(8,128)S(1)}, f32[9,3,16,128]{3,2,1,0:T(8,128)S(1)}, u32[]{:S(2)}, u32[]{:S(2)}) collective-permute-start(f32[9,3,16,128]{3,2,1,0:T(8,128)S(1)} %pad_maximum_fusion.4), channel_id=1, source_target_pairs={{0,12},{4,0},{8,4},{12,8},{1,13},{5,1},{9,5},{13,9},{2,14},{6,2},{... | collective-permute-start | bytes 663560 | tf_op jit(solution)/shard_map/ppermute | solution.py:387
  18.4 0.1 stack.52.flags.refs_0_
  18.5 6.1 %collective-permute-done.3.ylo = f32[9,3,16,128]{3,2,1,0:T(8,128)S(1)} collective-permute-done((f32[9,3,16,128]{3,2,1,0:T(8,128)S(1)}, f32[9,3,16,128]{3,2,1,0:T(8,128)S(1)}, u32[]{:S(2)}, u32[]{:S(2)}) %collective-permute-start.3) | collective-permute-done | bytes 221216 | tf_op jit(solution)/shard_map/ppermute | solution.py:387
  24.6 3.4 %collective-permute-done.4.yhi = f32[9,3,16,128]{3,2,1,0:T(8,128)S(1)} collective-permute-done((f32[9,3,16,128]{3,2,1,0:T(8,128)S(1)}, f32[9,3,16,128]{3,2,1,0:T(8,128)S(1)}, u32[]{:S(2)}, u32[]{:S(2)}) %collective-permute-start.4) | collective-permute-done | bytes 221216 | tf_op jit(solution)/shard_map/ppermute | solution.py:387
  28.0 3.2 %shard_map.41 = (f32[18,3,32,128]{3,2,1,0:T(8,128)S(1)}, f32[18,3,16,128]{3,2,1,0:T(8,128)S(1)}, f32[18,3,16,128]{3,2,1,0:T(8,128)S(1)}, f32[8,2,16,128]{3,2,1,0...) custom-call(s32[6]{0:T(128)S(1)} %stack.52.flags.refs_0_, ...), custom_call_target="tpu_custom_call" | custom-call | tf_op jit(solution)/shard_map/pallas_call | solution.py:426
  31.3 0.1 collective-permute-start.5
  31.4 0.5 collective-permute-start.6
  31.9 2.1 %collective-permute-done.5 = f32[192,128]{1,0:T(8,128)S(1)} collective-permute-done((f32[192,128]{1,0:T(8,128)S(1)}, f32[192,128]{1,0:T(8,128)S(1)}, u32[]{:S(2)}, u32[]{:S(2)}) %collective-permute-start.5) | collective-permute-done | bytes 98336 | tf_op jit(solution)/shard_map/ppermute | solution.py:387
  34.0 2.2 %collective-permute-done.6 = f32[192,128]{1,0:T(8,128)S(1)} collective-permute-done((f32[192,128]{1,0:T(8,128)S(1)}, f32[192,128]{1,0:T(8,128)S(1)}, u32[]{:S(2)}, u32[]{:S(2)}) %collective-permute-start.6) | collective-permute-done | bytes 98336 | tf_op jit(solution)/shard_map/ppermute | solution.py:387
  36.3 1.8 %collective-permute-start.9 = (f32[320,128]{1,0:T(8,128)S(1)}, f32[320,128]{1,0:T(8,128)S(1)}, u32[]{:S(2)}, u32[]{:S(2)}) collective-permute-start(f32[320,128]{1,0:T(8,128)S(1)} %get-tuple-element.26), channel_id=1, source_target_pairs={{0,12},{4,0},{8,4},{12,8},{1,13},{5,1},{9,5},{13,9},{2,14},{6,2},{... | collective-permute-start | bytes 491528 | tf_op jit(solution)/shard_map/ppermute | solution.py:387
  38.1 0.3 collective-permute-start.7
  38.4 0.9 %collective-permute-start.8 = (f32[128,128]{1,0:T(8,128)S(1)}, f32[128,128]{1,0:T(8,128)S(1)}, u32[]{:S(2)}, u32[]{:S(2)}) collective-permute-start(f32[128,128]{1,0:T(8,128)S(1)} %bitcast.42), channel_id=1, source_target_pairs={{0,8},{4,12},{8,0},{12,4},{1,9},{5,13},{9,1},{13,5},{2,10},{6,14},... | collective-permute-start | bytes 196616 | tf_op jit(solution)/shard_map/ppermute | solution.py:387
  39.3 3.6 %collective-permute-done.9 = f32[320,128]{1,0:T(8,128)S(1)} collective-permute-done((f32[320,128]{1,0:T(8,128)S(1)}, f32[320,128]{1,0:T(8,128)S(1)}, u32[]{:S(2)}, u32[]{:S(2)}) %collective-permute-start.9) | collective-permute-done | bytes 163872 | tf_op jit(solution)/shard_map/ppermute | solution.py:387
  42.9 3.6 %collective-permute-done.7 = f32[320,128]{1,0:T(8,128)S(1)} collective-permute-done((f32[320,128]{1,0:T(8,128)S(1)}, f32[320,128]{1,0:T(8,128)S(1)}, u32[]{:S(2)}, u32[]{:S(2)}) %collective-permute-start.7) | collective-permute-done | bytes 163872 | tf_op jit(solution)/shard_map/ppermute | solution.py:387
  46.5 3.1 %collective-permute-done.8 = f32[128,128]{1,0:T(8,128)S(1)} collective-permute-done((f32[128,128]{1,0:T(8,128)S(1)}, f32[128,128]{1,0:T(8,128)S(1)}, u32[]{:S(2)}, u32[]{:S(2)}) %collective-permute-start.8) | collective-permute-done | bytes 65568 | tf_op jit(solution)/shard_map/ppermute | solution.py:387
  49.6 7.3 %shard_map.42 = (f32[8,8,256]{2,1,0:T(8,128)}, f32[8,8,256]{2,1,0:T(8,128)}) custom-call(s32[6]{0:T(128)S(1)} %stack.52.flags.refs_0_, f32[2,4,2,8,128]{4,3,2,1,0:T(8,128)S(1)} %pad_maximum_fusion.9.refs_1_, f32[2,4,2,8,128]{4,3,2,1,0:T(8,128)S(1)} %bitcast.46, f32[2,4,2,8,128]{4,3,2,1,0:T(8,128)S(1)} %bitcast.48, f32[2,4,2,8,128]{4,3,2,1,0:T(8,128)S(1)} %bitcast.45, ...), custom_call_target="tpu_custom_call" | custom-call | tf_op jit(solution)/shard_map/pallas_call | solution.py:426
  (26 shorter events, 0.4 us)
Async XLA Ops:
  0.6 0.9 %copy-start = (f32[8,8,256]{2,1,0:T(8,128)S(1)}, f32[8,8,256]{2,1,0:T(8,128)}, u32[]{:S(2)}) copy-start(f32[8,8,256]{2,1,0:T(8,128)} %param.3) | copy-start | bytes 196612
  1.6 6.5 %collective-permute-start = (f32[2,8,2,8,128]{4,3,1,0,2:T(8,128)S(1)}, f32[2,8,2,8,128]{4,3,1,0,2:T(8,128)S(1)}, u32[]{:S(2)}, u32[]{:S(2)}) collective-permute-start(f32[2,8,2,8,128]{4,3,1,0,2:T(8,128)S(1)} %maximum_bitcast_fusion), channel_id=1, source_target_pairs={{0,16},{16,0},{1,17},{17,1},{2,18},{18,2},{3,19},{19,3},{4,20},{20... | collective-permute-start | bytes 393224 | tf_op jit(solution)/shard_map/ppermute | solution.py:395
  8.2 3.4 %collective-permute-start.1 = (f32[2,8,16,128]{3,2,1,0:T(8,128)S(1)}, f32[2,8,16,128]{3,2,1,0:T(8,128)S(1)}, u32[]{:S(2)}, u32[]{:S(2)}) collective-permute-start(f32[2,8,16,128]{3,2,1,0:T(8,128)S(1)} %get-tuple-element.18), channel_id=1, source_target_pairs={{0,3},{1,0},{2,1},{3,2},{4,7},{5,4},{6,5},{7,6},{8,11},{9,8},{10,9... | collective-permute-start | bytes 393224 | tf_op jit(solution)/shard_map/ppermute | solution.py:387
  8.6 5.8 %collective-permute-start.2 = (f32[2,8,16,128]{3,2,1,0:T(8,128)S(1)}, f32[2,8,16,128]{3,2,1,0:T(8,128)S(1)}, u32[]{:S(2)}, u32[]{:S(2)}) collective-permute-start(f32[2,8,16,128]{3,2,1,0:T(8,128)S(1)} %get-tuple-element.19), channel_id=1, source_target_pairs={{0,1},{1,2},{2,3},{3,0},{4,5},{5,6},{6,7},{7,4},{8,9},{9,10},{10,1... | collective-permute-start | bytes 393224 | tf_op jit(solution)/shard_map/ppermute | solution.py:387
  14.4 10.2 %collective-permute-start.3 = (f32[9,3,16,128]{3,2,1,0:T(8,128)S(1)}, f32[9,3,16,128]{3,2,1,0:T(8,128)S(1)}, u32[]{:S(2)}, u32[]{:S(2)}) collective-permute-start(f32[9,3,16,128]{3,2,1,0:T(8,128)S(1)} %pad_maximum_fusion.3), channel_id=1, source_target_pairs={{0,4},{4,8},{8,12},{12,0},{1,5},{5,9},{9,13},{13,1},{2,6},{6,10},{... | collective-permute-start | bytes 663560 | tf_op jit(solution)/shard_map/ppermute | solution.py:387
  16.1 11.9 %collective-permute-start.4 = (f32[9,3,16,128]{3,2,1,0:T(8,128)S(1)}, f32[9,3,16,128]{3,2,1,0:T(8,128)S(1)}, u32[]{:S(2)}, u32[]{:S(2)}) collective-permute-start(f32[9,3,16,128]{3,2,1,0:T(8,128)S(1)} %pad_maximum_fusion.4), channel_id=1, source_target_pairs={{0,12},{4,0},{8,4},{12,8},{1,13},{5,1},{9,5},{13,9},{2,14},{6,2},{... | collective-permute-start | bytes 663560 | tf_op jit(solution)/shard_map/ppermute | solution.py:387
  31.3 2.7 %collective-permute-start.5 = (f32[192,128]{1,0:T(8,128)S(1)}, f32[192,128]{1,0:T(8,128)S(1)}, u32[]{:S(2)}, u32[]{:S(2)}) collective-permute-start(f32[192,128]{1,0:T(8,128)S(1)} %get-tuple-element.28), channel_id=1, source_target_pairs={{0,3},{1,0},{2,1},{3,2},{4,7},{5,4},{6,5},{7,6},{8,11},{9,8},{10,9... | collective-permute-start | bytes 294920 | tf_op jit(solution)/shard_map/ppermute | solution.py:387
  31.4 4.8 %collective-permute-start.6 = (f32[192,128]{1,0:T(8,128)S(1)}, f32[192,128]{1,0:T(8,128)S(1)}, u32[]{:S(2)}, u32[]{:S(2)}) collective-permute-start(f32[192,128]{1,0:T(8,128)S(1)} %get-tuple-element.29), channel_id=1, source_target_pairs={{0,1},{1,2},{2,3},{3,0},{4,5},{5,6},{6,7},{7,4},{8,9},{9,10},{10,1... | collective-permute-start | bytes 294920 | tf_op jit(solution)/shard_map/ppermute | solution.py:387
  36.3 6.6 %collective-permute-start.9 = (f32[320,128]{1,0:T(8,128)S(1)}, f32[320,128]{1,0:T(8,128)S(1)}, u32[]{:S(2)}, u32[]{:S(2)}) collective-permute-start(f32[320,128]{1,0:T(8,128)S(1)} %get-tuple-element.26), channel_id=1, source_target_pairs={{0,12},{4,0},{8,4},{12,8},{1,13},{5,1},{9,5},{13,9},{2,14},{6,2},{... | collective-permute-start | bytes 491528 | tf_op jit(solution)/shard_map/ppermute | solution.py:387
  38.1 8.4 %collective-permute-start.7 = (f32[320,128]{1,0:T(8,128)S(1)}, f32[320,128]{1,0:T(8,128)S(1)}, u32[]{:S(2)}, u32[]{:S(2)}) collective-permute-start(f32[320,128]{1,0:T(8,128)S(1)} %get-tuple-element.27), channel_id=1, source_target_pairs={{0,4},{4,8},{8,12},{12,0},{1,5},{5,9},{9,13},{13,1},{2,6},{6,10},{... | collective-permute-start | bytes 491528 | tf_op jit(solution)/shard_map/ppermute | solution.py:387
  38.4 11.2 %collective-permute-start.8 = (f32[128,128]{1,0:T(8,128)S(1)}, f32[128,128]{1,0:T(8,128)S(1)}, u32[]{:S(2)}, u32[]{:S(2)}) collective-permute-start(f32[128,128]{1,0:T(8,128)S(1)} %bitcast.42), channel_id=1, source_target_pairs={{0,8},{4,12},{8,0},{12,4},{1,9},{5,13},{9,1},{13,5},{2,10},{6,14},... | collective-permute-start | bytes 196616 | tf_op jit(solution)/shard_map/ppermute | solution.py:387

commit v2 on v1

--- a/solution.py
+++ b/solution.py
@@ -255,11 +255,11 @@
     coarse[...] = flat[pl.ds(0, total // 2, stride=2), :] + flat[pl.ds(1, total // 2, stride=2), :]
 
 
-def after_kernel(flags, *refs, count, offsets):
+def after_kernel(places, *refs, count):
     blocks = refs[:count]
     (kap, diag, inv, xpre, rown, rlo, rhi, sol, resid) = refs[count : count + 9]
     (k1, d1, i1, r1, x1, va1, wa1, vb1, wb1, k2, d2, i2, r2, x2, va2, wa2, vb2, wb2, flat, va, wa, vb, wb, res, acc) = refs[count + 9 :]
-    me_x, me_y = flags[4], flags[5]
+    me_x, me_y = places[0], places[1]
     zero_pads((k1, va1, wa1, vb1, wb1, k2, va2, wa2, vb2, wb2, va, wa, vb, wb))
     each = blocks[0].shape[1]
     xc = blocks[0].shape[3]
@@ -269,8 +269,8 @@
     for ref in (k1, va1, wa1, vb1, wb1):
         zero_rows(ref, edge)
     zero_rows(x1, list(range(lo1)) + list(range(hi1, hi1 + COARSE_PAD)))
-    for block, offset in zip(blocks, offsets):
-        at = lax.rem(me_y - offset + count, count) * each + COARSE_PAD
+    for number, block in enumerate(blocks):
+        at = places[2 + number] * each + COARSE_PAD
         for y in range(each):
             k1[at + y, :, PAD : PAD + xc, :] = block[0, y] * 0.25
             r1[at + y] = block[1, y]
@@ -387,6 +387,25 @@
     return lax.ppermute(values, axis, [(i, (i + step) % count) for i in range(count)])
 
 
+def exchange(to_low, to_high, axis, across=None):
+    count = lax.axis_size(axis)
+    if count % 2:
+        return ring(to_high, axis, 1), ring(to_low, axis, -1)
+    odd = lax.axis_index(axis) % 2 == 1
+    inner = [i + 1 if i % 2 else i - 1 for i in range(count)]
+    one = lax.ppermute(jnp.where(odd, to_low, to_high), axis, [(i, i ^ 1) for i in range(count)])
+    names, pairs = axis, [(i, t % count) for i, t in enumerate(inner)]
+    if across is not None and lax.axis_size(across) % 2 == 0:
+        names = (across, axis)
+        pairs = [
+            (x * count + i, x * count + t if 0 <= t < count else (x ^ 1) * count + i)
+            for x in range(lax.axis_size(across))
+            for i, t in enumerate(inner)
+        ]
+    two = lax.ppermute(jnp.where(odd, to_high, to_low), names, pairs)
+    return jnp.where(odd, one, two), jnp.where(odd, two, one)
+
+
 def gather_first(values, axis, dim):
     count = lax.axis_size(axis)
     if count == 1:
@@ -399,6 +418,44 @@
         )
     every = lax.all_gather(values, axis)
     return jnp.concatenate([every[i] for i in range(count)], axis=dim)
+
+
+def gather_second(block, low_edge, high_edge, me, count):
+    size = block.size // LANES
+    shape = block.shape
+    low_edge = low_edge.reshape(-1, LANES)
+    high_edge = high_edge.reshape(-1, LANES)
+    block_rows = block.reshape(size, LANES)
+    blocks, sources = [block], [me]
+    low = high = low_edge
+    if count == 4:
+        odd = me % 2 == 1
+        got = []
+        for step in (1, 2, 3):
+            payload = block_rows
+            if step != 2:
+                edge = jnp.where(odd == (step == 1), low_edge, high_edge)
+                payload = jnp.concatenate([block_rows, edge], axis=0)
+            got.append(lax.ppermute(payload, "gy", [(i, i ^ step) for i in range(count)]))
+            blocks.append(got[-1][:size].reshape(shape))
+            sources.append(me ^ step)
+        low = jnp.where(odd, got[0][size:], got[2][size:])
+        high = jnp.where(odd, got[2][size:], got[0][size:])
+    else:
+        for step in range(1, count):
+            parts = [block_rows]
+            if step == 1:
+                parts.append(high_edge)
+            if step == count - 1:
+                parts.append(low_edge)
+            got = ring(jnp.concatenate(parts, axis=0), "gy", step)
+            blocks.append(got[:size].reshape(shape))
+            sources.append((me - step) % count)
+            if step == 1:
+                low = got[size : size + high_edge.shape[0]]
+            if step == count - 1:
+                high = got[got.shape[0] - low_edge.shape[0] :]
+    return blocks, sources, low, high
 
 
 def halo_tile(from_low, from_high, has_low, has_high):
@@ -438,7 +495,7 @@
     tiles = bz // LANES
     nx, ny, nz = (lax.axis_size(a) for a in ("gx", "gy", "gz"))
     ix, iy, iz = (lax.axis_index(a) for a in ("gx", "gy", "gz"))
-    flags = jnp.stack([iz > 0, iz < nz - 1, iy > 0, iy < ny - 1, ix, iy]).astype(jnp.int32)
+    flags = jnp.stack([iz > 0, iz < nz - 1, iy > 0, iy < ny - 1]).astype(jnp.int32)
     has_left, has_right = iz > 0, iz < nz - 1
     x_count = bx * nx
 
@@ -447,12 +504,15 @@
 
     both = jnp.stack([conductivity, source]).reshape(2, bx, by, tiles, LANES)
     both = gather_first(both.transpose(0, 2, 3, 1, 4), "gx", 3)
-    left = ring(both[:, :, tiles - 1], "gz", 1)
-    right = ring(both[:, :, 0], "gz", -1)
+    left, right = exchange(both[:, :, 0], both[:, :, tiles - 1], "gz")
     halo = halo_tile(left, right, has_left, has_right)
     own = jnp.concatenate([both, halo[:, :, None]], axis=2)
-    ylo = ring(jnp.concatenate([own[0, by - HALO :], own[1, by - HALO + 1 :]], axis=0), "gy", 1)
-    yhi = ring(jnp.concatenate([own[0, :HALO], own[1, : HALO - 1]], axis=0), "gy", -1)
+    ylo, yhi = exchange(
+        jnp.concatenate([own[0, :HALO], own[1, : HALO - 1]], axis=0),
+        jnp.concatenate([own[0, by - HALO :], own[1, by - HALO + 1 :]], axis=0),
+        "gy",
+        "gx",
+    )
 
     ext = by + 2 * HALO
     padded = x_count + 2 * PAD
@@ -479,8 +539,7 @@
     def with_tile(t):
         return jnp.concatenate([small, rpre[:, t].reshape(by * x_count, LANES)], axis=0)
 
-    left = ring(with_tile(tiles - 1), "gz", 1)
-    right = ring(with_tile(0), "gz", -1)
+    left, right = exchange(with_tile(0), with_tile(tiles - 1), "gz")
     halo = halo_tile(left, right, has_left, has_right)
     cut = 2 * each * xc
     coarse_halo = halo[:cut].reshape(2, each, 1, xc, LANES)
@@ -488,25 +547,7 @@
     rown = jnp.concatenate([rpre, halo[cut:].reshape(by, 1, x_count, LANES)], axis=1)
     flat_coarse = coarse_own.reshape(-1, LANES)
     edge = HALO - 1
-    n_flat = flat_coarse.shape[0]
-    blocks, offsets = [coarse_own], [0]
-    rlo = rhi = rown[:edge]
-    for step in range(1, ny):
-        parts = [flat_coarse]
-        if step == 1:
-            parts.append(rown[by - edge :].reshape(-1, LANES))
-        if step == ny - 1:
-            parts.append(rown[:edge].reshape(-1, LANES))
-        got = ring(jnp.concatenate(parts, axis=0), "gy", step)
-        blocks.append(got[:n_flat].reshape(coarse_own.shape))
-        offsets.append(step)
-        rest = got[n_flat:]
-        size = edge * (tiles + 1) * x_count
-        if step == 1:
-            rlo = rest[:size].reshape(edge, tiles + 1, x_count, LANES)
-            rest = rest[size:]
-        if step == ny - 1:
-            rhi = rest[:size].reshape(edge, tiles + 1, x_count, LANES)
+    blocks, sources, rlo, rhi = gather_second(coarse_own, rown[:edge], rown[by - edge :], iy, ny)
 
     yc = each * ny
     tiles1 = tiles // 2 + 1
@@ -518,8 +559,10 @@
     plain2 = (y2 + 2, 1, x2, LANES)
     flat_rows = max(y2 * xc, tiles1 * (ext // 2 + 1) * x_count)
 
+    places = jnp.stack([ix, iy] + sources).astype(jnp.int32)
+
     def kernel(*refs):
-        after_kernel(*refs, count=len(blocks), offsets=offsets)
+        after_kernel(*refs, count=len(blocks))
 
     sol, resid = call(
         kernel,
@@ -527,7 +570,9 @@
         [vmem(wide1)] + [vmem(plain1)] * 4 + [vmem(wide1)] * 4
         + [vmem(wide2)] + [vmem(plain2)] * 4 + [vmem(wide2)] * 4
         + [vmem((flat_rows, LANES))] + [vmem(wide)] * 4 + [vmem(plain)] * 2,
-        [flags] + blocks + [kap, diag, inv, xpre, rown, rlo, rhi],
+        [places] + blocks
+        + [kap, diag, inv, xpre, rown]
+        + [e.reshape(edge, tiles + 1, x_count, LANES) for e in (rlo, rhi)],
     )
     return sol, resid
 

time: 57 us -> 53.5 us (0.939)
  waiting for transfers between devices: 33.2 us -> 26.3 us
  starting transfers between devices: 11 us -> 14.2 us
    ppermute x9, waiting for transfers between devices: 29.7 us -> 22.8 us  [the longest x3 10.7 us: exchange(): two = lax.ppermute(jnp.where(odd, to_high, to_low), names, pairs)]
    ppermute x9, starting transfers between devices: 8 us -> 11.2 us  [the longest x3 5.17 us: exchange(): two = lax.ppermute(jnp.where(odd, to_high, to_low), names, pairs)]
  transfers between devices with their start and end apart: 10 -> 10, of which waited for: 10 -> 8; matrix products, arithmetic and copies ran while one was open for 0% -> 0% of each run, Pallas kernels for 0% -> 0%
where the time goes in v2:
time: 53.5 us; the launch traced here: 53.4 us
  waiting for transfers between devices  26.3 us (49%)
  starting transfers between devices  14.2 us (27%)
  Pallas kernels  10.5 us (20%)
  local copies, waits for them, and re-layouts  1.04 us (2%)
  between operations  0.82 us (2%)
    ppermute x3, waiting for transfers between devices, exchange(): two = lax.ppermute(jnp.where(odd, to_high, to_low), names, pairs)  10.7 us
    ppermute x3, waiting for transfers between devices, gather_second(): lax.ppermute(payload, 'gy', [(i, i ^ step) for i in range(count)])  10.7 us
    pallas_call x2, Pallas kernels, call(): pl.pallas_call(kernel, out_shape=out_shapes, in_specs=[pl.BlockSpec(memor...  10.5 us
    ppermute x3, starting transfers between devices, exchange(): two = lax.ppermute(jnp.where(odd, to_high, to_low), names, pairs)  5.17 us
    ppermute x3, starting transfers between devices, gather_second(): lax.ppermute(payload, 'gy', [(i, i ^ step) for i in range(count)])  4.24 us
    ppermute x1, waiting for transfers between devices, gather_first(): other = lax.ppermute(values, axis, [(0, 1), (1, 0)])  3.5 us
    ppermute x1, starting transfers between devices, gather_first(): other = lax.ppermute(values, axis, [(0, 1), (1, 0)])  3.03 us
    ppermute x3, starting transfers between devices, exchange(): lax.ppermute(jnp.where(odd, to_low, to_high), axis, [(i, i ^ 1) for i in...  1.8 us
  transfers between devices with their start and end apart: 10, of which 8 were waited for; matrix products, arithmetic and copies ran while one was open for 0% of the time, Pallas kernels for 0%

profile of v2, /device:TPU:0, one launch (start us, length us, event | category | flops | bytes accessed | tf_op | source)
XLA Modules:
  0.0 53.4 jit_solution(306439411562730471)
XLA Ops:
  0.6 0.9 %copy.6 = f32[1,8,8,2,128]{4,1,2,0,3:T(8,128)S(1)} copy(f32[1,8,8,2,128]{4,2,3,1,0:T(8,128)} %bitcast.59) | data formatting | bytes 131072 | tf_op jit(solution)/shard_map/stack | solution.py:505
  1.6 3.0 %collective-permute-start = (f32[2,8,2,8,128]{4,3,1,0,2:T(8,128)S(1)}, f32[2,8,2,8,128]{4,3,1,0,2:T(8,128)S(1)}, u32[]{:S(2)}, u32[]{:S(2)}) collective-permute-start(f32[2,8,2,8,128]{4,3,1,0,2:T(8,128)S(1)} %maximum_bitcast_fusion), channel_id=1, source_target_pairs={{0,16},{16,0},{1,17},{17,1},{2,18},{18,2},{3,19},{19,3},{4,20},{20... | collective-permute-start | bytes 393224 | tf_op jit(solution)/shard_map/ppermute | solution.py:414
  4.6 3.5 %collective-permute-done = f32[2,8,2,8,128]{4,3,1,0,2:T(8,128)S(1)} collective-permute-done((f32[2,8,2,8,128]{4,3,1,0,2:T(8,128)S(1)}, f32[2,8,2,8,128]{4,3,1,0,2:T(8,128)S(1)}, u32[]{:S(2)}, u32[]{:S(2)}) %collective-permute-start) | collective-permute-done | bytes 131104 | tf_op jit(solution)/shard_map/ppermute | solution.py:414
  8.2 0.1 collective-permute-start.2
  8.3 1.9 %collective-permute-start.1 = (f32[2,8,16,128]{3,2,1,0:T(8,128)S(1)}, f32[2,8,16,128]{3,2,1,0:T(8,128)S(1)}, u32[]{:S(2)}, u32[]{:S(2)}) collective-permute-start(f32[2,8,16,128]{3,2,1,0:T(8,128)S(1)} %get-tuple-element.24), channel_id=1, source_target_pairs={{0,3},{1,2},{2,1},{3,0},{4,7},{5,6},{6,5},{7,4},{8,11},{9,10},{10,... | collective-permute-start | bytes 393224 | tf_op jit(solution)/shard_map/ppermute | solution.py:405
  10.1 3.5 %collective-permute-done.1 = f32[2,8,16,128]{3,2,1,0:T(8,128)S(1)} collective-permute-done((f32[2,8,16,128]{3,2,1,0:T(8,128)S(1)}, f32[2,8,16,128]{3,2,1,0:T(8,128)S(1)}, u32[]{:S(2)}, u32[]{:S(2)}) %collective-permute-start.1) | collective-permute-done | bytes 131104 | tf_op jit(solution)/shard_map/ppermute | solution.py:405
  13.8 1.7 %collective-permute-start.4 = (f32[9,3,16,128]{3,2,1,0:T(8,128)S(1)}, f32[9,3,16,128]{3,2,1,0:T(8,128)S(1)}, u32[]{:S(2)}, u32[]{:S(2)}) collective-permute-start(f32[9,3,16,128]{3,2,1,0:T(8,128)S(1)} %get-tuple-element.16), channel_id=1, source_target_pairs={{0,16},{4,8},{8,4},{12,28},{16,0},{20,24},{24,20},{28,12},{1,17},{... | collective-permute-start | bytes 663560 | tf_op jit(solution)/shard_map/ppermute | solution.py:405
  15.4 1.7 %collective-permute-start.3 = (f32[9,3,16,128]{3,2,1,0:T(8,128)S(1)}, f32[9,3,16,128]{3,2,1,0:T(8,128)S(1)}, u32[]{:S(2)}, u32[]{:S(2)}) collective-permute-start(f32[9,3,16,128]{3,2,1,0:T(8,128)S(1)} %get-tuple-element.17), channel_id=1, source_target_pairs={{0,4},{4,0},{8,12},{12,8},{1,5},{5,1},{9,13},{13,9},{2,6},{6,2},{1... | collective-permute-start | bytes 663560 | tf_op jit(solution)/shard_map/ppermute | solution.py:396
  17.1 0.1 add_convert_fusion.flags
  17.2 4.3 %collective-permute-done.4 = f32[9,3,16,128]{3,2,1,0:T(8,128)S(1)} collective-permute-done((f32[9,3,16,128]{3,2,1,0:T(8,128)S(1)}, f32[9,3,16,128]{3,2,1,0:T(8,128)S(1)}, u32[]{:S(2)}, u32[]{:S(2)}) %collective-permute-start.4) | collective-permute-done | bytes 221216 | tf_op jit(solution)/shard_map/ppermute | solution.py:405
  21.5 1.4 %collective-permute-done.3 = f32[9,3,16,128]{3,2,1,0:T(8,128)S(1)} collective-permute-done((f32[9,3,16,128]{3,2,1,0:T(8,128)S(1)}, f32[9,3,16,128]{3,2,1,0:T(8,128)S(1)}, u32[]{:S(2)}, u32[]{:S(2)}) %collective-permute-start.3) | collective-permute-done | bytes 221216 | tf_op jit(solution)/shard_map/ppermute | solution.py:396
  23.0 3.2 %shard_map.41 = (f32[18,3,32,128]{3,2,1,0:T(8,128)S(1)}, f32[18,3,16,128]{3,2,1,0:T(8,128)S(1)}, f32[18,3,16,128]{3,2,1,0:T(8,128)S(1)}, f32[8,2,16,128]{3,2,1,0...) custom-call(s32[4]{0:T(128)S(1)} %add_convert_fusion.flags, ...), custom_call_target="tpu_custom_call" | custom-call | tf_op jit(solution)/shard_map/pallas_call | solution.py:483
  26.3 0.1 collective-permute-start.6
  26.3 1.6 %collective-permute-start.5 = (f32[192,128]{1,0:T(8,128)S(1)}, f32[192,128]{1,0:T(8,128)S(1)}, u32[]{:S(2)}, u32[]{:S(2)}) collective-permute-start(f32[192,128]{1,0:T(8,128)S(1)} %get-tuple-element.30), channel_id=1, source_target_pairs={{0,3},{1,2},{2,1},{3,0},{4,7},{5,6},{6,5},{7,4},{8,11},{9,10},{10,... | collective-permute-start | bytes 294920 | tf_op jit(solution)/shard_map/ppermute | solution.py:405
  28.0 0.0 collective-permute-done.6
  28.0 2.9 %collective-permute-done.5 = f32[192,128]{1,0:T(8,128)S(1)} collective-permute-done((f32[192,128]{1,0:T(8,128)S(1)}, f32[192,128]{1,0:T(8,128)S(1)}, u32[]{:S(2)}, u32[]{:S(2)}) %collective-permute-start.5) | collective-permute-done | bytes 98336 | tf_op jit(solution)/shard_map/ppermute | solution.py:405
  31.0 1.7 %collective-permute-start.7 = (f32[320,128]{1,0:T(8,128)S(1)}, f32[320,128]{1,0:T(8,128)S(1)}, u32[]{:S(2)}, u32[]{:S(2)}) collective-permute-start(f32[320,128]{1,0:T(8,128)S(1)} %get-tuple-element.35), channel_id=1, source_target_pairs={{0,4},{4,0},{8,12},{12,8},{1,5},{5,1},{9,13},{13,9},{2,6},{6,2},{1... | collective-permute-start | bytes 491528 | tf_op jit(solution)/shard_map/ppermute | solution.py:439
  32.7 2.2 %collective-permute-start.9 = (f32[320,128]{1,0:T(8,128)S(1)}, f32[320,128]{1,0:T(8,128)S(1)}, u32[]{:S(2)}, u32[]{:S(2)}) collective-permute-start(f32[320,128]{1,0:T(8,128)S(1)} %get-tuple-element.34), channel_id=1, source_target_pairs={{0,12},{4,8},{8,4},{12,0},{1,13},{5,9},{9,5},{13,1},{2,14},{6,10},... | collective-permute-start | bytes 491528 | tf_op jit(solution)/shard_map/ppermute | solution.py:439
  35.0 0.1 stack.48.refs_0_
  35.0 0.3 collective-permute-start.8
  35.3 2.3 %collective-permute-done.7 = f32[320,128]{1,0:T(8,128)S(1)} collective-permute-done((f32[320,128]{1,0:T(8,128)S(1)}, f32[320,128]{1,0:T(8,128)S(1)}, u32[]{:S(2)}, u32[]{:S(2)}) %collective-permute-start.7) | collective-permute-done | bytes 163872 | tf_op jit(solution)/shard_map/ppermute | solution.py:439
  37.6 6.0 %collective-permute-done.9 = f32[320,128]{1,0:T(8,128)S(1)} collective-permute-done((f32[320,128]{1,0:T(8,128)S(1)}, f32[320,128]{1,0:T(8,128)S(1)}, u32[]{:S(2)}, u32[]{:S(2)}) %collective-permute-start.9) | collective-permute-done | bytes 163872 | tf_op jit(solution)/shard_map/ppermute | solution.py:439
  43.7 2.4 %collective-permute-done.8 = f32[128,128]{1,0:T(8,128)S(1)} collective-permute-done((f32[128,128]{1,0:T(8,128)S(1)}, f32[128,128]{1,0:T(8,128)S(1)}, u32[]{:S(2)}, u32[]{:S(2)}) %collective-permute-start.8) | collective-permute-done | bytes 65568 | tf_op jit(solution)/shard_map/ppermute | solution.py:439
  46.1 7.3 %shard_map.42 = (f32[8,8,256]{2,1,0:T(8,128)}, f32[8,8,256]{2,1,0:T(8,128)}) custom-call(s32[6]{0:T(128)S(1)} %stack.48.refs_0_, f32[2,4,2,8,128]{4,3,2,1,0:T(8,128)S(1)} %pad_maximum_fusion.9.refs_1_, f32[2,4,2,8,128]{4,3,2,1,0:T(8,128)S(1)} %bitcast.48, f32[2,4,2,8,128]{4,3,2,1,0:T(8,128)S(1)} %bitcast.51, f32[2,4,2,8,128]{4,3,2,1,0:T(8,128)S(1)} %bitcast.49, ...), custom_call_target="tpu_custom_call" | custom-call | tf_op jit(solution)/shard_map/pallas_call | solution.py:483
  (26 shorter events, 0.4 us)
Async XLA Ops:
  0.6 0.9 %copy-start = (f32[8,8,256]{2,1,0:T(8,128)S(1)}, f32[8,8,256]{2,1,0:T(8,128)}, u32[]{:S(2)}) copy-start(f32[8,8,256]{2,1,0:T(8,128)} %param.2) | copy-start | bytes 196612
  1.6 6.5 %collective-permute-start = (f32[2,8,2,8,128]{4,3,1,0,2:T(8,128)S(1)}, f32[2,8,2,8,128]{4,3,1,0,2:T(8,128)S(1)}, u32[]{:S(2)}, u32[]{:S(2)}) collective-permute-start(f32[2,8,2,8,128]{4,3,1,0,2:T(8,128)S(1)} %maximum_bitcast_fusion), channel_id=1, source_target_pairs={{0,16},{16,0},{1,17},{17,1},{2,18},{18,2},{3,19},{19,3},{4,20},{20... | collective-permute-start | bytes 393224 | tf_op jit(solution)/shard_map/ppermute | solution.py:414
  8.2 2.0 %collective-permute-start.2 = (f32[2,8,16,128]{3,2,1,0:T(8,128)S(1)}, f32[2,8,16,128]{3,2,1,0:T(8,128)S(1)}, u32[]{:S(2)}, u32[]{:S(2)}) collective-permute-start(f32[2,8,16,128]{3,2,1,0:T(8,128)S(1)} %get-tuple-element.25), channel_id=1, source_target_pairs={{0,1},{1,0},{2,3},{3,2},{4,5},{5,4},{6,7},{7,6},{8,9},{9,8},{10,11... | collective-permute-start | bytes 393224 | tf_op jit(solution)/shard_map/ppermute | solution.py:396
  8.3 5.4 %collective-permute-start.1 = (f32[2,8,16,128]{3,2,1,0:T(8,128)S(1)}, f32[2,8,16,128]{3,2,1,0:T(8,128)S(1)}, u32[]{:S(2)}, u32[]{:S(2)}) collective-permute-start(f32[2,8,16,128]{3,2,1,0:T(8,128)S(1)} %get-tuple-element.24), channel_id=1, source_target_pairs={{0,3},{1,2},{2,1},{3,0},{4,7},{5,6},{6,5},{7,4},{8,11},{9,10},{10,... | collective-permute-start | bytes 393224 | tf_op jit(solution)/shard_map/ppermute | solution.py:405
  13.8 7.8 %collective-permute-start.4 = (f32[9,3,16,128]{3,2,1,0:T(8,128)S(1)}, f32[9,3,16,128]{3,2,1,0:T(8,128)S(1)}, u32[]{:S(2)}, u32[]{:S(2)}) collective-permute-start(f32[9,3,16,128]{3,2,1,0:T(8,128)S(1)} %get-tuple-element.16), channel_id=1, source_target_pairs={{0,16},{4,8},{8,4},{12,28},{16,0},{20,24},{24,20},{28,12},{1,17},{... | collective-permute-start | bytes 663560 | tf_op jit(solution)/shard_map/ppermute | solution.py:405
  15.4 7.5 %collective-permute-start.3 = (f32[9,3,16,128]{3,2,1,0:T(8,128)S(1)}, f32[9,3,16,128]{3,2,1,0:T(8,128)S(1)}, u32[]{:S(2)}, u32[]{:S(2)}) collective-permute-start(f32[9,3,16,128]{3,2,1,0:T(8,128)S(1)} %get-tuple-element.17), channel_id=1, source_target_pairs={{0,4},{4,0},{8,12},{12,8},{1,5},{5,1},{9,13},{13,9},{2,6},{6,2},{1... | collective-permute-start | bytes 663560 | tf_op jit(solution)/shard_map/ppermute | solution.py:396
  26.3 1.7 %collective-permute-start.6 = (f32[192,128]{1,0:T(8,128)S(1)}, f32[192,128]{1,0:T(8,128)S(1)}, u32[]{:S(2)}, u32[]{:S(2)}) collective-permute-start(f32[192,128]{1,0:T(8,128)S(1)} %get-tuple-element.31), channel_id=1, source_target_pairs={{0,1},{1,0},{2,3},{3,2},{4,5},{5,4},{6,7},{7,6},{8,9},{9,8},{10,11... | collective-permute-start | bytes 294920 | tf_op jit(solution)/shard_map/ppermute | solution.py:396
  26.3 4.5 %collective-permute-start.5 = (f32[192,128]{1,0:T(8,128)S(1)}, f32[192,128]{1,0:T(8,128)S(1)}, u32[]{:S(2)}, u32[]{:S(2)}) collective-permute-start(f32[192,128]{1,0:T(8,128)S(1)} %get-tuple-element.30), channel_id=1, source_target_pairs={{0,3},{1,2},{2,1},{3,0},{4,7},{5,6},{6,5},{7,4},{8,11},{9,10},{10,... | collective-permute-start | bytes 294920 | tf_op jit(solution)/shard_map/ppermute | solution.py:405
  31.0 6.6 %collective-permute-start.7 = (f32[320,128]{1,0:T(8,128)S(1)}, f32[320,128]{1,0:T(8,128)S(1)}, u32[]{:S(2)}, u32[]{:S(2)}) collective-permute-start(f32[320,128]{1,0:T(8,128)S(1)} %get-tuple-element.35), channel_id=1, source_target_pairs={{0,4},{4,0},{8,12},{12,8},{1,5},{5,1},{9,13},{13,9},{2,6},{6,2},{1... | collective-permute-start | bytes 491528 | tf_op jit(solution)/shard_map/ppermute | solution.py:439
  32.7 10.9 %collective-permute-start.9 = (f32[320,128]{1,0:T(8,128)S(1)}, f32[320,128]{1,0:T(8,128)S(1)}, u32[]{:S(2)}, u32[]{:S(2)}) collective-permute-start(f32[320,128]{1,0:T(8,128)S(1)} %get-tuple-element.34), channel_id=1, source_target_pairs={{0,12},{4,8},{8,4},{12,0},{1,13},{5,9},{9,5},{13,1},{2,14},{6,10},... | collective-permute-start | bytes 491528 | tf_op jit(solution)/shard_map/ppermute | solution.py:439
  35.0 11.0 %collective-permute-start.8 = (f32[128,128]{1,0:T(8,128)S(1)}, f32[128,128]{1,0:T(8,128)S(1)}, u32[]{:S(2)}, u32[]{:S(2)}) collective-permute-start(f32[128,128]{1,0:T(8,128)S(1)} %bitcast.45), channel_id=1, source_target_pairs={{0,8},{4,12},{8,0},{12,4},{1,9},{5,13},{9,1},{13,5},{2,10},{6,14},... | collective-permute-start | bytes 196616 | tf_op jit(solution)/shard_map/ppermute | solution.py:439

commit v3 on v2

--- a/solution.py
+++ b/solution.py
@@ -35,6 +35,8 @@
     return centre, weights
 
 
+EDGE = 8
+COARSE_EDGE = 32
 CHUNK = 16
 
 
@@ -123,13 +125,23 @@
     chunks(lo, hi, body)
 
 
-def first_update(kap, inv, res, v, w, acc, lo, hi, scale, add):
+def accumulate(acc, y, x, step, add, own):
+    tiles = step.shape[0]
+    if own is not None:
+        if isinstance(y, int) and not own[0] <= y < own[1]:
+            return
+        tiles = own[2]
+    step = step[0:tiles]
+    acc[y, 0:tiles, x : x + 8, :] = acc[y, 0:tiles, x : x + 8, :] + step if add else step
+
+
+def first_update(kap, inv, res, v, w, acc, lo, hi, scale, add, own=None):
     def body(y):
         for x in tiles_of(inv):
             step = (inv[y, :, x : x + 8, :] * scale) * res[y, :, x : x + 8, :]
             v[y, :, PAD + x : PAD + x + 8, :] = step
             w[y, :, PAD + x : PAD + x + 8, :] = kap[y, :, PAD + x : PAD + x + 8, :] * step
-            acc[y, :, x : x + 8, :] = acc[y, :, x : x + 8, :] + step if add else step
+            accumulate(acc, y, x, step, add, own)
 
     loop(lo, hi, body)
 
@@ -166,14 +178,14 @@
     chunks(lo, hi, body)
 
 
-def smoothing_step(kap, diag, inv, res, old, new, acc, lo, hi, pair):
+def smoothing_step(kap, diag, inv, res, old, new, acc, lo, hi, pair, own=None):
     def body(first, rows):
         for x in tiles_of(diag):
             for y, k, centre, value in new_residuals(kap, diag, res, old[0], old[1], first, rows, x):
                 step = pair[0] * centre + (pair[1] * inv[y, :, x : x + 8, :]) * value
                 new[0][y, :, PAD + x : PAD + x + 8, :] = step
                 new[1][y, :, PAD + x : PAD + x + 8, :] = k * step
-                acc[y, :, x : x + 8, :] = acc[y, :, x : x + 8, :] + step
+                accumulate(acc, y, x, step, True, own)
 
     chunks(lo, hi, body)
 
@@ -205,44 +217,63 @@
     return jnp.concatenate([values[t] for t in range(values.shape[0])], axis=-1)
 
 
-def before_kernel(flags, own, ylo, yhi, kap, diag, inv, xout, rout, coarse, va, wa, vb, wb, res, acc, flat):
+def pack(pieces, width, from_end):
+    lane = lax.broadcasted_iota(jnp.int32, pieces[0].shape, 1)
+    out = jnp.zeros(pieces[0].shape, F32)
+    for i, piece in enumerate(pieces):
+        shift = (width * i + (width if from_end else 0)) % LANES
+        moved = pltpu.roll(piece, shift, 1) if shift else piece
+        out = jnp.where((lane >= width * i) & (lane < width * (i + 1)), moved, out)
+    return out
+
+
+def unpack(left, right, i, width):
+    lane = lax.broadcasted_iota(jnp.int32, left.shape, 1)
+    back = (LANES - width * i) % LANES
+    end = (LANES - width - width * i) % LANES
+    first = pltpu.roll(right, back, 1) if back else right
+    last = pltpu.roll(left, end, 1) if end else left
+    return jnp.where(lane < width, first, jnp.where(lane >= LANES - width, last, 0.0))
+
+
+def before_kernel(flags, own, zown, ylo, zlo, yhi, zhi, kap, diag, inv, xout, rout, coarse, to_left, to_right, va, wa, vb, wb, res, acc, flat):
     rows = own.shape[1]
+    tiles = own.shape[2]
     x_count = own.shape[3]
     inner = slice(PAD, PAD + x_count)
     last = HALO + rows
-    has_lo = flags[2] > 0
-    has_hi = flags[3] > 0
     zero_pads((kap, va, wa, vb, wb))
 
-    def fill(y):
-        kap[HALO + y, :, inner, :] = SCALE * own[0, y]
-        res[HALO + y] = own[1, y]
-
-    loop(0, rows, fill)
+    def fill(j, k, b, z, y, there):
+        left = jnp.where((flags[0] > 0) & there, z[0], 0.0)
+        right = jnp.where((flags[1] > 0) & there, z[1], 0.0)
+        kap[j, 0:tiles, inner, :] = jnp.where(there, SCALE * k, 0.0)
+        kap[j, tiles, inner, :] = SCALE * unpack(left, right, y, EDGE)
+        if b is not None:
+            res[j, 0:tiles] = b
+            res[j, tiles] = unpack(z[0], z[1], rows + y, EDGE)
+
+    for y in range(rows):
+        fill(HALO + y, own[0, y], own[1, y], zown, y, flags[4] > 0)
     for j in range(HALO):
-        kap[j, :, inner, :] = jnp.where(has_lo, SCALE * ylo[j], 0.0)
-        kap[last + j, :, inner, :] = jnp.where(has_hi, SCALE * yhi[j], 0.0)
-    for j in range(HALO - 1):
-        res[1 + j] = ylo[HALO + j]
-        res[last + j] = yhi[HALO + j]
+        b = ylo[HALO + j - 1] if j else None
+        fill(j, ylo[j], b, zlo, rows - HALO + j, flags[2] > 0)
+        b = yhi[HALO + j] if j < HALO - 1 else None
+        fill(last + j, yhi[j], b, zhi, j, flags[3] > 0)
     make_diagonal(kap, diag, inv, 1, last + HALO - 1)
     centre, weights = chebyshev_coefs(DEGREE, smooth_low)
-    first_update(kap, inv, res, va, wa, acc, 1, last + HALO - 1, 1.0 / centre, False)
+    first_update(kap, inv, res, va, wa, acc, 1, last + HALO - 1, 1.0 / centre, False, (HALO, last, tiles))
     old, new = (va, wa), (vb, wb)
     lo, hi = 2, last + HALO - 2
     for pair in weights:
-        smoothing_step(kap, diag, inv, res, old, new, acc, lo, hi, pair)
+        smoothing_step(kap, diag, inv, res, old, new, acc, lo, hi, pair, (HALO, last, tiles))
         old, new = new, old
         lo, hi = lo + 1, hi - 1
     residual_only(kap, diag, res, old[0], old[1], HALO, last)
-    tiles = rout.shape[1]
-
-    def emit(y):
+    pieces = []
+    for y in range(rows):
         xout[y] = acc[HALO + y, 0:tiles]
         rout[y] = res[HALO + y, 0:tiles]
-
-    loop(0, rows, emit)
-    pieces = []
     for source, offset in ((kap, PAD), (res, 0)):
         for y in range(0, rows, 2):
             both = (
@@ -253,27 +284,40 @@
     flat[...] = product(jnp.concatenate(pieces, axis=0), halving(tiles * LANES))
     total = flat.shape[0]
     coarse[...] = flat[pl.ds(0, total // 2, stride=2), :] + flat[pl.ds(1, total // 2, stride=2), :]
+    each, xc = rows // 2, x_count // 2
+    for out, from_end in ((to_left, False), (to_right, True)):
+        for i in range(2):
+            value = [coarse[(i * each + y) * xc : (i * each + y + 1) * xc, :] for y in range(each)]
+            out[i * xc : (i + 1) * xc, :] = pack(value, COARSE_EDGE, from_end)
+        value = [res[HALO + y, tiles - 1 if from_end else 0] for y in range(rows)]
+        out[2 * xc : 2 * xc + x_count, :] = pack(value, EDGE, from_end)
 
 
 def after_kernel(places, *refs, count):
-    blocks = refs[:count]
-    (kap, diag, inv, xpre, rown, rlo, rhi, sol, resid) = refs[count : count + 9]
-    (k1, d1, i1, r1, x1, va1, wa1, vb1, wb1, k2, d2, i2, r2, x2, va2, wa2, vb2, wb2, flat, va, wa, vb, wb, res, acc) = refs[count + 9 :]
+    blocks, zblocks = refs[:count], refs[count : 2 * count]
+    refs = refs[2 * count :]
+    (kap, diag, inv, xpre, rown, zown, rlo, zlo, rhi, zhi, sol, resid) = refs[:12]
+    (k1, d1, i1, r1, x1, va1, wa1, vb1, wb1, k2, d2, i2, r2, x2, va2, wa2, vb2, wb2, flat, va, wa, vb, wb, res, acc) = refs[12:]
     me_x, me_y = places[0], places[1]
     zero_pads((k1, va1, wa1, vb1, wb1, k2, va2, wa2, vb2, wb2, va, wa, vb, wb))
     each = blocks[0].shape[1]
-    xc = blocks[0].shape[3]
+    xc = blocks[0].shape[2]
+    tiles = xpre.shape[1]
     yc = each * count
     lo1, hi1 = COARSE_PAD, COARSE_PAD + yc
     edge = [lo1 - 1, hi1]
     for ref in (k1, va1, wa1, vb1, wb1):
         zero_rows(ref, edge)
     zero_rows(x1, list(range(lo1)) + list(range(hi1, hi1 + COARSE_PAD)))
-    for number, block in enumerate(blocks):
-        at = places[2 + number] * each + COARSE_PAD
+    for number, (block, z) in enumerate(zip(blocks, zblocks)):
+        at = places[4 + number] * each + COARSE_PAD
+        left = jnp.where(places[2] > 0, z[0, 0], 0.0)
+        right = jnp.where(places[3] > 0, z[1, 0], 0.0)
         for y in range(each):
-            k1[at + y, :, PAD : PAD + xc, :] = block[0, y] * 0.25
-            r1[at + y] = block[1, y]
+            k1[at + y, 0, PAD : PAD + xc, :] = block[0, y] * 0.25
+            k1[at + y, 1, PAD : PAD + xc, :] = unpack(left, right, y, COARSE_EDGE) * 0.25
+            r1[at + y, 0] = block[1, y]
+            r1[at + y, 1] = unpack(z[0, 1], z[1, 1], y, COARSE_EDGE)
     make_diagonal(k1, d1, i1, lo1, hi1)
     centre, weights = chebyshev_coefs(DEGREE, smooth_low)
     first_update(k1, i1, r1, va1, wa1, x1, lo1, hi1, 1.0 / centre, False)
@@ -357,19 +401,22 @@
                 acc[j, t] = xpre[j - HALO, t] + value
     times(kap, va, wa, 0, rows + 2 * HALO)
 
-    def fill(y):
-        res[HALO + y] = rown[y]
-
-    loop(0, rows, fill)
-    for j in range(HALO - 1):
-        res[1 + j] = rlo[j]
-        res[last + j] = rhi[j]
+    edge = HALO - 1
+    for j in range(-edge, rows + edge):
+        if j < 0:
+            source, z, i, y = rlo, zlo, edge + j, rows + j
+        elif j < rows:
+            source, z, i, y = rown, zown, j, j
+        else:
+            source, z, i, y = rhi, zhi, j - rows, j - rows
+        res[HALO + j, 0:tiles] = source[i]
+        res[HALO + j, tiles] = unpack(z[0], z[1], y, EDGE)
     residual_only(kap, diag, res, va, wa, 1, last + HALO - 1)
-    first_update(kap, inv, res, va, wa, acc, 1, last + HALO - 1, 1.0 / centre, True)
+    first_update(kap, inv, res, va, wa, acc, 1, last + HALO - 1, 1.0 / centre, True, (HALO, last, tiles))
     old, new = (va, wa), (vb, wb)
     lo, hi = 2, last + HALO - 2
     for pair in weights:
-        smoothing_step(kap, diag, inv, res, old, new, acc, lo, hi, pair)
+        smoothing_step(kap, diag, inv, res, old, new, acc, lo, hi, pair, (HALO, last, tiles))
         old, new = new, old
         lo, hi = lo + 1, hi - 1
     residual_only(kap, diag, res, old[0], old[1], HALO, last)
@@ -406,6 +453,25 @@
     return jnp.where(odd, one, two), jnp.where(odd, two, one)
 
 
+def exchange_and_gather(to_low, to_high):
+    nx, nz = lax.axis_size("gx"), lax.axis_size("gz")
+    if nx != 2 or nz % 2:
+        return gather_first(jnp.stack(exchange(to_low, to_high, "gz")), "gx", 1)
+    odd = lax.axis_index("gz") % 2 == 1
+    out = []
+    for payload, step in (
+        (jnp.where(odd, to_low, to_high), [i ^ 1 for i in range(nz)]),
+        (jnp.where(odd, to_high, to_low), [(i + 1 if i % 2 else i - 1) % nz for i in range(nz)]),
+    ):
+        same = lax.ppermute(payload, "gz", list(enumerate(step)))
+        pairs = [(x * nz + i, (1 - x) * nz + t) for x in (0, 1) for i, t in enumerate(step)]
+        cross = lax.ppermute(payload, ("gx", "gz"), pairs)
+        first = lax.axis_index("gx") == 0
+        out.append(jnp.concatenate([jnp.where(first, same, cross), jnp.where(first, cross, same)], axis=0))
+    one, two = out
+    return jnp.stack([jnp.where(odd, one, two), jnp.where(odd, two, one)])
+
+
 def gather_first(values, axis, dim):
     count = lax.axis_size(axis)
     if count == 1:
@@ -421,48 +487,37 @@
 
 
 def gather_second(block, low_edge, high_edge, me, count):
-    size = block.size // LANES
-    shape = block.shape
-    low_edge = low_edge.reshape(-1, LANES)
-    high_edge = high_edge.reshape(-1, LANES)
-    block_rows = block.reshape(size, LANES)
+    size = block.shape[0]
     blocks, sources = [block], [me]
     low = high = low_edge
     if count == 4:
         odd = me % 2 == 1
         got = []
         for step in (1, 2, 3):
-            payload = block_rows
+            payload = block
             if step != 2:
                 edge = jnp.where(odd == (step == 1), low_edge, high_edge)
-                payload = jnp.concatenate([block_rows, edge], axis=0)
+                payload = jnp.concatenate([block, edge], axis=0)
             got.append(lax.ppermute(payload, "gy", [(i, i ^ step) for i in range(count)]))
-            blocks.append(got[-1][:size].reshape(shape))
+            blocks.append(got[-1][:size])
             sources.append(me ^ step)
         low = jnp.where(odd, got[0][size:], got[2][size:])
         high = jnp.where(odd, got[2][size:], got[0][size:])
     else:
         for step in range(1, count):
-            parts = [block_rows]
+            parts = [block]
             if step == 1:
                 parts.append(high_edge)
             if step == count - 1:
                 parts.append(low_edge)
             got = ring(jnp.concatenate(parts, axis=0), "gy", step)
-            blocks.append(got[:size].reshape(shape))
+            blocks.append(got[:size])
             sources.append((me - step) % count)
             if step == 1:
                 low = got[size : size + high_edge.shape[0]]
             if step == count - 1:
                 high = got[got.shape[0] - low_edge.shape[0] :]
     return blocks, sources, low, high
-
-
-def halo_tile(from_low, from_high, has_low, has_high):
-    lane = lax.broadcasted_iota(jnp.int32, from_low.shape, from_low.ndim - 1)
-    low = jnp.where(has_low, from_low, 0.0)
-    high = jnp.where(has_high, from_high, 0.0)
-    return jnp.where(lane < LANES // 2, high, low)
 
 
 def vmem(shape):
@@ -495,24 +550,31 @@
     tiles = bz // LANES
     nx, ny, nz = (lax.axis_size(a) for a in ("gx", "gy", "gz"))
     ix, iy, iz = (lax.axis_index(a) for a in ("gx", "gy", "gz"))
-    flags = jnp.stack([iz > 0, iz < nz - 1, iy > 0, iy < ny - 1]).astype(jnp.int32)
-    has_left, has_right = iz > 0, iz < nz - 1
+    yes = ix >= 0
+    flags = jnp.stack([iz > 0, iz < nz - 1, iy > 0, iy < ny - 1, yes]).astype(jnp.int32)
     x_count = bx * nx
 
     def shape(*dims):
         return jax.ShapeDtypeStruct(dims, F32)
 
-    both = jnp.stack([conductivity, source]).reshape(2, bx, by, tiles, LANES)
-    both = gather_first(both.transpose(0, 2, 3, 1, 4), "gx", 3)
-    left, right = exchange(both[:, :, 0], both[:, :, tiles - 1], "gz")
-    halo = halo_tile(left, right, has_left, has_right)
-    own = jnp.concatenate([both, halo[:, :, None]], axis=2)
-    ylo, yhi = exchange(
-        jnp.concatenate([own[0, :HALO], own[1, : HALO - 1]], axis=0),
-        jnp.concatenate([own[0, by - HALO :], own[1, by - HALO + 1 :]], axis=0),
-        "gy",
-        "gx",
+    def lines(*arrays):
+        return jnp.concatenate([a.reshape(-1, LANES) for a in arrays], axis=0)
+
+    mine = jnp.stack([conductivity, source]).reshape(2, bx, by, tiles, LANES).transpose(0, 2, 3, 1, 4)
+    first_edge = jnp.concatenate([mine[a, y, 0, :, :EDGE] for a in (0, 1) for y in range(by)], axis=-1)
+    last_edge = jnp.concatenate(
+        [mine[a, y, tiles - 1, :, LANES - EDGE :] for a in (0, 1) for y in range(by)], axis=-1
     )
+    own = gather_first(mine, "gx", 3)
+    zown = exchange_and_gather(first_edge, last_edge)
+    edge = HALO - 1
+    low_rows = lines(own[0, :HALO], own[1, :edge], zown)
+    high_rows = lines(own[0, by - HALO :], own[1, by - edge :], zown)
+    from_low, from_high = exchange(low_rows, high_rows, "gy", "gx")
+    cut = (HALO + edge) * tiles * x_count
+    rows_shape = (HALO + edge, tiles, x_count, LANES)
+    ylo, zlo = from_low[:cut].reshape(rows_shape), from_low[cut:].reshape(zown.shape)
+    yhi, zhi = from_high[:cut].reshape(rows_shape), from_high[cut:].reshape(zown.shape)
 
     ext = by + 2 * HALO
     padded = x_count + 2 * PAD
@@ -520,7 +582,7 @@
     plain = (ext, tiles + 1, x_count, LANES)
     each = by // 2
     xc = x_count // 2
-    kap, diag, inv, xpre, rpre, coarse = call(
+    kap, diag, inv, xpre, rpre, coarse, to_left, to_right = call(
         before_kernel,
         [
             shape(*wide),
@@ -529,25 +591,26 @@
             shape(by, tiles, x_count, LANES),
             shape(by, tiles, x_count, LANES),
             shape(2 * each * xc, LANES),
+            shape(2 * xc + x_count, LANES),
+            shape(2 * xc + x_count, LANES),
         ],
         [vmem(wide)] * 4 + [vmem(plain)] * 2 + [vmem((2 * each * x_count, LANES))],
-        [flags, own, ylo, yhi],
+        [flags, own, zown, ylo, zlo, yhi, zhi],
     )
 
-    small = coarse.reshape(2 * each * xc, LANES)
-
-    def with_tile(t):
-        return jnp.concatenate([small, rpre[:, t].reshape(by * x_count, LANES)], axis=0)
-
-    left, right = exchange(with_tile(0), with_tile(tiles - 1), "gz")
-    halo = halo_tile(left, right, has_left, has_right)
+    left, right = exchange(to_left, to_right, "gz")
+    coarse_z = jnp.stack([left[: 2 * xc], right[: 2 * xc]])
+    fine_z = jnp.stack([left[2 * xc :], right[2 * xc :]])
+    blocks, sources, low, high = gather_second(
+        lines(coarse, coarse_z), lines(rpre[:edge], fine_z), lines(rpre[by - edge :], fine_z), iy, ny
+    )
     cut = 2 * each * xc
-    coarse_halo = halo[:cut].reshape(2, each, 1, xc, LANES)
-    coarse_own = jnp.concatenate([coarse.reshape(2, each, 1, xc, LANES), coarse_halo], axis=2)
-    rown = jnp.concatenate([rpre, halo[cut:].reshape(by, 1, x_count, LANES)], axis=1)
-    flat_coarse = coarse_own.reshape(-1, LANES)
-    edge = HALO - 1
-    blocks, sources, rlo, rhi = gather_second(coarse_own, rown[:edge], rown[by - edge :], iy, ny)
+    zblocks = [b[cut:].reshape(2, 2, xc, LANES) for b in blocks]
+    blocks = [b[:cut].reshape(2, each, xc, LANES) for b in blocks]
+    cut = edge * tiles * x_count
+    rows_shape = (edge, tiles, x_count, LANES)
+    rlo, zrlo = low[:cut].reshape(rows_shape), low[cut:].reshape(fine_z.shape)
+    rhi, zrhi = high[:cut].reshape(rows_shape), high[cut:].reshape(fine_z.shape)
 
     yc = each * ny
     tiles1 = tiles // 2 + 1
@@ -559,7 +622,7 @@
     plain2 = (y2 + 2, 1, x2, LANES)
     flat_rows = max(y2 * xc, tiles1 * (ext // 2 + 1) * x_count)
 
-    places = jnp.stack([ix, iy] + sources).astype(jnp.int32)
+    places = jnp.stack([jnp.int32(p) for p in (ix, iy, iz > 0, iz < nz - 1, *sources)])
 
     def kernel(*refs):
         after_kernel(*refs, count=len(blocks))
@@ -570,9 +633,8 @@
         [vmem(wide1)] + [vmem(plain1)] * 4 + [vmem(wide1)] * 4
         + [vmem(wide2)] + [vmem(plain2)] * 4 + [vmem(wide2)] * 4
         + [vmem((flat_rows, LANES))] + [vmem(wide)] * 4 + [vmem(plain)] * 2,
-        [places] + blocks
-        + [kap, diag, inv, xpre, rown]
-        + [e.reshape(edge, tiles + 1, x_count, LANES) for e in (rlo, rhi)],
+        [places] + blocks + zblocks
+        + [kap, diag, inv, xpre, rpre, fine_z, rlo, zrlo, rhi, zrhi],
     )
     return sol, resid
 

time: 53.5 us -> 46.3 us (0.87)
  waiting for transfers between devices: 26.3 us -> 17.5 us
  Pallas kernels: 10.5 us -> 11.2 us
    ppermute x0 -> x4, starting transfers between devices: none -> 6.35 us  [the longest x2 3.63 us: exchange_and_gather(): cross = lax.ppermute(payload, ('gx', 'gz'), pairs)]
    ppermute x3 -> x2, waiting for transfers between devices: 10.7 us -> 4.6 us  [exchange(): two = lax.ppermute(jnp.where(odd, to_high, to_low), names, pairs)]
    ppermute x3 -> x2, starting transfers between devices: 5.17 us -> 2.13 us  [exchange(): two = lax.ppermute(jnp.where(odd, to_high, to_low), names, pairs)]
    ppermute x1, starting transfers between devices: 3.03 us -> 0.01 us  [gather_first(): other = lax.ppermute(values, axis, [(0, 1), (1, 0)])]
    ppermute x1, waiting for transfers between devices: 3.5 us -> 0.94 us  [gather_first(): other = lax.ppermute(values, axis, [(0, 1), (1, 0)])]
    ppermute x0 -> x4, waiting for transfers between devices: none -> 2.31 us  [the longest x2 2.3 us: exchange_and_gather(): cross = lax.ppermute(payload, ('gx', 'gz'), pairs)]
    ppermute x3, waiting for transfers between devices: 10.7 us -> 8.57 us  [gather_second(): lax.ppermute(payload, 'gy', [(i, i ^ step) for i in range(count)])]
    ppermute x3 -> x2, starting transfers between devices: 1.8 us -> 2.64 us  [exchange(): lax.ppermute(jnp.where(odd, to_low, to_high), axis, [(i, i ^ 1) for i in...]
  transfers between devices with their start and end apart: 10 -> 12, of which waited for: 8 -> 7; matrix products, arithmetic and copies ran while one was open for 0% -> 1% of each run, Pallas kernels for 0% -> 0%
where the time goes in v3:
time: 46.3 us; the launch traced here: 46.2 us
  waiting for transfers between devices  17.5 us (38%)
  starting transfers between devices  14.7 us (32%)
  Pallas kernels  11.2 us (24%)
  local copies, waits for them, and re-layouts  1.53 us (3%)
  between operations  0.92 us (2%)
    pallas_call x2, Pallas kernels, call(): pl.pallas_call(kernel, out_shape=out_shapes, in_specs=[pl.BlockSpec(memor...  11.2 us
    ppermute x3, waiting for transfers between devices, gather_second(): lax.ppermute(payload, 'gy', [(i, i ^ step) for i in range(count)])  8.57 us
    ppermute x2, waiting for transfers between devices, exchange(): two = lax.ppermute(jnp.where(odd, to_high, to_low), names, pairs)  4.6 us
    ppermute x2, starting transfers between devices, exchange_and_gather(): cross = lax.ppermute(payload, ('gx', 'gz'), pairs)  3.63 us
    ppermute x3, starting transfers between devices, gather_second(): lax.ppermute(payload, 'gy', [(i, i ^ step) for i in range(count)])  3.55 us
    ppermute x2, starting transfers between devices, exchange_and_gather(): same = lax.ppermute(payload, 'gz', list(enumerate(step)))  2.72 us
    ppermute x2, starting transfers between devices, exchange(): lax.ppermute(jnp.where(odd, to_low, to_high), axis, [(i, i ^ 1) for i in...  2.64 us
    ppermute x2, waiting for transfers between devices, exchange_and_gather(): cross = lax.ppermute(payload, ('gx', 'gz'), pairs)  2.3 us
  transfers between devices with their start and end apart: 12, of which 7 were waited for; matrix products, arithmetic and copies ran while one was open for 1% of the time, Pallas kernels for 0%

profile of v3, /device:TPU:0, one launch (start us, length us, event | category | flops | bytes accessed | tf_op | source)
XLA Modules:
  0.0 46.2 jit_solution(3664262007347511750)
XLA Ops:
  0.6 0.9 %copy.5 = f32[1,8,8,2,128]{4,1,3,2,0:T(8,128)S(1)} copy(f32[1,8,8,2,128]{4,2,3,1,0:T(8,128)} %bitcast.151) | data formatting | bytes 131072 | tf_op jit(solution)/shard_map/stack | solution.py:563
  1.6 0.1 slice_bitcast_fusion.27
  1.8 0.1 concatenate.77
  1.9 0.1 concatenate.78
  2.0 2.5 %collective-permute-start.3 = (f32[8,128]{1,0:T(8,128)S(1)}, f32[8,128]{1,0:T(8,128)S(1)}, u32[]{:S(2)}, u32[]{:S(2)}) collective-permute-start(f32[8,128]{1,0:T(8,128)S(1)} %get-tuple-element.83), channel_id=1, source_target_pairs={{0,3},{1,2},{2,1},{3,0},{4,7},{5,6},{6,5},{7,4},{8,11},{9,10},{10,... | collective-permute-start | bytes 12296 | tf_op jit(solution)/shard_map/ppermute | solution.py:466
  4.5 1.7 %collective-permute-start.4 = (f32[8,128]{1,0:T(8,128)S(1)}, f32[8,128]{1,0:T(8,128)S(1)}, u32[]{:S(2)}, u32[]{:S(2)}) collective-permute-start(f32[8,128]{1,0:T(8,128)S(1)} %get-tuple-element.83), channel_id=1, source_target_pairs={{0,19},{1,18},{2,17},{3,16},{16,3},{17,2},{18,1},{19,0},{4,23},{5,... | collective-permute-start | bytes 12296 | tf_op jit(solution)/shard_map/ppermute | solution.py:468
  6.2 0.2 collective-permute-start.1
  6.4 1.9 %collective-permute-start.2 = (f32[8,128]{1,0:T(8,128)S(1)}, f32[8,128]{1,0:T(8,128)S(1)}, u32[]{:S(2)}, u32[]{:S(2)}) collective-permute-start(f32[8,128]{1,0:T(8,128)S(1)} %get-tuple-element.82), channel_id=1, source_target_pairs={{0,17},{1,16},{2,19},{3,18},{16,1},{17,0},{18,3},{19,2},{4,21},{5,... | collective-permute-start | bytes 12296 | tf_op jit(solution)/shard_map/ppermute | solution.py:468
  8.4 2.2 %collective-permute-done.2 = f32[8,128]{1,0:T(8,128)S(1)} collective-permute-done((f32[8,128]{1,0:T(8,128)S(1)}, f32[8,128]{1,0:T(8,128)S(1)}, u32[]{:S(2)}, u32[]{:S(2)}) %collective-permute-start.2) | collective-permute-done | bytes 4128 | tf_op jit(solution)/shard_map/ppermute | solution.py:468
  10.6 0.9 %collective-permute-done = f32[2,8,2,8,128]{4,3,2,1,0:T(8,128)S(1)} collective-permute-done((f32[2,8,2,8,128]{4,3,2,1,0:T(8,128)S(1)}, f32[2,8,2,8,128]{4,3,2,1,0:T(8,128)S(1)}, u32[]{:S(2)}, u32[]{:S(2)}) %collective-permute-start) | collective-permute-done | bytes 131104 | tf_op jit(solution)/shard_map/ppermute | solution.py:480
  11.7 0.6 %collective-permute-start.6 = (f32[320,128]{1,0:T(8,128)S(1)}, f32[320,128]{1,0:T(8,128)S(1)}, u32[]{:S(2)}, u32[]{:S(2)}) collective-permute-start(f32[320,128]{1,0:T(8,128)S(1)} %get-tuple-element.20), channel_id=1, source_target_pairs={{0,16},{4,8},{8,4},{12,28},{16,0},{20,24},{24,20},{28,12},{1,17},{... | collective-permute-start | bytes 491528 | tf_op jit(solution)/shard_map/ppermute | solution.py:452
  12.3 2.6 %collective-permute-start.5 = (f32[320,128]{1,0:T(8,128)S(1)}, f32[320,128]{1,0:T(8,128)S(1)}, u32[]{:S(2)}, u32[]{:S(2)}) collective-permute-start(f32[320,128]{1,0:T(8,128)S(1)} %get-tuple-element.21), channel_id=1, source_target_pairs={{0,4},{4,0},{8,12},{12,8},{1,5},{5,1},{9,13},{13,9},{2,6},{6,2},{1... | collective-permute-start | bytes 491528 | tf_op jit(solution)/shard_map/ppermute | solution.py:443
  14.9 0.1 stack.96
  15.0 0.1 stack.92.refs_0_
  15.1 2.9 %collective-permute-done.6 = f32[320,128]{1,0:T(8,128)S(1)} collective-permute-done((f32[320,128]{1,0:T(8,128)S(1)}, f32[320,128]{1,0:T(8,128)S(1)}, u32[]{:S(2)}, u32[]{:S(2)}) %collective-permute-start.6) | collective-permute-done | bytes 163872 | tf_op jit(solution)/shard_map/ppermute | solution.py:452
  18.0 1.1 %collective-permute-done.5 = f32[320,128]{1,0:T(8,128)S(1)} collective-permute-done((f32[320,128]{1,0:T(8,128)S(1)}, f32[320,128]{1,0:T(8,128)S(1)}, u32[]{:S(2)}, u32[]{:S(2)}) %collective-permute-start.5) | collective-permute-done | bytes 163872 | tf_op jit(solution)/shard_map/ppermute | solution.py:443
  19.2 3.7 %shard_map.41 = (f32[18,3,32,128]{3,2,1,0:T(8,128)S(1)}, f32[18,3,16,128]{3,2,1,0:T(8,128)S(1)}, f32[18,3,16,128]{3,2,1,0:T(8,128)S(1)}, f32[8,2,16,128]{3,2,1,0...) custom-call(s32[5]{0:T(128)S(1)} %convert_element_type.2.flags, ...), custom_call_target="tpu_custom_call" | custom-call | tf_op jit(solution)/shard_map/pallas_call | solution.py:538
  23.0 1.5 %collective-permute-start.8 = (f32[32,128]{1,0:T(8,128)S(1)}, f32[32,128]{1,0:T(8,128)S(1)}, u32[]{:S(2)}, u32[]{:S(2)}) collective-permute-start(f32[32,128]{1,0:T(8,128)S(1)} %get-tuple-element.71), channel_id=1, source_target_pairs={{0,3},{1,2},{2,1},{3,0},{4,7},{5,6},{6,5},{7,4},{8,11},{9,10},{10,... | collective-permute-start | bytes 49160 | tf_op jit(solution)/shard_map/ppermute | solution.py:452
  24.5 1.7 %collective-permute-done.8 = f32[32,128]{1,0:T(8,128)S(1)} collective-permute-done((f32[32,128]{1,0:T(8,128)S(1)}, f32[32,128]{1,0:T(8,128)S(1)}, u32[]{:S(2)}, u32[]{:S(2)}) %collective-permute-start.8) | collective-permute-done | bytes 16416 | tf_op jit(solution)/shard_map/ppermute | solution.py:452
  26.3 1.8 %collective-permute-start.9 = (f32[256,128]{1,0:T(8,128)S(1)}, f32[256,128]{1,0:T(8,128)S(1)}, u32[]{:S(2)}, u32[]{:S(2)}) collective-permute-start(f32[256,128]{1,0:T(8,128)S(1)} %get-tuple-element.67), channel_id=1, source_target_pairs={{0,4},{4,0},{8,12},{12,8},{1,5},{5,1},{9,13},{13,9},{2,6},{6,2},{1... | collective-permute-start | bytes 393224 | tf_op jit(solution)/shard_map/ppermute | solution.py:501
  28.1 1.3 %collective-permute-start.11 = (f32[256,128]{1,0:T(8,128)S(1)}, f32[256,128]{1,0:T(8,128)S(1)}, u32[]{:S(2)}, u32[]{:S(2)}) collective-permute-start(f32[256,128]{1,0:T(8,128)S(1)} %get-tuple-element.66), channel_id=1, source_target_pairs={{0,12},{4,8},{8,4},{12,0},{1,13},{5,9},{9,5},{13,1},{2,14},{6,10},... | collective-permute-start | bytes 393224 | tf_op jit(solution)/shard_map/ppermute | solution.py:501
  29.5 0.4 collective-permute-start.10
  29.9 8.6 %collective-permute-done.10 = f32[96,128]{1,0:T(8,128)S(1)} collective-permute-done((f32[96,128]{1,0:T(8,128)S(1)}, f32[96,128]{1,0:T(8,128)S(1)}, u32[]{:S(2)}, u32[]{:S(2)}) %collective-permute-start.10) | collective-permute-done | bytes 49184 | tf_op jit(solution)/shard_map/ppermute | solution.py:501
  38.6 7.6 %shard_map.42 = (f32[8,8,256]{2,1,0:T(8,128)}, f32[8,8,256]{2,1,0:T(8,128)}) custom-call(s32[8]{0:T(128)S(1)} %stack.92.refs_0_, f32[2,4,8,128]{3,2,1,0:T(8,128)S(1)} %bitcast.128, f32[2,4,8,128]{3,2,1,0:T(8,128)S(1)} %bitcast.134, f32[2,4,8,128]{3,2,1,0:T(8,128)S(1)} %bitcast.133, f32[2,4,8,128]{3,2,1,0:T(8,128)S(1)} %bitcast.135, ...), custom_call_target="tpu_custom_call" | custom-call | tf_op jit(solution)/shard_map/pallas_call | solution.py:538
  (50 shorter events, 0.6 us)
Async XLA Ops:
  0.6 0.9 %copy-start = (f32[8,8,256]{2,1,0:T(8,128)S(1)}, f32[8,8,256]{2,1,0:T(8,128)}, u32[]{:S(2)}) copy-start(f32[8,8,256]{2,1,0:T(8,128)} %param.2) | copy-start | bytes 196612
  2.0 6.4 %collective-permute-start.3 = (f32[8,128]{1,0:T(8,128)S(1)}, f32[8,128]{1,0:T(8,128)S(1)}, u32[]{:S(2)}, u32[]{:S(2)}) collective-permute-start(f32[8,128]{1,0:T(8,128)S(1)} %get-tuple-element.83), channel_id=1, source_target_pairs={{0,3},{1,2},{2,1},{3,0},{4,7},{5,6},{6,5},{7,4},{8,11},{9,10},{10,... | collective-permute-start | bytes 12296 | tf_op jit(solution)/shard_map/ppermute | solution.py:466
  4.5 3.9 %collective-permute-start.4 = (f32[8,128]{1,0:T(8,128)S(1)}, f32[8,128]{1,0:T(8,128)S(1)}, u32[]{:S(2)}, u32[]{:S(2)}) collective-permute-start(f32[8,128]{1,0:T(8,128)S(1)} %get-tuple-element.83), channel_id=1, source_target_pairs={{0,19},{1,18},{2,17},{3,16},{16,3},{17,2},{18,1},{19,0},{4,23},{5,... | collective-permute-start | bytes 12296 | tf_op jit(solution)/shard_map/ppermute | solution.py:468
  6.2 5.4 %collective-permute-start = (f32[2,8,2,8,128]{4,3,2,1,0:T(8,128)S(1)}, f32[2,8,2,8,128]{4,3,2,1,0:T(8,128)S(1)}, u32[]{:S(2)}, u32[]{:S(2)}) collective-permute-start(f32[2,8,2,8,128]{4,3,2,1,0:T(8,128)S(1)} %maximum_bitcast_fusion), channel_id=1, source_target_pairs={{0,16},{16,0},{1,17},{17,1},{2,18},{18,2},{3,19},{19,3},{4,20},{20... | collective-permute-start | bytes 393224 | tf_op jit(solution)/shard_map/ppermute | solution.py:480
  6.2 2.2 %collective-permute-start.1 = (f32[8,128]{1,0:T(8,128)S(1)}, f32[8,128]{1,0:T(8,128)S(1)}, u32[]{:S(2)}, u32[]{:S(2)}) collective-permute-start(f32[8,128]{1,0:T(8,128)S(1)} %get-tuple-element.82), channel_id=1, source_target_pairs={{0,1},{1,0},{2,3},{3,2},{4,5},{5,4},{6,7},{7,6},{8,9},{9,8},{10,11... | collective-permute-start | bytes 12296 | tf_op jit(solution)/shard_map/ppermute | solution.py:466
  6.4 4.2 %collective-permute-start.2 = (f32[8,128]{1,0:T(8,128)S(1)}, f32[8,128]{1,0:T(8,128)S(1)}, u32[]{:S(2)}, u32[]{:S(2)}) collective-permute-start(f32[8,128]{1,0:T(8,128)S(1)} %get-tuple-element.82), channel_id=1, source_target_pairs={{0,17},{1,16},{2,19},{3,18},{16,1},{17,0},{18,3},{19,2},{4,21},{5,... | collective-permute-start | bytes 12296 | tf_op jit(solution)/shard_map/ppermute | solution.py:468
  11.7 6.3 %collective-permute-start.6 = (f32[320,128]{1,0:T(8,128)S(1)}, f32[320,128]{1,0:T(8,128)S(1)}, u32[]{:S(2)}, u32[]{:S(2)}) collective-permute-start(f32[320,128]{1,0:T(8,128)S(1)} %get-tuple-element.20), channel_id=1, source_target_pairs={{0,16},{4,8},{8,4},{12,28},{16,0},{20,24},{24,20},{28,12},{1,17},{... | collective-permute-start | bytes 491528 | tf_op jit(solution)/shard_map/ppermute | solution.py:452
  12.3 6.8 %collective-permute-start.5 = (f32[320,128]{1,0:T(8,128)S(1)}, f32[320,128]{1,0:T(8,128)S(1)}, u32[]{:S(2)}, u32[]{:S(2)}) collective-permute-start(f32[320,128]{1,0:T(8,128)S(1)} %get-tuple-element.21), channel_id=1, source_target_pairs={{0,4},{4,0},{8,12},{12,8},{1,5},{5,1},{9,13},{13,9},{2,6},{6,2},{1... | collective-permute-start | bytes 491528 | tf_op jit(solution)/shard_map/ppermute | solution.py:443
  22.9 1.6 %collective-permute-start.7 = (f32[32,128]{1,0:T(8,128)S(1)}, f32[32,128]{1,0:T(8,128)S(1)}, u32[]{:S(2)}, u32[]{:S(2)}) collective-permute-start(f32[32,128]{1,0:T(8,128)S(1)} %get-tuple-element.70), channel_id=1, source_target_pairs={{0,1},{1,0},{2,3},{3,2},{4,5},{5,4},{6,7},{7,6},{8,9},{9,8},{10,11... | collective-permute-start | bytes 49160 | tf_op jit(solution)/shard_map/ppermute | solution.py:443
  23.0 3.2 %collective-permute-start.8 = (f32[32,128]{1,0:T(8,128)S(1)}, f32[32,128]{1,0:T(8,128)S(1)}, u32[]{:S(2)}, u32[]{:S(2)}) collective-permute-start(f32[32,128]{1,0:T(8,128)S(1)} %get-tuple-element.71), channel_id=1, source_target_pairs={{0,3},{1,2},{2,1},{3,0},{4,7},{5,6},{6,5},{7,4},{8,11},{9,10},{10,... | collective-permute-start | bytes 49160 | tf_op jit(solution)/shard_map/ppermute | solution.py:452
  26.3 12.1 %collective-permute-start.9 = (f32[256,128]{1,0:T(8,128)S(1)}, f32[256,128]{1,0:T(8,128)S(1)}, u32[]{:S(2)}, u32[]{:S(2)}) collective-permute-start(f32[256,128]{1,0:T(8,128)S(1)} %get-tuple-element.67), channel_id=1, source_target_pairs={{0,4},{4,0},{8,12},{12,8},{1,5},{5,1},{9,13},{13,9},{2,6},{6,2},{1... | collective-permute-start | bytes 393224 | tf_op jit(solution)/shard_map/ppermute | solution.py:501
  28.1 10.3 %collective-permute-start.11 = (f32[256,128]{1,0:T(8,128)S(1)}, f32[256,128]{1,0:T(8,128)S(1)}, u32[]{:S(2)}, u32[]{:S(2)}) collective-permute-start(f32[256,128]{1,0:T(8,128)S(1)} %get-tuple-element.66), channel_id=1, source_target_pairs={{0,12},{4,8},{8,4},{12,0},{1,13},{5,9},{9,5},{13,1},{2,14},{6,10},... | collective-permute-start | bytes 393224 | tf_op jit(solution)/shard_map/ppermute | solution.py:501
  29.5 9.0 %collective-permute-start.10 = (f32[96,128]{1,0:T(8,128)S(1)}, f32[96,128]{1,0:T(8,128)S(1)}, u32[]{:S(2)}, u32[]{:S(2)}) collective-permute-start(f32[96,128]{1,0:T(8,128)S(1)} %pad_maximum_fusion.7), channel_id=1, source_target_pairs={{0,8},{4,12},{8,0},{12,4},{1,9},{5,13},{9,1},{13,5},{2,10},{6,14},... | collective-permute-start | bytes 147464 | tf_op jit(solution)/shard_map/ppermute | solution.py:501

commit v4 on v3

--- a/solution.py
+++ b/solution.py
@@ -4,6 +4,7 @@
 from jax.experimental import pallas as pl
 from jax.experimental.pallas import tpu as pltpu
 from jax.sharding import PartitionSpec as P
+
 
 DEGREE = 4
 COARSE_DEGREE = 8
@@ -28,7 +29,7 @@
     ratio_term = centre / half_width
     rho_prev = 1.0 / ratio_term
     weights = []
-    for number in range(1, degree):
+    for _ in range(1, degree):
         rho_next = 1.0 / (2.0 * ratio_term - rho_prev)
         weights.append((rho_next * rho_prev, 2.0 * rho_next / half_width))
         rho_prev = rho_next
@@ -165,15 +166,14 @@
             - diag[y, :, x : x + 8, :] * centre
             + (k * total[i][0] + weighted[i][0])
         )
-        res[y, :, x : x + 8, :] = value
         yield y, k, centre, value
 
 
 def residual_only(kap, diag, res, v, w, lo, hi):
     def body(first, rows):
         for x in tiles_of(diag):
-            for _ in new_residuals(kap, diag, res, v, w, first, rows, x):
-                pass
+            for y, _, _, value in new_residuals(kap, diag, res, v, w, first, rows, x):
+                res[y, :, x : x + 8, :] = value
 
     chunks(lo, hi, body)
 
@@ -182,6 +182,7 @@
     def body(first, rows):
         for x in tiles_of(diag):
             for y, k, centre, value in new_residuals(kap, diag, res, old[0], old[1], first, rows, x):
+                res[y, :, x : x + 8, :] = value
                 step = pair[0] * centre + (pair[1] * inv[y, :, x : x + 8, :]) * value
                 new[0][y, :, PAD + x : PAD + x + 8, :] = step
                 new[1][y, :, PAD + x : PAD + x + 8, :] = k * step
@@ -190,47 +191,46 @@
     chunks(lo, hi, body)
 
 
-def halving(rows):
-    row = lax.broadcasted_iota(jnp.int32, (rows, rows // 2), 0)
-    col = lax.broadcasted_iota(jnp.int32, (rows, rows // 2), 1)
-    return jnp.where(row // 2 == col, 0.125, 0.0).astype(F32)
-
-
-def doubling(cols):
-    row = lax.broadcasted_iota(jnp.int32, (cols // 2, cols), 0)
-    col = lax.broadcasted_iota(jnp.int32, (cols // 2, cols), 1)
-    return jnp.where(col // 2 == row, 1.0, 0.0).astype(F32)
-
-
-def halo_doubling():
-    row = lax.broadcasted_iota(jnp.int32, (LANES, LANES), 0)
-    col = lax.broadcasted_iota(jnp.int32, (LANES, LANES), 1)
-    source = col // 2 + jnp.where(col < LANES // 2, 0, LANES // 2)
-    return jnp.where(source == row, 1.0, 0.0).astype(F32)
-
-
-def product(left, right):
-    return jnp.dot(left, right, precision=lax.Precision.HIGHEST, preferred_element_type=F32)
-
-
-def along_lanes(values):
-    return jnp.concatenate([values[t] for t in range(values.shape[0])], axis=-1)
-
-
-def pack(pieces, width, from_end):
+def lanes_of(values):
+    return lax.broadcasted_iota(jnp.int32, values.shape, 1)
+
+
+def take(values, index):
+    return jnp.take_along_axis(values, index, axis=1, mode="promise_in_bounds")
+
+
+def halve(first, second):
+    lane = lanes_of(first)
+    even = (2 * lane) % LANES
+    low = take(first + pltpu.roll(first, LANES - 1, 1), even)
+    high = take(second + pltpu.roll(second, LANES - 1, 1), even)
+    return jnp.where(lane < LANES // 2, low, high) * 0.125
+
+
+def double(values):
+    half = lanes_of(values) // 2
+    return take(values, half), take(values, half + LANES // 2)
+
+
+def double_halo(values):
+    lane = lanes_of(values)
+    return take(values, lane // 2 + jnp.where(lane < LANES // 2, 0, LANES // 2))
+
+
+def pack(pieces, width, from_end, start=0):
     lane = lax.broadcasted_iota(jnp.int32, pieces[0].shape, 1)
     out = jnp.zeros(pieces[0].shape, F32)
-    for i, piece in enumerate(pieces):
+    for i, piece in enumerate(pieces, start):
         shift = (width * i + (width if from_end else 0)) % LANES
         moved = pltpu.roll(piece, shift, 1) if shift else piece
         out = jnp.where((lane >= width * i) & (lane < width * (i + 1)), moved, out)
     return out
 
 
-def unpack(left, right, i, width):
+def unpack(left, right, i, width, start=0):
     lane = lax.broadcasted_iota(jnp.int32, left.shape, 1)
     back = (LANES - width * i) % LANES
-    end = (LANES - width - width * i) % LANES
+    end = (LANES - width - width * (i + start)) % LANES
     first = pltpu.roll(right, back, 1) if back else right
     last = pltpu.roll(left, end, 1) if end else left
     return jnp.where(lane < width, first, jnp.where(lane >= LANES - width, last, 0.0))
@@ -270,7 +270,7 @@
         old, new = new, old
         lo, hi = lo + 1, hi - 1
     residual_only(kap, diag, res, old[0], old[1], HALO, last)
-    pieces = []
+    at = 0
     for y in range(rows):
         xout[y] = acc[HALO + y, 0:tiles]
         rout[y] = res[HALO + y, 0:tiles]
@@ -280,8 +280,8 @@
                 source[HALO + y, 0:tiles, offset : offset + x_count, :]
                 + source[HALO + y + 1, 0:tiles, offset : offset + x_count, :]
             )
-            pieces.append(along_lanes(both))
-    flat[...] = product(jnp.concatenate(pieces, axis=0), halving(tiles * LANES))
+            flat[at : at + x_count, :] = halve(both[0], both[1])
+            at += x_count
     total = flat.shape[0]
     coarse[...] = flat[pl.ds(0, total // 2, stride=2), :] + flat[pl.ds(1, total // 2, stride=2), :]
     each, xc = rows // 2, x_count // 2
@@ -290,7 +290,7 @@
             value = [coarse[(i * each + y) * xc : (i * each + y + 1) * xc, :] for y in range(each)]
             out[i * xc : (i + 1) * xc, :] = pack(value, COARSE_EDGE, from_end)
         value = [res[HALO + y, tiles - 1 if from_end else 0] for y in range(rows)]
-        out[2 * xc : 2 * xc + x_count, :] = pack(value, EDGE, from_end)
+        out[2 * xc : 2 * xc + x_count, :] = pack(value, EDGE, from_end, rows if from_end else 0)
 
 
 def after_kernel(places, *refs, count):
@@ -330,12 +330,10 @@
     y2 = yc // 2
     half = xc // 2
     for target, source, offset, factor in ((k2, k1, PAD, 0.25), (r2, r1, 0, 1.0)):
-        pieces = []
         for y in range(y2):
             a = lo1 + 2 * y
             both = source[a, :, offset : offset + xc, :] + source[a + 1, :, offset : offset + xc, :]
-            pieces.append(along_lanes(both))
-        flat[0 : y2 * xc, :] = product(jnp.concatenate(pieces, axis=0), halving(tiles1 * LANES))[:, 0:LANES]
+            flat[y * xc : (y + 1) * xc, :] = halve(both[0], both[1])
         if target is k2:
             zero_rows(k2, range(y2 + 2))
         for y in range(y2):
@@ -358,10 +356,8 @@
         value = x2[1 + y, 0, 0:half, :]
         flat[pl.ds(y * xc, half, stride=2), :] = value
         flat[pl.ds(y * xc + 1, half, stride=2), :] = value
-    wide = product(flat[0 : y2 * xc, :], doubling(2 * LANES))
     for y in range(y2):
-        for t in range(tiles1):
-            value = wide[y * xc : (y + 1) * xc, t * LANES : (t + 1) * LANES]
+        for t, value in enumerate(double(flat[y * xc : (y + 1) * xc, :])):
             for s in (0, 1):
                 at = lo1 + 2 * y + s
                 va1[at, t, PAD : PAD + xc, :] = value
@@ -385,21 +381,21 @@
             base = (t * wide_rows + y) * x_count
             flat[pl.ds(base, xc, stride=2), :] = value
             flat[pl.ds(base + 1, xc, stride=2), :] = value
-    n = wide_rows * x_count
-    parts = []
-    for t in range(tiles1 - 1):
-        both = product(flat[t * n : (t + 1) * n, :], doubling(2 * LANES))
-        parts += [both[:, 0:LANES], both[:, LANES:]]
-    parts.append(product(flat[(tiles1 - 1) * n : tiles1 * n, :], halo_doubling()))
-    own_tiles = len(parts) - 1
-    for j in range(rows + 2 * HALO):
-        y = (j + 1) // 2
-        for t, part in enumerate(parts):
-            value = part[y * x_count : (y + 1) * x_count, :]
-            va[j, t, PAD : PAD + x_count, :] = value
-            if HALO <= j < last and t < own_tiles:
-                acc[j, t] = xpre[j - HALO, t] + value
-    times(kap, va, wa, 0, rows + 2 * HALO)
+    inner = slice(PAD, PAD + x_count)
+    for y in range(wide_rows):
+        parts = []
+        for t in range(tiles1):
+            at = (t * wide_rows + y) * x_count
+            value = flat[at : at + x_count, :]
+            parts += double(value) if t < tiles1 - 1 else [double_halo(value)]
+        for j in (2 * y - 1, 2 * y):
+            if not 0 <= j < rows + 2 * HALO:
+                continue
+            for t, value in enumerate(parts):
+                va[j, t, inner, :] = value
+                wa[j, t, inner, :] = kap[j, t, inner, :] * value
+                if HALO <= j < last and t < tiles:
+                    acc[j, t] = xpre[j - HALO, t] + value
 
     edge = HALO - 1
     for j in range(-edge, rows + edge):
@@ -410,7 +406,8 @@
         else:
             source, z, i, y = rhi, zhi, j - rows, j - rows
         res[HALO + j, 0:tiles] = source[i]
-        res[HALO + j, tiles] = unpack(z[0], z[1], y, EDGE)
+        packed = z[...]
+        res[HALO + j, tiles] = unpack(packed, packed, y, EDGE, rows)
     residual_only(kap, diag, res, va, wa, 1, last + HALO - 1)
     first_update(kap, inv, res, va, wa, acc, 1, last + HALO - 1, 1.0 / centre, True, (HALO, last, tiles))
     old, new = (va, wa), (vb, wb)
@@ -419,14 +416,18 @@
         smoothing_step(kap, diag, inv, res, old, new, acc, lo, hi, pair, (HALO, last, tiles))
         old, new = new, old
         lo, hi = lo + 1, hi - 1
-    residual_only(kap, diag, res, old[0], old[1], HALO, last)
     block_x = sol.shape[0]
-    first = pl.multiple_of(me_x * block_x, 8)
-    for y in range(rows):
-        for t in range(own_tiles):
-            lanes = slice(t * LANES, (t + 1) * LANES)
-            sol[:, y, lanes] = acc[HALO + y, t, pl.ds(first, block_x), :]
-            resid[:, y, lanes] = res[HALO + y, t, pl.ds(first, block_x), :]
+    for x in range(0, x_count, 8):
+
+        @pl.when(me_x == x // block_x)
+        def _(x=x):
+            values = new_residuals(kap, diag, res, old[0], old[1], HALO, rows, x)
+            for y, (_, _, _, value) in enumerate(values):
+                for t in range(tiles):
+                    lanes = slice(t * LANES, (t + 1) * LANES)
+                    at = slice(x % block_x, x % block_x + 8)
+                    sol[at, y, lanes] = acc[HALO + y, t, x : x + 8, :]
+                    resid[at, y, lanes] = value[t]
 
 
 def ring(values, axis, step):
@@ -600,7 +601,8 @@
 
     left, right = exchange(to_left, to_right, "gz")
     coarse_z = jnp.stack([left[: 2 * xc], right[: 2 * xc]])
-    fine_z = jnp.stack([left[2 * xc :], right[2 * xc :]])
+    lane = lax.broadcasted_iota(jnp.int32, (x_count, LANES), 1)
+    fine_z = jnp.where(lane < LANES // 2, right[2 * xc :], left[2 * xc :])
     blocks, sources, low, high = gather_second(
         lines(coarse, coarse_z), lines(rpre[:edge], fine_z), lines(rpre[by - edge :], fine_z), iy, ny
     )
@@ -641,4 +643,5 @@
 
 def solution(mesh):
     spec = P("gx", "gy", "gz")
+
     return jax.shard_map(body, mesh=mesh, in_specs=(spec, spec), out_specs=(spec, spec), check_vma=False)

time: 46.3 us -> 45.5 us (0.983)
  waiting for transfers between devices: 17.5 us -> 16.9 us
    ppermute x2, starting transfers between devices: 2.64 us -> 3.79 us  [exchange(): lax.ppermute(jnp.where(odd, to_low, to_high), axis, [(i, i ^ 1) for i in...]
    ppermute x2, starting transfers between devices: 2.13 us -> 1 us  [exchange(): two = lax.ppermute(jnp.where(odd, to_high, to_low), names, pairs)]
    ppermute x3, waiting for transfers between devices: 8.57 us -> 7.84 us  [gather_second(): lax.ppermute(payload, 'gy', [(i, i ^ step) for i in range(count)])]
where the time goes in v4:
time: 45.5 us; the launch traced here: 45.3 us
  waiting for transfers between devices  16.9 us (37%)
  starting transfers between devices  14.7 us (32%)
  Pallas kernels  11.1 us (24%)
  local copies, waits for them, and re-layouts  1.52 us (3%)
  between operations  0.91 us (2%)
    pallas_call x2, Pallas kernels, call(): pl.pallas_call(kernel, out_shape=out_shapes, in_specs=[pl.BlockSpec(memor...  11.1 us
    ppermute x3, waiting for transfers between devices, gather_second(): lax.ppermute(payload, 'gy', [(i, i ^ step) for i in range(count)])  7.84 us
    ppermute x2, waiting for transfers between devices, exchange(): two = lax.ppermute(jnp.where(odd, to_high, to_low), names, pairs)  4.64 us
    ppermute x2, starting transfers between devices, exchange(): lax.ppermute(jnp.where(odd, to_low, to_high), axis, [(i, i ^ 1) for i in...  3.79 us
    ppermute x2, starting transfers between devices, exchange_and_gather(): cross = lax.ppermute(payload, ('gx', 'gz'), pairs)  3.63 us
    ppermute x3, starting transfers between devices, gather_second(): lax.ppermute(payload, 'gy', [(i, i ^ step) for i in range(count)])  3.55 us
    ppermute x2, starting transfers between devices, exchange_and_gather(): same = lax.ppermute(payload, 'gz', list(enumerate(step)))  2.72 us
    ppermute x2, waiting for transfers between devices, exchange_and_gather(): cross = lax.ppermute(payload, ('gx', 'gz'), pairs)  2.3 us
  transfers between devices with their start and end apart: 12, of which 7 were waited for; matrix products, arithmetic and copies ran while one was open for 1% of the time, Pallas kernels for 0%

profile of v4, /device:TPU:0, one launch (start us, length us, event | category | flops | bytes accessed | tf_op | source)
XLA Modules:
  0.0 45.3 jit_solution(827843973328897568)
XLA Ops:
  0.6 0.9 %copy.5 = f32[1,8,8,2,128]{4,1,3,2,0:T(8,128)S(1)} copy(f32[1,8,8,2,128]{4,2,3,1,0:T(8,128)} %bitcast.141) | data formatting | bytes 131072 | tf_op jit(solution)/shard_map/stack | solution.py:564
  1.8 0.1 concatenate.77
  1.9 0.1 concatenate.78
  2.0 2.5 %collective-permute-start.3 = (f32[8,128]{1,0:T(8,128)S(1)}, f32[8,128]{1,0:T(8,128)S(1)}, u32[]{:S(2)}, u32[]{:S(2)}) collective-permute-start(f32[8,128]{1,0:T(8,128)S(1)} %get-tuple-element.82), channel_id=1, source_target_pairs={{0,3},{1,2},{2,1},{3,0},{4,7},{5,6},{6,5},{7,4},{8,11},{9,10},{10,... | collective-permute-start | bytes 12296 | tf_op jit(solution)/shard_map/ppermute | solution.py:467
  4.5 1.7 %collective-permute-start.4 = (f32[8,128]{1,0:T(8,128)S(1)}, f32[8,128]{1,0:T(8,128)S(1)}, u32[]{:S(2)}, u32[]{:S(2)}) collective-permute-start(f32[8,128]{1,0:T(8,128)S(1)} %get-tuple-element.82), channel_id=1, source_target_pairs={{0,19},{1,18},{2,17},{3,16},{16,3},{17,2},{18,1},{19,0},{4,23},{5,... | collective-permute-start | bytes 12296 | tf_op jit(solution)/shard_map/ppermute | solution.py:469
  6.2 0.2 collective-permute-start.1
  6.4 1.9 %collective-permute-start.2 = (f32[8,128]{1,0:T(8,128)S(1)}, f32[8,128]{1,0:T(8,128)S(1)}, u32[]{:S(2)}, u32[]{:S(2)}) collective-permute-start(f32[8,128]{1,0:T(8,128)S(1)} %get-tuple-element.81), channel_id=1, source_target_pairs={{0,17},{1,16},{2,19},{3,18},{16,1},{17,0},{18,3},{19,2},{4,21},{5,... | collective-permute-start | bytes 12296 | tf_op jit(solution)/shard_map/ppermute | solution.py:469
  8.4 2.2 %collective-permute-done.2 = f32[8,128]{1,0:T(8,128)S(1)} collective-permute-done((f32[8,128]{1,0:T(8,128)S(1)}, f32[8,128]{1,0:T(8,128)S(1)}, u32[]{:S(2)}, u32[]{:S(2)}) %collective-permute-start.2) | collective-permute-done | bytes 4128 | tf_op jit(solution)/shard_map/ppermute | solution.py:469
  10.6 0.9 %collective-permute-done = f32[2,8,2,8,128]{4,3,2,1,0:T(8,128)S(1)} collective-permute-done((f32[2,8,2,8,128]{4,3,2,1,0:T(8,128)S(1)}, f32[2,8,2,8,128]{4,3,2,1,0:T(8,128)S(1)}, u32[]{:S(2)}, u32[]{:S(2)}) %collective-permute-start) | collective-permute-done | bytes 131104 | tf_op jit(solution)/shard_map/ppermute | solution.py:481
  11.7 0.6 %collective-permute-start.6 = (f32[320,128]{1,0:T(8,128)S(1)}, f32[320,128]{1,0:T(8,128)S(1)}, u32[]{:S(2)}, u32[]{:S(2)}) collective-permute-start(f32[320,128]{1,0:T(8,128)S(1)} %get-tuple-element.20), channel_id=1, source_target_pairs={{0,16},{4,8},{8,4},{12,28},{16,0},{20,24},{24,20},{28,12},{1,17},{... | collective-permute-start | bytes 491528 | tf_op jit(solution)/shard_map/ppermute | solution.py:453
  12.3 2.6 %collective-permute-start.5 = (f32[320,128]{1,0:T(8,128)S(1)}, f32[320,128]{1,0:T(8,128)S(1)}, u32[]{:S(2)}, u32[]{:S(2)}) collective-permute-start(f32[320,128]{1,0:T(8,128)S(1)} %get-tuple-element.21), channel_id=1, source_target_pairs={{0,4},{4,0},{8,12},{12,8},{1,5},{5,1},{9,13},{13,9},{2,6},{6,2},{1... | collective-permute-start | bytes 491528 | tf_op jit(solution)/shard_map/ppermute | solution.py:444
  14.9 0.1 stack.87
  15.0 0.1 stack.83.refs_0_
  15.1 2.9 %collective-permute-done.6 = f32[320,128]{1,0:T(8,128)S(1)} collective-permute-done((f32[320,128]{1,0:T(8,128)S(1)}, f32[320,128]{1,0:T(8,128)S(1)}, u32[]{:S(2)}, u32[]{:S(2)}) %collective-permute-start.6) | collective-permute-done | bytes 163872 | tf_op jit(solution)/shard_map/ppermute | solution.py:453
  18.0 1.1 %collective-permute-done.5 = f32[320,128]{1,0:T(8,128)S(1)} collective-permute-done((f32[320,128]{1,0:T(8,128)S(1)}, f32[320,128]{1,0:T(8,128)S(1)}, u32[]{:S(2)}, u32[]{:S(2)}) %collective-permute-start.5) | collective-permute-done | bytes 163872 | tf_op jit(solution)/shard_map/ppermute | solution.py:444
  19.2 3.8 %shard_map.41 = (f32[18,3,32,128]{3,2,1,0:T(8,128)S(1)}, f32[18,3,16,128]{3,2,1,0:T(8,128)S(1)}, f32[18,3,16,128]{3,2,1,0:T(8,128)S(1)}, f32[8,2,16,128]{3,2,1,0...) custom-call(s32[5]{0:T(128)S(1)} %convert_element_type.2.flags, ...), custom_call_target="tpu_custom_call" | custom-call | tf_op jit(solution)/shard_map/pallas_call | solution.py:539
  23.1 0.4 collective-permute-start.8
  23.4 1.2 %collective-permute-start.7 = (f32[32,128]{1,0:T(8,128)S(1)}, f32[32,128]{1,0:T(8,128)S(1)}, u32[]{:S(2)}, u32[]{:S(2)}) collective-permute-start(f32[32,128]{1,0:T(8,128)S(1)} %get-tuple-element.71), channel_id=1, source_target_pairs={{0,1},{1,0},{2,3},{3,2},{4,5},{5,4},{6,7},{7,6},{8,9},{9,8},{10,11... | collective-permute-start | bytes 49160 | tf_op jit(solution)/shard_map/ppermute | solution.py:444
  24.7 1.8 %collective-permute-done.8 = f32[32,128]{1,0:T(8,128)S(1)} collective-permute-done((f32[32,128]{1,0:T(8,128)S(1)}, f32[32,128]{1,0:T(8,128)S(1)}, u32[]{:S(2)}, u32[]{:S(2)}) %collective-permute-start.8) | collective-permute-done | bytes 16416 | tf_op jit(solution)/shard_map/ppermute | solution.py:453
  26.5 1.8 %collective-permute-start.9 = (f32[240,128]{1,0:T(8,128)S(1)}, f32[240,128]{1,0:T(8,128)S(1)}, u32[]{:S(2)}, u32[]{:S(2)}) collective-permute-start(f32[240,128]{1,0:T(8,128)S(1)} %get-tuple-element.67), channel_id=1, source_target_pairs={{0,4},{4,0},{8,12},{12,8},{1,5},{5,1},{9,13},{13,9},{2,6},{6,2},{1... | collective-permute-start | bytes 368648 | tf_op jit(solution)/shard_map/ppermute | solution.py:502
  28.3 1.3 %collective-permute-start.11 = (f32[240,128]{1,0:T(8,128)S(1)}, f32[240,128]{1,0:T(8,128)S(1)}, u32[]{:S(2)}, u32[]{:S(2)}) collective-permute-start(f32[240,128]{1,0:T(8,128)S(1)} %get-tuple-element.66), channel_id=1, source_target_pairs={{0,12},{4,8},{8,4},{12,0},{1,13},{5,9},{9,5},{13,1},{2,14},{6,10},... | collective-permute-start | bytes 368648 | tf_op jit(solution)/shard_map/ppermute | solution.py:502
  29.7 0.4 collective-permute-start.10
  30.1 7.8 %collective-permute-done.10 = f32[96,128]{1,0:T(8,128)S(1)} collective-permute-done((f32[96,128]{1,0:T(8,128)S(1)}, f32[96,128]{1,0:T(8,128)S(1)}, u32[]{:S(2)}, u32[]{:S(2)}) %collective-permute-start.10) | collective-permute-done | bytes 49184 | tf_op jit(solution)/shard_map/ppermute | solution.py:502
  38.1 7.2 %shard_map.42 = (f32[8,8,256]{2,1,0:T(8,128)}, f32[8,8,256]{2,1,0:T(8,128)}) custom-call(s32[8]{0:T(128)S(1)} %stack.83.refs_0_, f32[2,4,8,128]{3,2,1,0:T(8,128)S(1)} %bitcast.121, f32[2,4,8,128]{3,2,1,0:T(8,128)S(1)} %bitcast.126, f32[2,4,8,128]{3,2,1,0:T(8,128)S(1)} %bitcast.125, f32[2,4,8,128]{3,2,1,0:T(8,128)S(1)} %bitcast.127, ...), custom_call_target="tpu_custom_call" | custom-call | tf_op jit(solution)/shard_map/pallas_call | solution.py:539
  (50 shorter events, 0.6 us)
Async XLA Ops:
  0.6 0.9 %copy-start = (f32[8,8,256]{2,1,0:T(8,128)S(1)}, f32[8,8,256]{2,1,0:T(8,128)}, u32[]{:S(2)}) copy-start(f32[8,8,256]{2,1,0:T(8,128)} %param.2) | copy-start | bytes 196612
  2.0 6.4 %collective-permute-start.3 = (f32[8,128]{1,0:T(8,128)S(1)}, f32[8,128]{1,0:T(8,128)S(1)}, u32[]{:S(2)}, u32[]{:S(2)}) collective-permute-start(f32[8,128]{1,0:T(8,128)S(1)} %get-tuple-element.82), channel_id=1, source_target_pairs={{0,3},{1,2},{2,1},{3,0},{4,7},{5,6},{6,5},{7,4},{8,11},{9,10},{10,... | collective-permute-start | bytes 12296 | tf_op jit(solution)/shard_map/ppermute | solution.py:467
  4.5 3.9 %collective-permute-start.4 = (f32[8,128]{1,0:T(8,128)S(1)}, f32[8,128]{1,0:T(8,128)S(1)}, u32[]{:S(2)}, u32[]{:S(2)}) collective-permute-start(f32[8,128]{1,0:T(8,128)S(1)} %get-tuple-element.82), channel_id=1, source_target_pairs={{0,19},{1,18},{2,17},{3,16},{16,3},{17,2},{18,1},{19,0},{4,23},{5,... | collective-permute-start | bytes 12296 | tf_op jit(solution)/shard_map/ppermute | solution.py:469
  6.2 5.4 %collective-permute-start = (f32[2,8,2,8,128]{4,3,2,1,0:T(8,128)S(1)}, f32[2,8,2,8,128]{4,3,2,1,0:T(8,128)S(1)}, u32[]{:S(2)}, u32[]{:S(2)}) collective-permute-start(f32[2,8,2,8,128]{4,3,2,1,0:T(8,128)S(1)} %maximum_bitcast_fusion), channel_id=1, source_target_pairs={{0,16},{16,0},{1,17},{17,1},{2,18},{18,2},{3,19},{19,3},{4,20},{20... | collective-permute-start | bytes 393224 | tf_op jit(solution)/shard_map/ppermute | solution.py:481
  6.2 2.2 %collective-permute-start.1 = (f32[8,128]{1,0:T(8,128)S(1)}, f32[8,128]{1,0:T(8,128)S(1)}, u32[]{:S(2)}, u32[]{:S(2)}) collective-permute-start(f32[8,128]{1,0:T(8,128)S(1)} %get-tuple-element.81), channel_id=1, source_target_pairs={{0,1},{1,0},{2,3},{3,2},{4,5},{5,4},{6,7},{7,6},{8,9},{9,8},{10,11... | collective-permute-start | bytes 12296 | tf_op jit(solution)/shard_map/ppermute | solution.py:467
  6.4 4.2 %collective-permute-start.2 = (f32[8,128]{1,0:T(8,128)S(1)}, f32[8,128]{1,0:T(8,128)S(1)}, u32[]{:S(2)}, u32[]{:S(2)}) collective-permute-start(f32[8,128]{1,0:T(8,128)S(1)} %get-tuple-element.81), channel_id=1, source_target_pairs={{0,17},{1,16},{2,19},{3,18},{16,1},{17,0},{18,3},{19,2},{4,21},{5,... | collective-permute-start | bytes 12296 | tf_op jit(solution)/shard_map/ppermute | solution.py:469
  11.7 6.3 %collective-permute-start.6 = (f32[320,128]{1,0:T(8,128)S(1)}, f32[320,128]{1,0:T(8,128)S(1)}, u32[]{:S(2)}, u32[]{:S(2)}) collective-permute-start(f32[320,128]{1,0:T(8,128)S(1)} %get-tuple-element.20), channel_id=1, source_target_pairs={{0,16},{4,8},{8,4},{12,28},{16,0},{20,24},{24,20},{28,12},{1,17},{... | collective-permute-start | bytes 491528 | tf_op jit(solution)/shard_map/ppermute | solution.py:453
  12.3 6.8 %collective-permute-start.5 = (f32[320,128]{1,0:T(8,128)S(1)}, f32[320,128]{1,0:T(8,128)S(1)}, u32[]{:S(2)}, u32[]{:S(2)}) collective-permute-start(f32[320,128]{1,0:T(8,128)S(1)} %get-tuple-element.21), channel_id=1, source_target_pairs={{0,4},{4,0},{8,12},{12,8},{1,5},{5,1},{9,13},{13,9},{2,6},{6,2},{1... | collective-permute-start | bytes 491528 | tf_op jit(solution)/shard_map/ppermute | solution.py:444
  23.1 3.3 %collective-permute-start.8 = (f32[32,128]{1,0:T(8,128)S(1)}, f32[32,128]{1,0:T(8,128)S(1)}, u32[]{:S(2)}, u32[]{:S(2)}) collective-permute-start(f32[32,128]{1,0:T(8,128)S(1)} %get-tuple-element.70), channel_id=1, source_target_pairs={{0,3},{1,2},{2,1},{3,0},{4,7},{5,6},{6,5},{7,4},{8,11},{9,10},{10,... | collective-permute-start | bytes 49160 | tf_op jit(solution)/shard_map/ppermute | solution.py:453
  23.4 3.0 %collective-permute-start.7 = (f32[32,128]{1,0:T(8,128)S(1)}, f32[32,128]{1,0:T(8,128)S(1)}, u32[]{:S(2)}, u32[]{:S(2)}) collective-permute-start(f32[32,128]{1,0:T(8,128)S(1)} %get-tuple-element.71), channel_id=1, source_target_pairs={{0,1},{1,0},{2,3},{3,2},{4,5},{5,4},{6,7},{7,6},{8,9},{9,8},{10,11... | collective-permute-start | bytes 49160 | tf_op jit(solution)/shard_map/ppermute | solution.py:444
  26.5 11.4 %collective-permute-start.9 = (f32[240,128]{1,0:T(8,128)S(1)}, f32[240,128]{1,0:T(8,128)S(1)}, u32[]{:S(2)}, u32[]{:S(2)}) collective-permute-start(f32[240,128]{1,0:T(8,128)S(1)} %get-tuple-element.67), channel_id=1, source_target_pairs={{0,4},{4,0},{8,12},{12,8},{1,5},{5,1},{9,13},{13,9},{2,6},{6,2},{1... | collective-permute-start | bytes 368648 | tf_op jit(solution)/shard_map/ppermute | solution.py:502
  28.3 9.6 %collective-permute-start.11 = (f32[240,128]{1,0:T(8,128)S(1)}, f32[240,128]{1,0:T(8,128)S(1)}, u32[]{:S(2)}, u32[]{:S(2)}) collective-permute-start(f32[240,128]{1,0:T(8,128)S(1)} %get-tuple-element.66), channel_id=1, source_target_pairs={{0,12},{4,8},{8,4},{12,0},{1,13},{5,9},{9,5},{13,1},{2,14},{6,10},... | collective-permute-start | bytes 368648 | tf_op jit(solution)/shard_map/ppermute | solution.py:502
  29.7 8.2 %collective-permute-start.10 = (f32[96,128]{1,0:T(8,128)S(1)}, f32[96,128]{1,0:T(8,128)S(1)}, u32[]{:S(2)}, u32[]{:S(2)}) collective-permute-start(f32[96,128]{1,0:T(8,128)S(1)} %pad_maximum_fusion.7), channel_id=1, source_target_pairs={{0,8},{4,12},{8,0},{12,4},{1,9},{5,13},{9,1},{13,5},{2,10},{6,14},... | collective-permute-start | bytes 147464 | tf_op jit(solution)/shard_map/ppermute | solution.py:502

commit v5 on v4

--- a/solution.py
+++ b/solution.py
@@ -493,17 +493,21 @@
     low = high = low_edge
     if count == 4:
         odd = me % 2 == 1
+        near = jnp.where(odd, low_edge, high_edge)
+        far = jnp.where(odd, high_edge, low_edge)
+        nx = lax.axis_size("gx")
+        pairs = [(x * 4 + i, x * 4 + 3 - i if i in (1, 2) else (x ^ 1) * 4 + i) for x in range(nx) for i in range(4)]
+        if nx % 2:
+            pairs = [(x * 4 + i, x * 4 + 3 - i) for x in range(nx) for i in range(4)]
         got = []
         for step in (1, 2, 3):
-            payload = block
-            if step != 2:
-                edge = jnp.where(odd == (step == 1), low_edge, high_edge)
-                payload = jnp.concatenate([block, edge], axis=0)
+            payload = jnp.concatenate([block, near], axis=0) if step == 1 else block
             got.append(lax.ppermute(payload, "gy", [(i, i ^ step) for i in range(count)]))
             blocks.append(got[-1][:size])
             sources.append(me ^ step)
-        low = jnp.where(odd, got[0][size:], got[2][size:])
-        high = jnp.where(odd, got[2][size:], got[0][size:])
+        far = lax.ppermute(far, ("gx", "gy"), pairs)
+        near = got[0][size:]
+        low, high = jnp.where(odd, near, far), jnp.where(odd, far, near)
     else:
         for step in range(1, count):
             parts = [block]

time: 45.5 us -> 43.4 us (0.954)
  waiting for transfers between devices: 16.9 us -> 13.3 us
  starting transfers between devices: 14.7 us -> 16.2 us
    ppermute x3, waiting for transfers between devices: 7.84 us -> 4.31 us  [gather_second(): lax.ppermute(payload, 'gy', [(i, i ^ step) for i in range(count)])]
    ppermute x3, starting transfers between devices: 3.55 us -> 4.45 us  [gather_second(): lax.ppermute(payload, 'gy', [(i, i ^ step) for i in range(count)])]
    ppermute x0 -> x1, starting transfers between devices: none -> 0.62 us  [gather_second(): far = lax.ppermute(far, ('gx', 'gy'), pairs)]
  transfers between devices with their start and end apart: 12 -> 13, of which waited for: 7 -> 8; matrix products, arithmetic and copies ran while one was open for 1% -> 1% of each run, Pallas kernels for 0% -> 0%
where the time goes in v5:
time: 43.4 us; the launch traced here: 43.3 us
  starting transfers between devices  16.2 us (37%)
  waiting for transfers between devices  13.3 us (31%)
  Pallas kernels  11.1 us (26%)
  local copies, waits for them, and re-layouts  1.52 us (4%)
  between operations  0.9 us (2%)
    pallas_call x2, Pallas kernels, call(): pl.pallas_call(kernel, out_shape=out_shapes, in_specs=[pl.BlockSpec(memor...  11.1 us
    ppermute x2, waiting for transfers between devices, exchange(): two = lax.ppermute(jnp.where(odd, to_high, to_low), names, pairs)  4.64 us
    ppermute x3, starting transfers between devices, gather_second(): lax.ppermute(payload, 'gy', [(i, i ^ step) for i in range(count)])  4.45 us
    ppermute x3, waiting for transfers between devices, gather_second(): lax.ppermute(payload, 'gy', [(i, i ^ step) for i in range(count)])  4.31 us
    ppermute x2, starting transfers between devices, exchange(): lax.ppermute(jnp.where(odd, to_low, to_high), axis, [(i, i ^ 1) for i in...  3.79 us
    ppermute x2, starting transfers between devices, exchange_and_gather(): cross = lax.ppermute(payload, ('gx', 'gz'), pairs)  3.63 us
    ppermute x2, starting transfers between devices, exchange_and_gather(): same = lax.ppermute(payload, 'gz', list(enumerate(step)))  2.72 us
    ppermute x2, waiting for transfers between devices, exchange_and_gather(): cross = lax.ppermute(payload, ('gx', 'gz'), pairs)  2.3 us
  transfers between devices with their start and end apart: 13, of which 8 were waited for; matrix products, arithmetic and copies ran while one was open for 1% of the time, Pallas kernels for 0%

profile of v5, /device:TPU:0, one launch (start us, length us, event | category | flops | bytes accessed | tf_op | source)
XLA Modules:
  0.0 43.3 jit_solution(13015563567241773955)
XLA Ops:
  0.6 0.9 %copy.5 = f32[1,8,8,2,128]{4,1,3,2,0:T(8,128)S(1)} copy(f32[1,8,8,2,128]{4,2,3,1,0:T(8,128)} %bitcast.141) | data formatting | bytes 131072 | tf_op jit(solution)/shard_map/stack | solution.py:568
  1.8 0.1 concatenate.73
  2.0 2.5 %collective-permute-start.3 = (f32[8,128]{1,0:T(8,128)S(1)}, f32[8,128]{1,0:T(8,128)S(1)}, u32[]{:S(2)}, u32[]{:S(2)}) collective-permute-start(f32[8,128]{1,0:T(8,128)S(1)} %get-tuple-element.80), channel_id=1, source_target_pairs={{0,3},{1,2},{2,1},{3,0},{4,7},{5,6},{6,5},{7,4},{8,11},{9,10},{10,... | collective-permute-start | bytes 12296 | tf_op jit(solution)/shard_map/ppermute | solution.py:467
  4.5 1.7 %collective-permute-start.4 = (f32[8,128]{1,0:T(8,128)S(1)}, f32[8,128]{1,0:T(8,128)S(1)}, u32[]{:S(2)}, u32[]{:S(2)}) collective-permute-start(f32[8,128]{1,0:T(8,128)S(1)} %get-tuple-element.80), channel_id=1, source_target_pairs={{0,19},{1,18},{2,17},{3,16},{16,3},{17,2},{18,1},{19,0},{4,23},{5,... | collective-permute-start | bytes 12296 | tf_op jit(solution)/shard_map/ppermute | solution.py:469
  6.2 0.2 collective-permute-start.1
  6.4 1.9 %collective-permute-start.2 = (f32[8,128]{1,0:T(8,128)S(1)}, f32[8,128]{1,0:T(8,128)S(1)}, u32[]{:S(2)}, u32[]{:S(2)}) collective-permute-start(f32[8,128]{1,0:T(8,128)S(1)} %get-tuple-element.79), channel_id=1, source_target_pairs={{0,17},{1,16},{2,19},{3,18},{16,1},{17,0},{18,3},{19,2},{4,21},{5,... | collective-permute-start | bytes 12296 | tf_op jit(solution)/shard_map/ppermute | solution.py:469
  8.4 2.2 %collective-permute-done.2 = f32[8,128]{1,0:T(8,128)S(1)} collective-permute-done((f32[8,128]{1,0:T(8,128)S(1)}, f32[8,128]{1,0:T(8,128)S(1)}, u32[]{:S(2)}, u32[]{:S(2)}) %collective-permute-start.2) | collective-permute-done | bytes 4128 | tf_op jit(solution)/shard_map/ppermute | solution.py:469
  10.6 0.9 %collective-permute-done = f32[2,8,2,8,128]{4,3,2,1,0:T(8,128)S(1)} collective-permute-done((f32[2,8,2,8,128]{4,3,2,1,0:T(8,128)S(1)}, f32[2,8,2,8,128]{4,3,2,1,0:T(8,128)S(1)}, u32[]{:S(2)}, u32[]{:S(2)}) %collective-permute-start) | collective-permute-done | bytes 131104 | tf_op jit(solution)/shard_map/ppermute | solution.py:481
  11.7 0.6 %collective-permute-start.6 = (f32[320,128]{1,0:T(8,128)S(1)}, f32[320,128]{1,0:T(8,128)S(1)}, u32[]{:S(2)}, u32[]{:S(2)}) collective-permute-start(f32[320,128]{1,0:T(8,128)S(1)} %get-tuple-element.20), channel_id=1, source_target_pairs={{0,16},{4,8},{8,4},{12,28},{16,0},{20,24},{24,20},{28,12},{1,17},{... | collective-permute-start | bytes 491528 | tf_op jit(solution)/shard_map/ppermute | solution.py:453
  12.3 2.6 %collective-permute-start.5 = (f32[320,128]{1,0:T(8,128)S(1)}, f32[320,128]{1,0:T(8,128)S(1)}, u32[]{:S(2)}, u32[]{:S(2)}) collective-permute-start(f32[320,128]{1,0:T(8,128)S(1)} %get-tuple-element.21), channel_id=1, source_target_pairs={{0,4},{4,0},{8,12},{12,8},{1,5},{5,1},{9,13},{13,9},{2,6},{6,2},{1... | collective-permute-start | bytes 491528 | tf_op jit(solution)/shard_map/ppermute | solution.py:444
  14.9 0.1 stack.87
  15.1 2.9 %collective-permute-done.6 = f32[320,128]{1,0:T(8,128)S(1)} collective-permute-done((f32[320,128]{1,0:T(8,128)S(1)}, f32[320,128]{1,0:T(8,128)S(1)}, u32[]{:S(2)}, u32[]{:S(2)}) %collective-permute-start.6) | collective-permute-done | bytes 163872 | tf_op jit(solution)/shard_map/ppermute | solution.py:453
  18.0 1.1 %collective-permute-done.5 = f32[320,128]{1,0:T(8,128)S(1)} collective-permute-done((f32[320,128]{1,0:T(8,128)S(1)}, f32[320,128]{1,0:T(8,128)S(1)}, u32[]{:S(2)}, u32[]{:S(2)}) %collective-permute-start.5) | collective-permute-done | bytes 163872 | tf_op jit(solution)/shard_map/ppermute | solution.py:444
  19.2 3.8 %shard_map.41 = (f32[18,3,32,128]{3,2,1,0:T(8,128)S(1)}, f32[18,3,16,128]{3,2,1,0:T(8,128)S(1)}, f32[18,3,16,128]{3,2,1,0:T(8,128)S(1)}, f32[8,2,16,128]{3,2,1,0...) custom-call(s32[5]{0:T(128)S(1)} %convert_element_type.2.flags, ...), custom_call_target="tpu_custom_call" | custom-call | tf_op jit(solution)/shard_map/pallas_call | solution.py:543
  23.1 0.4 collective-permute-start.8
  23.4 1.2 %collective-permute-start.7 = (f32[32,128]{1,0:T(8,128)S(1)}, f32[32,128]{1,0:T(8,128)S(1)}, u32[]{:S(2)}, u32[]{:S(2)}) collective-permute-start(f32[32,128]{1,0:T(8,128)S(1)} %get-tuple-element.69), channel_id=1, source_target_pairs={{0,1},{1,0},{2,3},{3,2},{4,5},{5,4},{6,7},{7,6},{8,9},{9,8},{10,11... | collective-permute-start | bytes 49160 | tf_op jit(solution)/shard_map/ppermute | solution.py:444
  24.7 1.8 %collective-permute-done.8 = f32[32,128]{1,0:T(8,128)S(1)} collective-permute-done((f32[32,128]{1,0:T(8,128)S(1)}, f32[32,128]{1,0:T(8,128)S(1)}, u32[]{:S(2)}, u32[]{:S(2)}) %collective-permute-start.8) | collective-permute-done | bytes 16416 | tf_op jit(solution)/shard_map/ppermute | solution.py:453
  26.5 1.8 %collective-permute-start.9 = (f32[240,128]{1,0:T(8,128)S(1)}, f32[240,128]{1,0:T(8,128)S(1)}, u32[]{:S(2)}, u32[]{:S(2)}) collective-permute-start(f32[240,128]{1,0:T(8,128)S(1)} %pad_maximum_fusion.3), channel_id=1, source_target_pairs={{0,4},{4,0},{8,12},{12,8},{1,5},{5,1},{9,13},{13,9},{2,6},{6,2},{1... | collective-permute-start | bytes 368648 | tf_op jit(solution)/shard_map/ppermute | solution.py:505
  28.3 1.6 %collective-permute-start.10 = (f32[96,128]{1,0:T(8,128)S(1)}, f32[96,128]{1,0:T(8,128)S(1)}, u32[]{:S(2)}, u32[]{:S(2)}) collective-permute-start(f32[96,128]{1,0:T(8,128)S(1)} %pad_maximum_fusion.6), channel_id=1, source_target_pairs={{0,8},{4,12},{8,0},{12,4},{1,9},{5,13},{9,1},{13,5},{2,10},{6,14},... | collective-permute-start | bytes 147464 | tf_op jit(solution)/shard_map/ppermute | solution.py:505
  29.9 1.1 %collective-permute-start.11 = (f32[96,128]{1,0:T(8,128)S(1)}, f32[96,128]{1,0:T(8,128)S(1)}, u32[]{:S(2)}, u32[]{:S(2)}) collective-permute-start(f32[96,128]{1,0:T(8,128)S(1)} %pad_maximum_fusion.6), channel_id=1, source_target_pairs={{0,12},{4,8},{8,4},{12,0},{1,13},{5,9},{9,5},{13,1},{2,14},{6,10},... | collective-permute-start | bytes 147464 | tf_op jit(solution)/shard_map/ppermute | solution.py:505
  31.0 0.6 %collective-permute-start.12 = (f32[144,128]{1,0:T(8,128)S(1)}, f32[144,128]{1,0:T(8,128)S(1)}, u32[]{:S(2)}, u32[]{:S(2)}) collective-permute-start(f32[144,128]{1,0:T(8,128)S(1)} %get-tuple-element.30), channel_id=1, source_target_pairs={{0,16},{4,8},{8,4},{12,28},{16,0},{20,24},{24,20},{28,12},{1,17},{... | collective-permute-start | bytes 221192 | tf_op jit(solution)/shard_map/ppermute | solution.py:508
  31.6 3.4 %collective-permute-done.10 = f32[96,128]{1,0:T(8,128)S(1)} collective-permute-done((f32[96,128]{1,0:T(8,128)S(1)}, f32[96,128]{1,0:T(8,128)S(1)}, u32[]{:S(2)}, u32[]{:S(2)}) %collective-permute-start.10) | collective-permute-done | bytes 49184 | tf_op jit(solution)/shard_map/ppermute | solution.py:505
  35.0 0.9 %collective-permute-done.11 = f32[96,128]{1,0:T(8,128)S(1)} collective-permute-done((f32[96,128]{1,0:T(8,128)S(1)}, f32[96,128]{1,0:T(8,128)S(1)}, u32[]{:S(2)}, u32[]{:S(2)}) %collective-permute-start.11) | collective-permute-done | bytes 49184 | tf_op jit(solution)/shard_map/ppermute | solution.py:505
  36.0 7.2 %shard_map.42 = (f32[8,8,256]{2,1,0:T(8,128)}, f32[8,8,256]{2,1,0:T(8,128)}) custom-call(s32[8]{0:T(128)S(1)} %stack.83.refs_0_, f32[2,4,8,128]{3,2,1,0:T(8,128)S(1)} %bitcast.121, f32[2,4,8,128]{3,2,1,0:T(8,128)S(1)} %bitcast.127, f32[2,4,8,128]{3,2,1,0:T(8,128)S(1)} %bitcast.125, f32[2,4,8,128]{3,2,1,0:T(8,128)S(1)} %bitcast.126, ...), custom_call_target="tpu_custom_call" | custom-call | tf_op jit(solution)/shard_map/pallas_call | solution.py:543
  (52 shorter events, 0.8 us)
Async XLA Ops:
  0.6 0.9 %copy-start = (f32[8,8,256]{2,1,0:T(8,128)S(1)}, f32[8,8,256]{2,1,0:T(8,128)}, u32[]{:S(2)}) copy-start(f32[8,8,256]{2,1,0:T(8,128)} %param.2) | copy-start | bytes 196612
  2.0 6.4 %collective-permute-start.3 = (f32[8,128]{1,0:T(8,128)S(1)}, f32[8,128]{1,0:T(8,128)S(1)}, u32[]{:S(2)}, u32[]{:S(2)}) collective-permute-start(f32[8,128]{1,0:T(8,128)S(1)} %get-tuple-element.80), channel_id=1, source_target_pairs={{0,3},{1,2},{2,1},{3,0},{4,7},{5,6},{6,5},{7,4},{8,11},{9,10},{10,... | collective-permute-start | bytes 12296 | tf_op jit(solution)/shard_map/ppermute | solution.py:467
  4.5 3.9 %collective-permute-start.4 = (f32[8,128]{1,0:T(8,128)S(1)}, f32[8,128]{1,0:T(8,128)S(1)}, u32[]{:S(2)}, u32[]{:S(2)}) collective-permute-start(f32[8,128]{1,0:T(8,128)S(1)} %get-tuple-element.80), channel_id=1, source_target_pairs={{0,19},{1,18},{2,17},{3,16},{16,3},{17,2},{18,1},{19,0},{4,23},{5,... | collective-permute-start | bytes 12296 | tf_op jit(solution)/shard_map/ppermute | solution.py:469
  6.2 5.4 %collective-permute-start = (f32[2,8,2,8,128]{4,3,2,1,0:T(8,128)S(1)}, f32[2,8,2,8,128]{4,3,2,1,0:T(8,128)S(1)}, u32[]{:S(2)}, u32[]{:S(2)}) collective-permute-start(f32[2,8,2,8,128]{4,3,2,1,0:T(8,128)S(1)} %maximum_bitcast_fusion), channel_id=1, source_target_pairs={{0,16},{16,0},{1,17},{17,1},{2,18},{18,2},{3,19},{19,3},{4,20},{20... | collective-permute-start | bytes 393224 | tf_op jit(solution)/shard_map/ppermute | solution.py:481
  6.2 2.2 %collective-permute-start.1 = (f32[8,128]{1,0:T(8,128)S(1)}, f32[8,128]{1,0:T(8,128)S(1)}, u32[]{:S(2)}, u32[]{:S(2)}) collective-permute-start(f32[8,128]{1,0:T(8,128)S(1)} %get-tuple-element.79), channel_id=1, source_target_pairs={{0,1},{1,0},{2,3},{3,2},{4,5},{5,4},{6,7},{7,6},{8,9},{9,8},{10,11... | collective-permute-start | bytes 12296 | tf_op jit(solution)/shard_map/ppermute | solution.py:467
  6.4 4.2 %collective-permute-start.2 = (f32[8,128]{1,0:T(8,128)S(1)}, f32[8,128]{1,0:T(8,128)S(1)}, u32[]{:S(2)}, u32[]{:S(2)}) collective-permute-start(f32[8,128]{1,0:T(8,128)S(1)} %get-tuple-element.79), channel_id=1, source_target_pairs={{0,17},{1,16},{2,19},{3,18},{16,1},{17,0},{18,3},{19,2},{4,21},{5,... | collective-permute-start | bytes 12296 | tf_op jit(solution)/shard_map/ppermute | solution.py:469
  11.7 6.3 %collective-permute-start.6 = (f32[320,128]{1,0:T(8,128)S(1)}, f32[320,128]{1,0:T(8,128)S(1)}, u32[]{:S(2)}, u32[]{:S(2)}) collective-permute-start(f32[320,128]{1,0:T(8,128)S(1)} %get-tuple-element.20), channel_id=1, source_target_pairs={{0,16},{4,8},{8,4},{12,28},{16,0},{20,24},{24,20},{28,12},{1,17},{... | collective-permute-start | bytes 491528 | tf_op jit(solution)/shard_map/ppermute | solution.py:453
  12.3 6.8 %collective-permute-start.5 = (f32[320,128]{1,0:T(8,128)S(1)}, f32[320,128]{1,0:T(8,128)S(1)}, u32[]{:S(2)}, u32[]{:S(2)}) collective-permute-start(f32[320,128]{1,0:T(8,128)S(1)} %get-tuple-element.21), channel_id=1, source_target_pairs={{0,4},{4,0},{8,12},{12,8},{1,5},{5,1},{9,13},{13,9},{2,6},{6,2},{1... | collective-permute-start | bytes 491528 | tf_op jit(solution)/shard_map/ppermute | solution.py:444
  23.1 3.3 %collective-permute-start.8 = (f32[32,128]{1,0:T(8,128)S(1)}, f32[32,128]{1,0:T(8,128)S(1)}, u32[]{:S(2)}, u32[]{:S(2)}) collective-permute-start(f32[32,128]{1,0:T(8,128)S(1)} %get-tuple-element.68), channel_id=1, source_target_pairs={{0,3},{1,2},{2,1},{3,0},{4,7},{5,6},{6,5},{7,4},{8,11},{9,10},{10,... | collective-permute-start | bytes 49160 | tf_op jit(solution)/shard_map/ppermute | solution.py:453
  23.4 3.0 %collective-permute-start.7 = (f32[32,128]{1,0:T(8,128)S(1)}, f32[32,128]{1,0:T(8,128)S(1)}, u32[]{:S(2)}, u32[]{:S(2)}) collective-permute-start(f32[32,128]{1,0:T(8,128)S(1)} %get-tuple-element.69), channel_id=1, source_target_pairs={{0,1},{1,0},{2,3},{3,2},{4,5},{5,4},{6,7},{7,6},{8,9},{9,8},{10,11... | collective-permute-start | bytes 49160 | tf_op jit(solution)/shard_map/ppermute | solution.py:444
  26.5 9.4 %collective-permute-start.9 = (f32[240,128]{1,0:T(8,128)S(1)}, f32[240,128]{1,0:T(8,128)S(1)}, u32[]{:S(2)}, u32[]{:S(2)}) collective-permute-start(f32[240,128]{1,0:T(8,128)S(1)} %pad_maximum_fusion.3), channel_id=1, source_target_pairs={{0,4},{4,0},{8,12},{12,8},{1,5},{5,1},{9,13},{13,9},{2,6},{6,2},{1... | collective-permute-start | bytes 368648 | tf_op jit(solution)/shard_map/ppermute | solution.py:505
  28.3 6.7 %collective-permute-start.10 = (f32[96,128]{1,0:T(8,128)S(1)}, f32[96,128]{1,0:T(8,128)S(1)}, u32[]{:S(2)}, u32[]{:S(2)}) collective-permute-start(f32[96,128]{1,0:T(8,128)S(1)} %pad_maximum_fusion.6), channel_id=1, source_target_pairs={{0,8},{4,12},{8,0},{12,4},{1,9},{5,13},{9,1},{13,5},{2,10},{6,14},... | collective-permute-start | bytes 147464 | tf_op jit(solution)/shard_map/ppermute | solution.py:505
  29.9 6.0 %collective-permute-start.11 = (f32[96,128]{1,0:T(8,128)S(1)}, f32[96,128]{1,0:T(8,128)S(1)}, u32[]{:S(2)}, u32[]{:S(2)}) collective-permute-start(f32[96,128]{1,0:T(8,128)S(1)} %pad_maximum_fusion.6), channel_id=1, source_target_pairs={{0,12},{4,8},{8,4},{12,0},{1,13},{5,9},{9,5},{13,1},{2,14},{6,10},... | collective-permute-start | bytes 147464 | tf_op jit(solution)/shard_map/ppermute | solution.py:505
  31.0 4.9 %collective-permute-start.12 = (f32[144,128]{1,0:T(8,128)S(1)}, f32[144,128]{1,0:T(8,128)S(1)}, u32[]{:S(2)}, u32[]{:S(2)}) collective-permute-start(f32[144,128]{1,0:T(8,128)S(1)} %get-tuple-element.30), channel_id=1, source_target_pairs={{0,16},{4,8},{8,4},{12,28},{16,0},{20,24},{24,20},{28,12},{1,17},{... | collective-permute-start | bytes 221192 | tf_op jit(solution)/shard_map/ppermute | solution.py:508

commit v6 on v5

--- a/solution.py
+++ b/solution.py
@@ -236,17 +236,20 @@
     return jnp.where(lane < width, first, jnp.where(lane >= LANES - width, last, 0.0))
 
 
-def before_kernel(flags, own, zown, ylo, zlo, yhi, zhi, kap, diag, inv, xout, rout, coarse, to_left, to_right, va, wa, vb, wb, res, acc, flat):
+def before_kernel(own, zown, ylo, zlo, yhi, zhi, kap, diag, inv, xout, rout, coarse, to_left, to_right, va, wa, vb, wb, res, acc, flat):
     rows = own.shape[1]
     tiles = own.shape[2]
     x_count = own.shape[3]
     inner = slice(PAD, PAD + x_count)
     last = HALO + rows
+    iy, iz = lax.axis_index("gy"), lax.axis_index("gz")
+    ny, nz = lax.axis_size("gy"), lax.axis_size("gz")
+    has_left, has_right = iz > 0, iz < nz - 1
     zero_pads((kap, va, wa, vb, wb))
 
     def fill(j, k, b, z, y, there):
-        left = jnp.where((flags[0] > 0) & there, z[0], 0.0)
-        right = jnp.where((flags[1] > 0) & there, z[1], 0.0)
+        left = jnp.where(has_left & there, z[0], 0.0)
+        right = jnp.where(has_right & there, z[1], 0.0)
         kap[j, 0:tiles, inner, :] = jnp.where(there, SCALE * k, 0.0)
         kap[j, tiles, inner, :] = SCALE * unpack(left, right, y, EDGE)
         if b is not None:
@@ -254,12 +257,12 @@
             res[j, tiles] = unpack(z[0], z[1], rows + y, EDGE)
 
     for y in range(rows):
-        fill(HALO + y, own[0, y], own[1, y], zown, y, flags[4] > 0)
+        fill(HALO + y, own[0, y], own[1, y], zown, y, iy >= 0)
     for j in range(HALO):
         b = ylo[HALO + j - 1] if j else None
-        fill(j, ylo[j], b, zlo, rows - HALO + j, flags[2] > 0)
+        fill(j, ylo[j], b, zlo, rows - HALO + j, iy > 0)
         b = yhi[HALO + j] if j < HALO - 1 else None
-        fill(last + j, yhi[j], b, zhi, j, flags[3] > 0)
+        fill(last + j, yhi[j], b, zhi, j, iy < ny - 1)
     make_diagonal(kap, diag, inv, 1, last + HALO - 1)
     centre, weights = chebyshev_coefs(DEGREE, smooth_low)
     first_update(kap, inv, res, va, wa, acc, 1, last + HALO - 1, 1.0 / centre, False, (HALO, last, tiles))
@@ -293,12 +296,20 @@
         out[2 * xc : 2 * xc + x_count, :] = pack(value, EDGE, from_end, rows if from_end else 0)
 
 
-def after_kernel(places, *refs, count):
+def sources_of(me, count):
+    if count == 4:
+        return [me] + [jnp.bitwise_xor(me, step) for step in (1, 2, 3)]
+    return [me] + [lax.rem(me - step + count, count) for step in range(1, count)]
+
+
+def after_kernel(*refs, count):
     blocks, zblocks = refs[:count], refs[count : 2 * count]
     refs = refs[2 * count :]
     (kap, diag, inv, xpre, rown, zown, rlo, zlo, rhi, zhi, sol, resid) = refs[:12]
     (k1, d1, i1, r1, x1, va1, wa1, vb1, wb1, k2, d2, i2, r2, x2, va2, wa2, vb2, wb2, flat, va, wa, vb, wb, res, acc) = refs[12:]
-    me_x, me_y = places[0], places[1]
+    me_x, me_y, me_z = (lax.axis_index(a) for a in ("gx", "gy", "gz"))
+    has_left, has_right = me_z > 0, me_z < lax.axis_size("gz") - 1
+    sources = sources_of(me_y, count)
     zero_pads((k1, va1, wa1, vb1, wb1, k2, va2, wa2, vb2, wb2, va, wa, vb, wb))
     each = blocks[0].shape[1]
     xc = blocks[0].shape[2]
@@ -310,9 +321,9 @@
         zero_rows(ref, edge)
     zero_rows(x1, list(range(lo1)) + list(range(hi1, hi1 + COARSE_PAD)))
     for number, (block, z) in enumerate(zip(blocks, zblocks)):
-        at = places[4 + number] * each + COARSE_PAD
-        left = jnp.where(places[2] > 0, z[0, 0], 0.0)
-        right = jnp.where(places[3] > 0, z[1, 0], 0.0)
+        at = sources[number] * each + COARSE_PAD
+        left = jnp.where(has_left, z[0, 0], 0.0)
+        right = jnp.where(has_right, z[1, 0], 0.0)
         for y in range(each):
             k1[at + y, 0, PAD : PAD + xc, :] = block[0, y] * 0.25
             k1[at + y, 1, PAD : PAD + xc, :] = unpack(left, right, y, COARSE_EDGE) * 0.25
@@ -489,7 +500,7 @@
 
 def gather_second(block, low_edge, high_edge, me, count):
     size = block.shape[0]
-    blocks, sources = [block], [me]
+    blocks = [block]
     low = high = low_edge
     if count == 4:
         odd = me % 2 == 1
@@ -504,7 +515,6 @@
             payload = jnp.concatenate([block, near], axis=0) if step == 1 else block
             got.append(lax.ppermute(payload, "gy", [(i, i ^ step) for i in range(count)]))
             blocks.append(got[-1][:size])
-            sources.append(me ^ step)
         far = lax.ppermute(far, ("gx", "gy"), pairs)
         near = got[0][size:]
         low, high = jnp.where(odd, near, far), jnp.where(odd, far, near)
@@ -517,12 +527,11 @@
                 parts.append(low_edge)
             got = ring(jnp.concatenate(parts, axis=0), "gy", step)
             blocks.append(got[:size])
-            sources.append((me - step) % count)
             if step == 1:
                 low = got[size : size + high_edge.shape[0]]
             if step == count - 1:
                 high = got[got.shape[0] - low_edge.shape[0] :]
-    return blocks, sources, low, high
+    return blocks, low, high
 
 
 def vmem(shape):
@@ -543,7 +552,7 @@
     return pl.pallas_call(
         kernel,
         out_shape=out_shapes,
-        in_specs=[pl.BlockSpec(memory_space=pltpu.SMEM)] + [whole] * (len(inputs) - 1),
+        in_specs=[whole] * len(inputs),
         out_specs=[whole] * len(out_shapes),
         scratch_shapes=scratch,
         compiler_params=pltpu.CompilerParams(vmem_limit_bytes=limit),
@@ -553,10 +562,8 @@
 def body(conductivity, source):
     bx, by, bz = conductivity.shape
     tiles = bz // LANES
-    nx, ny, nz = (lax.axis_size(a) for a in ("gx", "gy", "gz"))
-    ix, iy, iz = (lax.axis_index(a) for a in ("gx", "gy", "gz"))
-    yes = ix >= 0
-    flags = jnp.stack([iz > 0, iz < nz - 1, iy > 0, iy < ny - 1, yes]).astype(jnp.int32)
+    nx, ny, _ = (lax.axis_size(a) for a in ("gx", "gy", "gz"))
+    iy = lax.axis_index("gy")
     x_count = bx * nx
 
     def shape(*dims):
@@ -600,14 +607,14 @@
             shape(2 * xc + x_count, LANES),
         ],
         [vmem(wide)] * 4 + [vmem(plain)] * 2 + [vmem((2 * each * x_count, LANES))],
-        [flags, own, zown, ylo, zlo, yhi, zhi],
+        [own, zown, ylo, zlo, yhi, zhi],
     )
 
     left, right = exchange(to_left, to_right, "gz")
     coarse_z = jnp.stack([left[: 2 * xc], right[: 2 * xc]])
     lane = lax.broadcasted_iota(jnp.int32, (x_count, LANES), 1)
     fine_z = jnp.where(lane < LANES // 2, right[2 * xc :], left[2 * xc :])
-    blocks, sources, low, high = gather_second(
+    blocks, low, high = gather_second(
         lines(coarse, coarse_z), lines(rpre[:edge], fine_z), lines(rpre[by - edge :], fine_z), iy, ny
     )
     cut = 2 * each * xc
@@ -628,7 +635,6 @@
     plain2 = (y2 + 2, 1, x2, LANES)
     flat_rows = max(y2 * xc, tiles1 * (ext // 2 + 1) * x_count)
 
-    places = jnp.stack([jnp.int32(p) for p in (ix, iy, iz > 0, iz < nz - 1, *sources)])
 
     def kernel(*refs):
         after_kernel(*refs, count=len(blocks))
@@ -639,7 +645,7 @@
         [vmem(wide1)] + [vmem(plain1)] * 4 + [vmem(wide1)] * 4
         + [vmem(wide2)] + [vmem(plain2)] * 4 + [vmem(wide2)] * 4
         + [vmem((flat_rows, LANES))] + [vmem(wide)] * 4 + [vmem(plain)] * 2,
-        [places] + blocks + zblocks
+        blocks + zblocks
         + [kap, diag, inv, xpre, rpre, fine_z, rlo, zrlo, rhi, zrhi],
     )
     return sol, resid

time: 43.4 us -> 42.7 us (0.984)
  Pallas kernels: 11.1 us -> 9.58 us
  starting transfers between devices: 16.2 us -> 17.2 us
    ppermute x2, starting transfers between devices: 1 us -> 3.07 us  [exchange(): two = lax.ppermute(jnp.where(odd, to_high, to_low), names, pairs)]
    ppermute x1, starting transfers between devices: 0.01 us -> 1.98 us  [gather_first(): other = lax.ppermute(values, axis, [(0, 1), (1, 0)])]
    ppermute x2, starting transfers between devices: 3.79 us -> 1.87 us  [exchange(): lax.ppermute(jnp.where(odd, to_low, to_high), axis, [(i, i ^ 1) for i in...]
    ppermute x2, waiting for transfers between devices: 4.64 us -> 2.98 us  [exchange(): two = lax.ppermute(jnp.where(odd, to_high, to_low), names, pairs)]
    pallas_call x2, Pallas kernels: 11.1 us -> 9.58 us  [call(): pl.pallas_call(kernel, out_shape=out_shapes, in_specs=[whole] * len(input...]
    ppermute x2, waiting for transfers between devices: 1.13 us -> 2.45 us  [exchange(): lax.ppermute(jnp.where(odd, to_low, to_high), axis, [(i, i ^ 1) for i in...]
    ppermute x2, starting transfers between devices: 3.63 us -> 2.61 us  [exchange_and_gather(): cross = lax.ppermute(payload, ('gx', 'gz'), pairs)]
    ppermute x1, waiting for transfers between devices: 0.94 us -> 1.93 us  [gather_first(): other = lax.ppermute(values, axis, [(0, 1), (1, 0)])]
  transfers between devices with their start and end apart: 13 -> 13, of which waited for: 8 -> 7; matrix products, arithmetic and copies ran while one was open for 1% -> 0% of each run, Pallas kernels for 0% -> 0%
where the time goes in v6:
time: 42.7 us; the launch traced here: 42.5 us
  starting transfers between devices  17.2 us (40%)
  waiting for transfers between devices  13.3 us (31%)
  Pallas kernels  9.58 us (22%)
  local copies, waits for them, and re-layouts  1.34 us (3%)
  between operations  0.9 us (2%)
    pallas_call x2, Pallas kernels, call(): pl.pallas_call(kernel, out_shape=out_shapes, in_specs=[whole] * len(input...  9.58 us
    ppermute x3, starting transfers between devices, gather_second(): lax.ppermute(payload, 'gy', [(i, i ^ step) for i in range(count)])  4.45 us
    ppermute x3, waiting for transfers between devices, gather_second(): lax.ppermute(payload, 'gy', [(i, i ^ step) for i in range(count)])  4.04 us
    ppermute x2, starting transfers between devices, exchange(): two = lax.ppermute(jnp.where(odd, to_high, to_low), names, pairs)  3.07 us
    ppermute x2, waiting for transfers between devices, exchange(): two = lax.ppermute(jnp.where(odd, to_high, to_low), names, pairs)  2.98 us
    ppermute x2, starting transfers between devices, exchange_and_gather(): cross = lax.ppermute(payload, ('gx', 'gz'), pairs)  2.61 us
    ppermute x2, waiting for transfers between devices, exchange(): lax.ppermute(jnp.where(odd, to_low, to_high), axis, [(i, i ^ 1) for i in...  2.45 us
    ppermute x1, starting transfers between devices, gather_first(): other = lax.ppermute(values, axis, [(0, 1), (1, 0)])  1.98 us
  transfers between devices with their start and end apart: 13, of which 7 were waited for; matrix products, arithmetic and copies ran while one was open for 0% of the time, Pallas kernels for 0%

profile of v6, /device:TPU:0, one launch (start us, length us, event | category | flops | bytes accessed | tf_op | source)
XLA Modules:
  0.0 42.5 jit_solution(4368367417474622217)
XLA Ops:
  0.6 0.9 %copy.4 = f32[1,8,8,2,128]{4,1,3,2,0:T(8,128)S(1)} copy(f32[1,8,8,2,128]{4,2,3,1,0:T(8,128)} %bitcast.131) | data formatting | bytes 131072 | tf_op jit(solution)/shard_map/stack | solution.py:575
  1.6 0.1 slice_bitcast_fusion.20
  1.8 0.1 concatenate.74
  1.8 0.1 concatenate.73
  2.0 0.6 %collective-permute-start.1 = (f32[8,128]{1,0:T(8,128)S(1)}, f32[8,128]{1,0:T(8,128)S(1)}, u32[]{:S(2)}, u32[]{:S(2)}) collective-permute-start(f32[8,128]{1,0:T(8,128)S(1)} %get-tuple-element.79), channel_id=1, source_target_pairs={{0,1},{1,0},{2,3},{3,2},{4,5},{5,4},{6,7},{7,6},{8,9},{9,8},{10,11... | collective-permute-start | bytes 12296 | tf_op jit(solution)/shard_map/ppermute | solution.py:478
  2.5 2.6 %collective-permute-start.2 = (f32[8,128]{1,0:T(8,128)S(1)}, f32[8,128]{1,0:T(8,128)S(1)}, u32[]{:S(2)}, u32[]{:S(2)}) collective-permute-start(f32[8,128]{1,0:T(8,128)S(1)} %get-tuple-element.79), channel_id=1, source_target_pairs={{0,17},{1,16},{2,19},{3,18},{16,1},{17,0},{18,3},{19,2},{4,21},{5,... | collective-permute-start | bytes 12296 | tf_op jit(solution)/shard_map/ppermute | solution.py:480
  5.1 1.2 %collective-permute-start.3 = (f32[8,128]{1,0:T(8,128)S(1)}, f32[8,128]{1,0:T(8,128)S(1)}, u32[]{:S(2)}, u32[]{:S(2)}) collective-permute-start(f32[8,128]{1,0:T(8,128)S(1)} %get-tuple-element.80), channel_id=1, source_target_pairs={{0,3},{1,2},{2,1},{3,0},{4,7},{5,6},{6,5},{7,4},{8,11},{9,10},{10,... | collective-permute-start | bytes 12296 | tf_op jit(solution)/shard_map/ppermute | solution.py:478
  6.3 2.0 %collective-permute-start = (f32[2,8,2,8,128]{4,3,2,1,0:T(8,128)S(1)}, f32[2,8,2,8,128]{4,3,2,1,0:T(8,128)S(1)}, u32[]{:S(2)}, u32[]{:S(2)}) collective-permute-start(f32[2,8,2,8,128]{4,3,2,1,0:T(8,128)S(1)} %maximum_bitcast_fusion), channel_id=1, source_target_pairs={{0,16},{16,0},{1,17},{17,1},{2,18},{18,2},{3,19},{19,3},{4,20},{20... | collective-permute-start | bytes 393224 | tf_op jit(solution)/shard_map/ppermute | solution.py:492
  8.3 1.9 %collective-permute-done.4 = f32[8,128]{1,0:T(8,128)S(1)} collective-permute-done((f32[8,128]{1,0:T(8,128)S(1)}, f32[8,128]{1,0:T(8,128)S(1)}, u32[]{:S(2)}, u32[]{:S(2)}) %collective-permute-start.4) | collective-permute-done | bytes 4128 | tf_op jit(solution)/shard_map/ppermute | solution.py:480
  10.3 1.9 %collective-permute-done = f32[2,8,2,8,128]{4,3,2,1,0:T(8,128)S(1)} collective-permute-done((f32[2,8,2,8,128]{4,3,2,1,0:T(8,128)S(1)}, f32[2,8,2,8,128]{4,3,2,1,0:T(8,128)S(1)}, u32[]{:S(2)}, u32[]{:S(2)}) %collective-permute-start) | collective-permute-done | bytes 131104 | tf_op jit(solution)/shard_map/ppermute | solution.py:492
  12.3 1.8 %collective-permute-start.5 = (f32[320,128]{1,0:T(8,128)S(1)}, f32[320,128]{1,0:T(8,128)S(1)}, u32[]{:S(2)}, u32[]{:S(2)}) collective-permute-start(f32[320,128]{1,0:T(8,128)S(1)} %get-tuple-element.21), channel_id=1, source_target_pairs={{0,4},{4,0},{8,12},{12,8},{1,5},{5,1},{9,13},{13,9},{2,6},{6,2},{1... | collective-permute-start | bytes 491528 | tf_op jit(solution)/shard_map/ppermute | solution.py:455
  14.1 1.4 %collective-permute-start.6 = (f32[320,128]{1,0:T(8,128)S(1)}, f32[320,128]{1,0:T(8,128)S(1)}, u32[]{:S(2)}, u32[]{:S(2)}) collective-permute-start(f32[320,128]{1,0:T(8,128)S(1)} %get-tuple-element.20), channel_id=1, source_target_pairs={{0,16},{4,8},{8,4},{12,28},{16,0},{20,24},{24,20},{28,12},{1,17},{... | collective-permute-start | bytes 491528 | tf_op jit(solution)/shard_map/ppermute | solution.py:464
  15.6 2.5 %collective-permute-done.5 = f32[320,128]{1,0:T(8,128)S(1)} collective-permute-done((f32[320,128]{1,0:T(8,128)S(1)}, f32[320,128]{1,0:T(8,128)S(1)}, u32[]{:S(2)}, u32[]{:S(2)}) %collective-permute-start.5) | collective-permute-done | bytes 163872 | tf_op jit(solution)/shard_map/ppermute | solution.py:455
  18.0 1.4 %collective-permute-done.6 = f32[320,128]{1,0:T(8,128)S(1)} collective-permute-done((f32[320,128]{1,0:T(8,128)S(1)}, f32[320,128]{1,0:T(8,128)S(1)}, u32[]{:S(2)}, u32[]{:S(2)}) %collective-permute-start.6) | collective-permute-done | bytes 163872 | tf_op jit(solution)/shard_map/ppermute | solution.py:464
  19.5 3.0 %shard_map.41 = (f32[18,3,32,128]{3,2,1,0:T(8,128)S(1)}, f32[18,3,16,128]{3,2,1,0:T(8,128)S(1)}, f32[18,3,16,128]{3,2,1,0:T(8,128)S(1)}, f32[8,2,16,128]{3,2,1,0...) custom-call(f32[2,8,2,16,128]{4,3,2,1,0:T(8,128)S(1)} %pad_maximum_f, ...), custom_call_target="tpu_custom_call" | custom-call | tf_op jit(solution)/shard_map/pallas_call | solution.py:552
  22.6 1.6 %collective-permute-start.8 = (f32[32,128]{1,0:T(8,128)S(1)}, f32[32,128]{1,0:T(8,128)S(1)}, u32[]{:S(2)}, u32[]{:S(2)}) collective-permute-start(f32[32,128]{1,0:T(8,128)S(1)} %get-tuple-element.68), channel_id=1, source_target_pairs={{0,3},{1,2},{2,1},{3,0},{4,7},{5,6},{6,5},{7,4},{8,11},{9,10},{10,... | collective-permute-start | bytes 49160 | tf_op jit(solution)/shard_map/ppermute | solution.py:464
  24.3 1.6 %collective-permute-done.8 = f32[32,128]{1,0:T(8,128)S(1)} collective-permute-done((f32[32,128]{1,0:T(8,128)S(1)}, f32[32,128]{1,0:T(8,128)S(1)}, u32[]{:S(2)}, u32[]{:S(2)}) %collective-permute-start.8) | collective-permute-done | bytes 16416 | tf_op jit(solution)/shard_map/ppermute | solution.py:464
  25.9 1.2 %collective-permute-start.9 = (f32[240,128]{1,0:T(8,128)S(1)}, f32[240,128]{1,0:T(8,128)S(1)}, u32[]{:S(2)}, u32[]{:S(2)}) collective-permute-start(f32[240,128]{1,0:T(8,128)S(1)} %pad_maximum_fusion.3), channel_id=1, source_target_pairs={{0,4},{4,0},{8,12},{12,8},{1,5},{5,1},{9,13},{13,9},{2,6},{6,2},{1... | collective-permute-start | bytes 368648 | tf_op jit(solution)/shard_map/ppermute | solution.py:516
  27.2 1.9 %collective-permute-start.10 = (f32[96,128]{1,0:T(8,128)S(1)}, f32[96,128]{1,0:T(8,128)S(1)}, u32[]{:S(2)}, u32[]{:S(2)}) collective-permute-start(f32[96,128]{1,0:T(8,128)S(1)} %pad_maximum_fusion.6), channel_id=1, source_target_pairs={{0,8},{4,12},{8,0},{12,4},{1,9},{5,13},{9,1},{13,5},{2,10},{6,14},... | collective-permute-start | bytes 147464 | tf_op jit(solution)/shard_map/ppermute | solution.py:516
  29.0 1.3 %collective-permute-start.11 = (f32[96,128]{1,0:T(8,128)S(1)}, f32[96,128]{1,0:T(8,128)S(1)}, u32[]{:S(2)}, u32[]{:S(2)}) collective-permute-start(f32[96,128]{1,0:T(8,128)S(1)} %pad_maximum_fusion.6), channel_id=1, source_target_pairs={{0,12},{4,8},{8,4},{12,0},{1,13},{5,9},{9,5},{13,1},{2,14},{6,10},... | collective-permute-start | bytes 147464 | tf_op jit(solution)/shard_map/ppermute | solution.py:516
  30.4 1.4 %collective-permute-start.12 = (f32[144,128]{1,0:T(8,128)S(1)}, f32[144,128]{1,0:T(8,128)S(1)}, u32[]{:S(2)}, u32[]{:S(2)}) collective-permute-start(f32[144,128]{1,0:T(8,128)S(1)} %get-tuple-element.30), channel_id=1, source_target_pairs={{0,16},{4,8},{8,4},{12,28},{16,0},{20,24},{24,20},{28,12},{1,17},{... | collective-permute-start | bytes 221192 | tf_op jit(solution)/shard_map/ppermute | solution.py:518
  31.8 0.3 collective-permute-done.10
  32.2 3.7 %collective-permute-done.11 = f32[96,128]{1,0:T(8,128)S(1)} collective-permute-done((f32[96,128]{1,0:T(8,128)S(1)}, f32[96,128]{1,0:T(8,128)S(1)}, u32[]{:S(2)}, u32[]{:S(2)}) %collective-permute-start.11) | collective-permute-done | bytes 49184 | tf_op jit(solution)/shard_map/ppermute | solution.py:516
  36.0 6.6 %shard_map.42 = (f32[8,8,256]{2,1,0:T(8,128)}, f32[8,8,256]{2,1,0:T(8,128)}) custom-call(f32[2,4,8,128]{3,2,1,0:T(8,128)S(1)} %bitcast.111, f32[2,4,8,128]{3,2,1,0:T(8,128)S(1)} %bitcast.117, f32[2,4,8,128]{3,2,1,0:T(8,128)S(1)} %bitcast.115, f32[2,4,8,128]{3,2,1,0:T(8,128)S(1)} %bitcast.116, f32[2,2,8,128]{3,2,1,0:T(8,128)S(1)} %pad_maximum_fusion.9.refs_4_, ...), custom_call_target="tpu_custom_call" | custom-call | tf_op jit(solution)/shard_map/pallas_call | solution.py:552
  (49 shorter events, 0.5 us)
Async XLA Ops:
  0.6 0.9 %copy-start = (f32[8,8,256]{2,1,0:T(8,128)S(1)}, f32[8,8,256]{2,1,0:T(8,128)}, u32[]{:S(2)}) copy-start(f32[8,8,256]{2,1,0:T(8,128)} %param.3) | copy-start | bytes 196612
  2.0 6.4 %collective-permute-start.1 = (f32[8,128]{1,0:T(8,128)S(1)}, f32[8,128]{1,0:T(8,128)S(1)}, u32[]{:S(2)}, u32[]{:S(2)}) collective-permute-start(f32[8,128]{1,0:T(8,128)S(1)} %get-tuple-element.79), channel_id=1, source_target_pairs={{0,1},{1,0},{2,3},{3,2},{4,5},{5,4},{6,7},{7,6},{8,9},{9,8},{10,11... | collective-permute-start | bytes 12296 | tf_op jit(solution)/shard_map/ppermute | solution.py:478
  2.5 5.8 %collective-permute-start.2 = (f32[8,128]{1,0:T(8,128)S(1)}, f32[8,128]{1,0:T(8,128)S(1)}, u32[]{:S(2)}, u32[]{:S(2)}) collective-permute-start(f32[8,128]{1,0:T(8,128)S(1)} %get-tuple-element.79), channel_id=1, source_target_pairs={{0,17},{1,16},{2,19},{3,18},{16,1},{17,0},{18,3},{19,2},{4,21},{5,... | collective-permute-start | bytes 12296 | tf_op jit(solution)/shard_map/ppermute | solution.py:480
  5.1 3.2 %collective-permute-start.3 = (f32[8,128]{1,0:T(8,128)S(1)}, f32[8,128]{1,0:T(8,128)S(1)}, u32[]{:S(2)}, u32[]{:S(2)}) collective-permute-start(f32[8,128]{1,0:T(8,128)S(1)} %get-tuple-element.80), channel_id=1, source_target_pairs={{0,3},{1,2},{2,1},{3,0},{4,7},{5,6},{6,5},{7,4},{8,11},{9,10},{10,... | collective-permute-start | bytes 12296 | tf_op jit(solution)/shard_map/ppermute | solution.py:478
  6.3 3.9 %collective-permute-start.4 = (f32[8,128]{1,0:T(8,128)S(1)}, f32[8,128]{1,0:T(8,128)S(1)}, u32[]{:S(2)}, u32[]{:S(2)}) collective-permute-start(f32[8,128]{1,0:T(8,128)S(1)} %get-tuple-element.80), channel_id=1, source_target_pairs={{0,19},{1,18},{2,17},{3,16},{16,3},{17,2},{18,1},{19,0},{4,23},{5,... | collective-permute-start | bytes 12296 | tf_op jit(solution)/shard_map/ppermute | solution.py:480
  6.3 5.9 %collective-permute-start = (f32[2,8,2,8,128]{4,3,2,1,0:T(8,128)S(1)}, f32[2,8,2,8,128]{4,3,2,1,0:T(8,128)S(1)}, u32[]{:S(2)}, u32[]{:S(2)}) collective-permute-start(f32[2,8,2,8,128]{4,3,2,1,0:T(8,128)S(1)} %maximum_bitcast_fusion), channel_id=1, source_target_pairs={{0,16},{16,0},{1,17},{17,1},{2,18},{18,2},{3,19},{19,3},{4,20},{20... | collective-permute-start | bytes 393224 | tf_op jit(solution)/shard_map/ppermute | solution.py:492
  12.3 5.7 %collective-permute-start.5 = (f32[320,128]{1,0:T(8,128)S(1)}, f32[320,128]{1,0:T(8,128)S(1)}, u32[]{:S(2)}, u32[]{:S(2)}) collective-permute-start(f32[320,128]{1,0:T(8,128)S(1)} %get-tuple-element.21), channel_id=1, source_target_pairs={{0,4},{4,0},{8,12},{12,8},{1,5},{5,1},{9,13},{13,9},{2,6},{6,2},{1... | collective-permute-start | bytes 491528 | tf_op jit(solution)/shard_map/ppermute | solution.py:455
  14.1 5.3 %collective-permute-start.6 = (f32[320,128]{1,0:T(8,128)S(1)}, f32[320,128]{1,0:T(8,128)S(1)}, u32[]{:S(2)}, u32[]{:S(2)}) collective-permute-start(f32[320,128]{1,0:T(8,128)S(1)} %get-tuple-element.20), channel_id=1, source_target_pairs={{0,16},{4,8},{8,4},{12,28},{16,0},{20,24},{24,20},{28,12},{1,17},{... | collective-permute-start | bytes 491528 | tf_op jit(solution)/shard_map/ppermute | solution.py:464
  22.5 1.7 %collective-permute-start.7 = (f32[32,128]{1,0:T(8,128)S(1)}, f32[32,128]{1,0:T(8,128)S(1)}, u32[]{:S(2)}, u32[]{:S(2)}) collective-permute-start(f32[32,128]{1,0:T(8,128)S(1)} %get-tuple-element.69), channel_id=1, source_target_pairs={{0,1},{1,0},{2,3},{3,2},{4,5},{5,4},{6,7},{7,6},{8,9},{9,8},{10,11... | collective-permute-start | bytes 49160 | tf_op jit(solution)/shard_map/ppermute | solution.py:455
  22.6 3.2 %collective-permute-start.8 = (f32[32,128]{1,0:T(8,128)S(1)}, f32[32,128]{1,0:T(8,128)S(1)}, u32[]{:S(2)}, u32[]{:S(2)}) collective-permute-start(f32[32,128]{1,0:T(8,128)S(1)} %get-tuple-element.68), channel_id=1, source_target_pairs={{0,3},{1,2},{2,1},{3,0},{4,7},{5,6},{6,5},{7,4},{8,11},{9,10},{10,... | collective-permute-start | bytes 49160 | tf_op jit(solution)/shard_map/ppermute | solution.py:464
  25.9 10.0 %collective-permute-start.9 = (f32[240,128]{1,0:T(8,128)S(1)}, f32[240,128]{1,0:T(8,128)S(1)}, u32[]{:S(2)}, u32[]{:S(2)}) collective-permute-start(f32[240,128]{1,0:T(8,128)S(1)} %pad_maximum_fusion.3), channel_id=1, source_target_pairs={{0,4},{4,0},{8,12},{12,8},{1,5},{5,1},{9,13},{13,9},{2,6},{6,2},{1... | collective-permute-start | bytes 368648 | tf_op jit(solution)/shard_map/ppermute | solution.py:516
  27.2 5.0 %collective-permute-start.10 = (f32[96,128]{1,0:T(8,128)S(1)}, f32[96,128]{1,0:T(8,128)S(1)}, u32[]{:S(2)}, u32[]{:S(2)}) collective-permute-start(f32[96,128]{1,0:T(8,128)S(1)} %pad_maximum_fusion.6), channel_id=1, source_target_pairs={{0,8},{4,12},{8,0},{12,4},{1,9},{5,13},{9,1},{13,5},{2,10},{6,14},... | collective-permute-start | bytes 147464 | tf_op jit(solution)/shard_map/ppermute | solution.py:516
  29.0 6.8 %collective-permute-start.11 = (f32[96,128]{1,0:T(8,128)S(1)}, f32[96,128]{1,0:T(8,128)S(1)}, u32[]{:S(2)}, u32[]{:S(2)}) collective-permute-start(f32[96,128]{1,0:T(8,128)S(1)} %pad_maximum_fusion.6), channel_id=1, source_target_pairs={{0,12},{4,8},{8,4},{12,0},{1,13},{5,9},{9,5},{13,1},{2,14},{6,10},... | collective-permute-start | bytes 147464 | tf_op jit(solution)/shard_map/ppermute | solution.py:516
  30.4 5.5 %collective-permute-start.12 = (f32[144,128]{1,0:T(8,128)S(1)}, f32[144,128]{1,0:T(8,128)S(1)}, u32[]{:S(2)}, u32[]{:S(2)}) collective-permute-start(f32[144,128]{1,0:T(8,128)S(1)} %get-tuple-element.30), channel_id=1, source_target_pairs={{0,16},{4,8},{8,4},{12,28},{16,0},{20,24},{24,20},{28,12},{1,17},{... | collective-permute-start | bytes 221192 | tf_op jit(solution)/shard_map/ppermute | solution.py:518

commit v7 on v6

--- a/solution.py
+++ b/solution.py
@@ -302,18 +302,17 @@
     return [me] + [lax.rem(me - step + count, count) for step in range(1, count)]
 
 
-def after_kernel(*refs, count):
+def coarse_kernel(*refs, count):
     blocks, zblocks = refs[:count], refs[count : 2 * count]
     refs = refs[2 * count :]
-    (kap, diag, inv, xpre, rown, zown, rlo, zlo, rhi, zhi, sol, resid) = refs[:12]
-    (k1, d1, i1, r1, x1, va1, wa1, vb1, wb1, k2, d2, i2, r2, x2, va2, wa2, vb2, wb2, flat, va, wa, vb, wb, res, acc) = refs[12:]
-    me_x, me_y, me_z = (lax.axis_index(a) for a in ("gx", "gy", "gz"))
+    window = refs[0]
+    (k1, d1, i1, r1, x1, va1, wa1, vb1, wb1, k2, d2, i2, r2, x2, va2, wa2, vb2, wb2, flat) = refs[1:]
+    me_y, me_z = lax.axis_index("gy"), lax.axis_index("gz")
     has_left, has_right = me_z > 0, me_z < lax.axis_size("gz") - 1
     sources = sources_of(me_y, count)
-    zero_pads((k1, va1, wa1, vb1, wb1, k2, va2, wa2, vb2, wb2, va, wa, vb, wb))
+    zero_pads((k1, va1, wa1, vb1, wb1, k2, va2, wa2, vb2, wb2))
     each = blocks[0].shape[1]
     xc = blocks[0].shape[2]
-    tiles = xpre.shape[1]
     yc = each * count
     lo1, hi1 = COARSE_PAD, COARSE_PAD + yc
     edge = [lo1 - 1, hi1]
@@ -337,7 +336,6 @@
         smoothing_step(k1, d1, i1, r1, old, new, x1, lo1, hi1, pair)
         old, new = new, old
     residual_only(k1, d1, r1, old[0], old[1], lo1, hi1)
-    tiles1 = k1.shape[1]
     y2 = yc // 2
     half = xc // 2
     for target, source, offset, factor in ((k2, k1, PAD, 0.25), (r2, r1, 0, 1.0)):
@@ -381,14 +379,22 @@
     for pair in weights:
         smoothing_step(k1, d1, i1, r1, old, new, x1, lo1, hi1, pair)
         old, new = new, old
-    rows = rown.shape[0]
+    wide_rows = window.shape[0]
+    start = COARSE_PAD - (HALO + 1) // 2 + each * me_y
+    for y in range(wide_rows):
+        window[y] = x1[start + y]
+
+
+def after_kernel(window, kap, diag, inv, xpre, rown, zown, rlo, zlo, rhi, zhi, sol, resid, flat, va, wa, vb, wb, res, acc):
+    me_x = lax.axis_index("gx")
+    zero_pads((va, wa, vb, wb))
+    rows, tiles, x_count, _ = rown.shape
     last = HALO + rows
-    x_count = rown.shape[2]
-    wide_rows = (rows + 2 * HALO) // 2 + 1
-    start = COARSE_PAD - (HALO + 1) // 2 + each * me_y
+    wide_rows, tiles1, xc, _ = window.shape
+    centre, weights = chebyshev_coefs(DEGREE, smooth_low)
     for t in range(tiles1):
         for y in range(wide_rows):
-            value = x1[start + y, t]
+            value = window[y, t]
             base = (t * wide_rows + y) * x_count
             flat[pl.ds(base, xc, stride=2), :] = value
             flat[pl.ds(base + 1, xc, stride=2), :] = value
@@ -512,11 +518,10 @@
             pairs = [(x * 4 + i, x * 4 + 3 - i) for x in range(nx) for i in range(4)]
         got = []
         for step in (1, 2, 3):
-            payload = jnp.concatenate([block, near], axis=0) if step == 1 else block
-            got.append(lax.ppermute(payload, "gy", [(i, i ^ step) for i in range(count)]))
+            got.append(lax.ppermute(block, "gy", [(i, i ^ step) for i in range(count)]))
             blocks.append(got[-1][:size])
         far = lax.ppermute(far, ("gx", "gy"), pairs)
-        near = got[0][size:]
+        near = lax.ppermute(near, "gy", [(i, i ^ 1) for i in range(count)])
         low, high = jnp.where(odd, near, far), jnp.where(odd, far, near)
     else:
         for step in range(1, count):
@@ -633,20 +638,24 @@
     x2 = max(xc // 2, 8)
     wide2 = (y2 + 2, 1, x2 + 2 * PAD, LANES)
     plain2 = (y2 + 2, 1, x2, LANES)
-    flat_rows = max(y2 * xc, tiles1 * (ext // 2 + 1) * x_count)
-
+    wide_rows = ext // 2 + 1
 
     def kernel(*refs):
-        after_kernel(*refs, count=len(blocks))
-
-    sol, resid = call(
+        coarse_kernel(*refs, count=len(blocks))
+
+    (window,) = call(
         kernel,
-        [shape(bx, by, bz), shape(bx, by, bz)],
+        [shape(wide_rows, tiles1, xc, LANES)],
         [vmem(wide1)] + [vmem(plain1)] * 4 + [vmem(wide1)] * 4
         + [vmem(wide2)] + [vmem(plain2)] * 4 + [vmem(wide2)] * 4
-        + [vmem((flat_rows, LANES))] + [vmem(wide)] * 4 + [vmem(plain)] * 2,
-        blocks + zblocks
-        + [kap, diag, inv, xpre, rpre, fine_z, rlo, zrlo, rhi, zrhi],
+        + [vmem((y2 * xc, LANES))],
+        blocks + zblocks,
+    )
+    sol, resid = call(
+        after_kernel,
+        [shape(bx, by, bz), shape(bx, by, bz)],
+        [vmem((tiles1 * wide_rows * x_count, LANES))] + [vmem(wide)] * 4 + [vmem(plain)] * 2,
+        [window, kap, diag, inv, xpre, rpre, fine_z, rlo, zrlo, rhi, zrhi],
     )
     return sol, resid
 

time: 42.7 us -> 42.1 us (0.986)
  waiting for transfers between devices: 13.3 us -> 12.3 us
    ppermute x3 -> x4, waiting for transfers between devices: 4.04 us -> 3.07 us  [the longest x3 3.07 us: gather_second(): got.append(lax.ppermute(block, 'gy', [(i, i ^ step) for i in range(count)]))]
    ppermute x3 -> x4, starting transfers between devices: 4.45 us -> 4.8 us  [the longest x3 4.45 us: gather_second(): got.append(lax.ppermute(block, 'gy', [(i, i ^ step) for i in range(count)]))]
    pallas_call x2 -> x3, Pallas kernels: 9.58 us -> 9.69 us  [call(): pl.pallas_call(kernel, out_shape=out_shapes, in_specs=[whole] * len(input...]
  transfers between devices with their start and end apart: 13 -> 14, of which waited for: 7 -> 7; matrix products, arithmetic and copies ran while one was open for 0% -> 0% of each run, Pallas kernels for 0% -> 7%
where the time goes in v7:
time: 42.1 us; the launch traced here: 42 us
  starting transfers between devices  17.5 us (42%)
  waiting for transfers between devices  12.3 us (29%)
  Pallas kernels  9.69 us (23%)
  local copies, waits for them, and re-layouts  1.33 us (3%)
  between operations  0.9 us (2%)
    pallas_call x3, Pallas kernels, call(): pl.pallas_call(kernel, out_shape=out_shapes, in_specs=[whole] * len(input...  9.69 us
    ppermute x3, starting transfers between devices, gather_second(): got.append(lax.ppermute(block, 'gy', [(i, i ^ step) for i in range(count)]))  4.45 us
    ppermute x2, starting transfers between devices, exchange(): two = lax.ppermute(jnp.where(odd, to_high, to_low), names, pairs)  3.07 us
    ppermute x3, waiting for transfers between devices, gather_second(): got.append(lax.ppermute(block, 'gy', [(i, i ^ step) for i in range(count)]))  3.07 us
    ppermute x2, waiting for transfers between devices, exchange(): two = lax.ppermute(jnp.where(odd, to_high, to_low), names, pairs)  2.98 us
    ppermute x2, starting transfers between devices, exchange_and_gather(): cross = lax.ppermute(payload, ('gx', 'gz'), pairs)  2.61 us
    ppermute x2, waiting for transfers between devices, exchange(): lax.ppermute(jnp.where(odd, to_low, to_high), axis, [(i, i ^ 1) for i in...  2.45 us
    ppermute x1, starting transfers between devices, gather_first(): other = lax.ppermute(values, axis, [(0, 1), (1, 0)])  1.98 us
  transfers between devices with their start and end apart: 14, of which 7 were waited for; matrix products, arithmetic and copies ran while one was open for 0% of the time, Pallas kernels for 7%

profile of v7, /device:TPU:0, one launch (start us, length us, event | category | flops | bytes accessed | tf_op | source)
XLA Modules:
  0.0 42.0 jit_solution(5282953638255633329)
XLA Ops:
  0.6 0.9 %copy.4 = f32[1,8,8,2,128]{4,1,3,2,0:T(8,128)S(1)} copy(f32[1,8,8,2,128]{4,2,3,1,0:T(8,128)} %bitcast.129) | data formatting | bytes 131072 | tf_op jit(solution)/shard_map/stack | solution.py:580
  1.8 0.1 concatenate.70
  2.0 0.6 %collective-permute-start.1 = (f32[8,128]{1,0:T(8,128)S(1)}, f32[8,128]{1,0:T(8,128)S(1)}, u32[]{:S(2)}, u32[]{:S(2)}) collective-permute-start(f32[8,128]{1,0:T(8,128)S(1)} %get-tuple-element.79), channel_id=1, source_target_pairs={{0,1},{1,0},{2,3},{3,2},{4,5},{5,4},{6,7},{7,6},{8,9},{9,8},{10,11... | collective-permute-start | bytes 12296 | tf_op jit(solution)/shard_map/ppermute | solution.py:484
  2.5 2.6 %collective-permute-start.2 = (f32[8,128]{1,0:T(8,128)S(1)}, f32[8,128]{1,0:T(8,128)S(1)}, u32[]{:S(2)}, u32[]{:S(2)}) collective-permute-start(f32[8,128]{1,0:T(8,128)S(1)} %get-tuple-element.79), channel_id=1, source_target_pairs={{0,17},{1,16},{2,19},{3,18},{16,1},{17,0},{18,3},{19,2},{4,21},{5,... | collective-permute-start | bytes 12296 | tf_op jit(solution)/shard_map/ppermute | solution.py:486
  5.1 1.2 %collective-permute-start.3 = (f32[8,128]{1,0:T(8,128)S(1)}, f32[8,128]{1,0:T(8,128)S(1)}, u32[]{:S(2)}, u32[]{:S(2)}) collective-permute-start(f32[8,128]{1,0:T(8,128)S(1)} %get-tuple-element.80), channel_id=1, source_target_pairs={{0,3},{1,2},{2,1},{3,0},{4,7},{5,6},{6,5},{7,4},{8,11},{9,10},{10,... | collective-permute-start | bytes 12296 | tf_op jit(solution)/shard_map/ppermute | solution.py:484
  6.3 2.0 %collective-permute-start = (f32[2,8,2,8,128]{4,3,2,1,0:T(8,128)S(1)}, f32[2,8,2,8,128]{4,3,2,1,0:T(8,128)S(1)}, u32[]{:S(2)}, u32[]{:S(2)}) collective-permute-start(f32[2,8,2,8,128]{4,3,2,1,0:T(8,128)S(1)} %maximum_bitcast_fusion), channel_id=1, source_target_pairs={{0,16},{16,0},{1,17},{17,1},{2,18},{18,2},{3,19},{19,3},{4,20},{20... | collective-permute-start | bytes 393224 | tf_op jit(solution)/shard_map/ppermute | solution.py:498
  8.3 1.9 %collective-permute-done.4 = f32[8,128]{1,0:T(8,128)S(1)} collective-permute-done((f32[8,128]{1,0:T(8,128)S(1)}, f32[8,128]{1,0:T(8,128)S(1)}, u32[]{:S(2)}, u32[]{:S(2)}) %collective-permute-start.4) | collective-permute-done | bytes 4128 | tf_op jit(solution)/shard_map/ppermute | solution.py:486
  10.3 1.9 %collective-permute-done = f32[2,8,2,8,128]{4,3,2,1,0:T(8,128)S(1)} collective-permute-done((f32[2,8,2,8,128]{4,3,2,1,0:T(8,128)S(1)}, f32[2,8,2,8,128]{4,3,2,1,0:T(8,128)S(1)}, u32[]{:S(2)}, u32[]{:S(2)}) %collective-permute-start) | collective-permute-done | bytes 131104 | tf_op jit(solution)/shard_map/ppermute | solution.py:498
  12.3 1.8 %collective-permute-start.5 = (f32[320,128]{1,0:T(8,128)S(1)}, f32[320,128]{1,0:T(8,128)S(1)}, u32[]{:S(2)}, u32[]{:S(2)}) collective-permute-start(f32[320,128]{1,0:T(8,128)S(1)} %get-tuple-element.21), channel_id=1, source_target_pairs={{0,4},{4,0},{8,12},{12,8},{1,5},{5,1},{9,13},{13,9},{2,6},{6,2},{1... | collective-permute-start | bytes 491528 | tf_op jit(solution)/shard_map/ppermute | solution.py:461
  14.1 1.4 %collective-permute-start.6 = (f32[320,128]{1,0:T(8,128)S(1)}, f32[320,128]{1,0:T(8,128)S(1)}, u32[]{:S(2)}, u32[]{:S(2)}) collective-permute-start(f32[320,128]{1,0:T(8,128)S(1)} %get-tuple-element.20), channel_id=1, source_target_pairs={{0,16},{4,8},{8,4},{12,28},{16,0},{20,24},{24,20},{28,12},{1,17},{... | collective-permute-start | bytes 491528 | tf_op jit(solution)/shard_map/ppermute | solution.py:470
  15.6 2.5 %collective-permute-done.5 = f32[320,128]{1,0:T(8,128)S(1)} collective-permute-done((f32[320,128]{1,0:T(8,128)S(1)}, f32[320,128]{1,0:T(8,128)S(1)}, u32[]{:S(2)}, u32[]{:S(2)}) %collective-permute-start.5) | collective-permute-done | bytes 163872 | tf_op jit(solution)/shard_map/ppermute | solution.py:461
  18.0 1.4 %collective-permute-done.6 = f32[320,128]{1,0:T(8,128)S(1)} collective-permute-done((f32[320,128]{1,0:T(8,128)S(1)}, f32[320,128]{1,0:T(8,128)S(1)}, u32[]{:S(2)}, u32[]{:S(2)}) %collective-permute-start.6) | collective-permute-done | bytes 163872 | tf_op jit(solution)/shard_map/ppermute | solution.py:470
  19.5 3.0 %shard_map.41 = (f32[18,3,32,128]{3,2,1,0:T(8,128)S(1)}, f32[18,3,16,128]{3,2,1,0:T(8,128)S(1)}, f32[18,3,16,128]{3,2,1,0:T(8,128)S(1)}, f32[8,2,16,128]{3,2,1,0...) custom-call(f32[2,8,2,16,128]{4,3,2,1,0:T(8,128)S(1)} %pad_maximum_f, ...), custom_call_target="tpu_custom_call" | custom-call | tf_op jit(solution)/shard_map/pallas_call | solution.py:557
  22.6 1.6 %collective-permute-start.8 = (f32[32,128]{1,0:T(8,128)S(1)}, f32[32,128]{1,0:T(8,128)S(1)}, u32[]{:S(2)}, u32[]{:S(2)}) collective-permute-start(f32[32,128]{1,0:T(8,128)S(1)} %get-tuple-element.69), channel_id=1, source_target_pairs={{0,3},{1,2},{2,1},{3,0},{4,7},{5,6},{6,5},{7,4},{8,11},{9,10},{10,... | collective-permute-start | bytes 49160 | tf_op jit(solution)/shard_map/ppermute | solution.py:470
  24.3 1.6 %collective-permute-done.8 = f32[32,128]{1,0:T(8,128)S(1)} collective-permute-done((f32[32,128]{1,0:T(8,128)S(1)}, f32[32,128]{1,0:T(8,128)S(1)}, u32[]{:S(2)}, u32[]{:S(2)}) %collective-permute-start.8) | collective-permute-done | bytes 16416 | tf_op jit(solution)/shard_map/ppermute | solution.py:470
  25.9 1.2 %collective-permute-start.9 = (f32[96,128]{1,0:T(8,128)S(1)}, f32[96,128]{1,0:T(8,128)S(1)}, u32[]{:S(2)}, u32[]{:S(2)}) collective-permute-start(f32[96,128]{1,0:T(8,128)S(1)} %pad_maximum_fusion.5), channel_id=1, source_target_pairs={{0,4},{4,0},{8,12},{12,8},{1,5},{5,1},{9,13},{13,9},{2,6},{6,2},{1... | collective-permute-start | bytes 147464 | tf_op jit(solution)/shard_map/ppermute | solution.py:521
  27.1 1.9 %collective-permute-start.10 = (f32[96,128]{1,0:T(8,128)S(1)}, f32[96,128]{1,0:T(8,128)S(1)}, u32[]{:S(2)}, u32[]{:S(2)}) collective-permute-start(f32[96,128]{1,0:T(8,128)S(1)} %pad_maximum_fusion.5), channel_id=1, source_target_pairs={{0,8},{4,12},{8,0},{12,4},{1,9},{5,13},{9,1},{13,5},{2,10},{6,14},... | collective-permute-start | bytes 147464 | tf_op jit(solution)/shard_map/ppermute | solution.py:521
  29.0 1.3 %collective-permute-start.11 = (f32[96,128]{1,0:T(8,128)S(1)}, f32[96,128]{1,0:T(8,128)S(1)}, u32[]{:S(2)}, u32[]{:S(2)}) collective-permute-start(f32[96,128]{1,0:T(8,128)S(1)} %pad_maximum_fusion.5), channel_id=1, source_target_pairs={{0,12},{4,8},{8,4},{12,0},{1,13},{5,9},{9,5},{13,1},{2,14},{6,10},... | collective-permute-start | bytes 147464 | tf_op jit(solution)/shard_map/ppermute | solution.py:521
  30.4 0.3 collective-permute-start.12
  30.7 1.4 %collective-permute-start.13 = (f32[144,128]{1,0:T(8,128)S(1)}, f32[144,128]{1,0:T(8,128)S(1)}, u32[]{:S(2)}, u32[]{:S(2)}) collective-permute-start(f32[144,128]{1,0:T(8,128)S(1)} %get-tuple-element.30), channel_id=1, source_target_pairs={{0,16},{4,8},{8,4},{12,28},{16,0},{20,24},{24,20},{28,12},{1,17},{... | collective-permute-start | bytes 221192 | tf_op jit(solution)/shard_map/ppermute | solution.py:523
  32.1 1.1 %collective-permute-done.10 = f32[96,128]{1,0:T(8,128)S(1)} collective-permute-done((f32[96,128]{1,0:T(8,128)S(1)}, f32[96,128]{1,0:T(8,128)S(1)}, u32[]{:S(2)}, u32[]{:S(2)}) %collective-permute-start.10) | collective-permute-done | bytes 49184 | tf_op jit(solution)/shard_map/ppermute | solution.py:521
  33.2 2.0 %collective-permute-done.11 = f32[96,128]{1,0:T(8,128)S(1)} collective-permute-done((f32[96,128]{1,0:T(8,128)S(1)}, f32[96,128]{1,0:T(8,128)S(1)}, u32[]{:S(2)}, u32[]{:S(2)}) %collective-permute-start.11) | collective-permute-done | bytes 49184 | tf_op jit(solution)/shard_map/ppermute | solution.py:521
  35.2 3.1 %shard_map.42.window = f32[10,2,8,128]{3,2,1,0:T(8,128)S(1)} custom-call(f32[2,4,8,128]{3,2,1,0:T(8,128)S(1)} %bitcast.114, f32[2,4,8,128]{3,2,1,0:T(8,128)S(1)} %bitcast.115, f32[2,4,8,128]{3,2,1,0:T(8,128)S(1)} %bitcast.116, f32[2,4,8,128]{3,2,1,0:T(8,128)S(1)} %bitcast.117, f32[2,2,8,128]{3,2,1,0:T(8,128)S(1)} %pad_maximum_fusion.8.refs_4_, ...), custom_call_target="tpu_custom_call" | custom-call | tf_op jit(solution)/shard_map/pallas_call | solution.py:557
  38.4 3.6 %shard_map.43 = (f32[8,8,256]{2,1,0:T(8,128)}, f32[8,8,256]{2,1,0:T(8,128)}) custom-call(f32[10,2,8,128]{3,2,1,0:T(8,128)S(1)} %shard_map.42.window, f32[18,3,32,128]{3,2,1,0:T(8,128)S(1)} %get-tuple-element.13.kap, f32[18,3,16,128]{3,2,1,0:T(8,128)S(1)} %get-tuple-element.14.diag, f32[18,3,16,128]{3,2,1,0:T(8,128)S(1)} %get-tuple-element.15.inv, ...), custom_call_target="tpu_custom_call" | custom-call | tf_op jit(solution)/shard_map/pallas_call | solution.py:557
  (51 shorter events, 0.7 us)
Async XLA Ops:
  0.6 0.9 %copy-start = (f32[8,8,256]{2,1,0:T(8,128)S(1)}, f32[8,8,256]{2,1,0:T(8,128)}, u32[]{:S(2)}) copy-start(f32[8,8,256]{2,1,0:T(8,128)} %param.3) | copy-start | bytes 196612
  2.0 6.4 %collective-permute-start.1 = (f32[8,128]{1,0:T(8,128)S(1)}, f32[8,128]{1,0:T(8,128)S(1)}, u32[]{:S(2)}, u32[]{:S(2)}) collective-permute-start(f32[8,128]{1,0:T(8,128)S(1)} %get-tuple-element.79), channel_id=1, source_target_pairs={{0,1},{1,0},{2,3},{3,2},{4,5},{5,4},{6,7},{7,6},{8,9},{9,8},{10,11... | collective-permute-start | bytes 12296 | tf_op jit(solution)/shard_map/ppermute | solution.py:484
  2.5 5.8 %collective-permute-start.2 = (f32[8,128]{1,0:T(8,128)S(1)}, f32[8,128]{1,0:T(8,128)S(1)}, u32[]{:S(2)}, u32[]{:S(2)}) collective-permute-start(f32[8,128]{1,0:T(8,128)S(1)} %get-tuple-element.79), channel_id=1, source_target_pairs={{0,17},{1,16},{2,19},{3,18},{16,1},{17,0},{18,3},{19,2},{4,21},{5,... | collective-permute-start | bytes 12296 | tf_op jit(solution)/shard_map/ppermute | solution.py:486
  5.1 3.2 %collective-permute-start.3 = (f32[8,128]{1,0:T(8,128)S(1)}, f32[8,128]{1,0:T(8,128)S(1)}, u32[]{:S(2)}, u32[]{:S(2)}) collective-permute-start(f32[8,128]{1,0:T(8,128)S(1)} %get-tuple-element.80), channel_id=1, source_target_pairs={{0,3},{1,2},{2,1},{3,0},{4,7},{5,6},{6,5},{7,4},{8,11},{9,10},{10,... | collective-permute-start | bytes 12296 | tf_op jit(solution)/shard_map/ppermute | solution.py:484
  6.3 3.9 %collective-permute-start.4 = (f32[8,128]{1,0:T(8,128)S(1)}, f32[8,128]{1,0:T(8,128)S(1)}, u32[]{:S(2)}, u32[]{:S(2)}) collective-permute-start(f32[8,128]{1,0:T(8,128)S(1)} %get-tuple-element.80), channel_id=1, source_target_pairs={{0,19},{1,18},{2,17},{3,16},{16,3},{17,2},{18,1},{19,0},{4,23},{5,... | collective-permute-start | bytes 12296 | tf_op jit(solution)/shard_map/ppermute | solution.py:486
  6.3 5.9 %collective-permute-start = (f32[2,8,2,8,128]{4,3,2,1,0:T(8,128)S(1)}, f32[2,8,2,8,128]{4,3,2,1,0:T(8,128)S(1)}, u32[]{:S(2)}, u32[]{:S(2)}) collective-permute-start(f32[2,8,2,8,128]{4,3,2,1,0:T(8,128)S(1)} %maximum_bitcast_fusion), channel_id=1, source_target_pairs={{0,16},{16,0},{1,17},{17,1},{2,18},{18,2},{3,19},{19,3},{4,20},{20... | collective-permute-start | bytes 393224 | tf_op jit(solution)/shard_map/ppermute | solution.py:498
  12.3 5.7 %collective-permute-start.5 = (f32[320,128]{1,0:T(8,128)S(1)}, f32[320,128]{1,0:T(8,128)S(1)}, u32[]{:S(2)}, u32[]{:S(2)}) collective-permute-start(f32[320,128]{1,0:T(8,128)S(1)} %get-tuple-element.21), channel_id=1, source_target_pairs={{0,4},{4,0},{8,12},{12,8},{1,5},{5,1},{9,13},{13,9},{2,6},{6,2},{1... | collective-permute-start | bytes 491528 | tf_op jit(solution)/shard_map/ppermute | solution.py:461
  14.1 5.3 %collective-permute-start.6 = (f32[320,128]{1,0:T(8,128)S(1)}, f32[320,128]{1,0:T(8,128)S(1)}, u32[]{:S(2)}, u32[]{:S(2)}) collective-permute-start(f32[320,128]{1,0:T(8,128)S(1)} %get-tuple-element.20), channel_id=1, source_target_pairs={{0,16},{4,8},{8,4},{12,28},{16,0},{20,24},{24,20},{28,12},{1,17},{... | collective-permute-start | bytes 491528 | tf_op jit(solution)/shard_map/ppermute | solution.py:470
  22.5 1.7 %collective-permute-start.7 = (f32[32,128]{1,0:T(8,128)S(1)}, f32[32,128]{1,0:T(8,128)S(1)}, u32[]{:S(2)}, u32[]{:S(2)}) collective-permute-start(f32[32,128]{1,0:T(8,128)S(1)} %get-tuple-element.68), channel_id=1, source_target_pairs={{0,1},{1,0},{2,3},{3,2},{4,5},{5,4},{6,7},{7,6},{8,9},{9,8},{10,11... | collective-permute-start | bytes 49160 | tf_op jit(solution)/shard_map/ppermute | solution.py:461
  22.6 3.2 %collective-permute-start.8 = (f32[32,128]{1,0:T(8,128)S(1)}, f32[32,128]{1,0:T(8,128)S(1)}, u32[]{:S(2)}, u32[]{:S(2)}) collective-permute-start(f32[32,128]{1,0:T(8,128)S(1)} %get-tuple-element.69), channel_id=1, source_target_pairs={{0,3},{1,2},{2,1},{3,0},{4,7},{5,6},{6,5},{7,4},{8,11},{9,10},{10,... | collective-permute-start | bytes 49160 | tf_op jit(solution)/shard_map/ppermute | solution.py:470
  25.9 6.2 %collective-permute-start.9 = (f32[96,128]{1,0:T(8,128)S(1)}, f32[96,128]{1,0:T(8,128)S(1)}, u32[]{:S(2)}, u32[]{:S(2)}) collective-permute-start(f32[96,128]{1,0:T(8,128)S(1)} %pad_maximum_fusion.5), channel_id=1, source_target_pairs={{0,4},{4,0},{8,12},{12,8},{1,5},{5,1},{9,13},{13,9},{2,6},{6,2},{1... | collective-permute-start | bytes 147464 | tf_op jit(solution)/shard_map/ppermute | solution.py:521
  27.1 6.1 %collective-permute-start.10 = (f32[96,128]{1,0:T(8,128)S(1)}, f32[96,128]{1,0:T(8,128)S(1)}, u32[]{:S(2)}, u32[]{:S(2)}) collective-permute-start(f32[96,128]{1,0:T(8,128)S(1)} %pad_maximum_fusion.5), channel_id=1, source_target_pairs={{0,8},{4,12},{8,0},{12,4},{1,9},{5,13},{9,1},{13,5},{2,10},{6,14},... | collective-permute-start | bytes 147464 | tf_op jit(solution)/shard_map/ppermute | solution.py:521
  29.0 6.2 %collective-permute-start.11 = (f32[96,128]{1,0:T(8,128)S(1)}, f32[96,128]{1,0:T(8,128)S(1)}, u32[]{:S(2)}, u32[]{:S(2)}) collective-permute-start(f32[96,128]{1,0:T(8,128)S(1)} %pad_maximum_fusion.5), channel_id=1, source_target_pairs={{0,12},{4,8},{8,4},{12,0},{1,13},{5,9},{9,5},{13,1},{2,14},{6,10},... | collective-permute-start | bytes 147464 | tf_op jit(solution)/shard_map/ppermute | solution.py:521
  30.4 8.0 %collective-permute-start.12 = (f32[144,128]{1,0:T(8,128)S(1)}, f32[144,128]{1,0:T(8,128)S(1)}, u32[]{:S(2)}, u32[]{:S(2)}) collective-permute-start(f32[144,128]{1,0:T(8,128)S(1)} %get-tuple-element.31), channel_id=1, source_target_pairs={{0,4},{4,0},{8,12},{12,8},{1,5},{5,1},{9,13},{13,9},{2,6},{6,2},{1... | collective-permute-start | bytes 221192 | tf_op jit(solution)/shard_map/ppermute | solution.py:524
  30.7 7.6 %collective-permute-start.13 = (f32[144,128]{1,0:T(8,128)S(1)}, f32[144,128]{1,0:T(8,128)S(1)}, u32[]{:S(2)}, u32[]{:S(2)}) collective-permute-start(f32[144,128]{1,0:T(8,128)S(1)} %get-tuple-element.30), channel_id=1, source_target_pairs={{0,16},{4,8},{8,4},{12,28},{16,0},{20,24},{24,20},{28,12},{1,17},{... | collective-permute-start | bytes 221192 | tf_op jit(solution)/shard_map/ppermute | solution.py:523
